TPU v7x, 256 devices: a 8x8x2 block of a 8x8x16 slice. The times are simulated.
256 devices in a mesh: groups: 2 (over z), section: 2 (over core), mesh: 64 (over x, y).
Axes of the slice: x: 8, y: 8, z: 2, core: 2. Of those that a mesh axis runs over, the one named last changes fastest.
The devices are a block of a 8x8x16 slice.
Arguments:
- inputs: bfloat16 [4, 128, 8192], P('groups', None, 'mesh'), parts along dimension 0, may hold values from -12 to 12
- segments: int32 [4, 128], P('groups'), parts along dimension 0, may hold values from 0 to 3, never falling along the last dimension, each value on 1 to 64 neighbouring positions
- gains: bfloat16 [2, 1, 8192], P('section'), may hold values from 0.25 to 1.75
- w_query: bfloat16 [2, 1, 8192, 8192], P('section', None, None, 'mesh'), may hold values from -1.3258252 to 1.3258252
- w_keyval: bfloat16 [2, 1, 8192, 2048], P('section', None, None, 'mesh'), may hold values from -0.055242717 to 0.055242717
- w_output: bfloat16 [2, 1, 8192, 8192], P('section', None, None, 'mesh'), may hold values from -0.0625 to 0.0625
Outputs:
- section_outputs: bfloat16 [2, 4, 128, 8192], P('section', 'groups', None, 'mesh'), parts along dimension 1
There are 2 independent parts, one for each index of `groups`. A program takes and returns all parts, laid end to end along the dimension named above; an argument that names none is the same for every part. Nothing has to cross between parts.
Inputs may be any that keep to these rules, and one draw needn't show every extreme that they name: `segments`: along each micro-batch the document ids never fall; each document spans 1 to 64 positions.
All inputs are finite; a program needn't handle non-finite values.
Results may differ from a plain program's by a relative error of at most 0.0052.
Values may be sent and summed in bfloat16 or wider, within the bound.
No kernel may reach another device: no remote copies, remote signals or barrier semaphores. Data moves between devices by JAX's collectives and lax.ppermute only.
A program may use at most 64 MiB of HBM per device.

v0:
```python
import jax
import jax.numpy as jnp
from jax import lax
from jax.sharding import Mesh
from jax.sharding import PartitionSpec as P

HD = 128
GROUP = 8
MESH = ("mesh_0", "mesh_1")


norm_epsilon = 1e-05
rope_theta = 500000.0


def joined_along(parts, dim):
    lengths = list(parts.shape[1:])
    lengths[dim] *= parts.shape[0]
    return jnp.moveaxis(parts, 0, dim).reshape(lengths)


def gather_in_order(x, axes, sequence):
    parts = x[None]
    for k in sequence:
        parts = lax.all_gather(parts, axes[k], axis=0, tiled=True)
    block = [lax.axis_size(axes[k]) for k in reversed(sequence)]
    parts = parts.reshape(*block, *x.shape)
    turned = sorted(range(len(sequence)), key=lambda place: sequence[len(sequence) - 1 - place])
    return parts.transpose(*turned, *range(len(sequence), parts.ndim)).reshape(-1, *x.shape)


def whole_of(x, axes, sequence, dim):
    return joined_along(gather_in_order(x, axes, sequence), dim)


def partner_2(x, axis, distance):
    return lax.ppermute(x, axis, [(i, i ^ 1 << distance) for i in range(lax.axis_size(axis))])


def from_behind(block, axis, distance):
    devices = range(lax.axis_size(axis))
    route = [(i - distance, i) for i in devices if i - distance in devices]
    return lax.ppermute(block, axis, route)


def position_tables(segment_row):
    row_length = segment_row.shape[0]
    indices = jnp.arange(row_length, dtype=jnp.int32)
    doc_starts = jnp.concatenate([jnp.ones((1,), dtype=bool), segment_row[1:] != segment_row[:-1]])
    first_index = lax.cummax(jnp.where(doc_starts, indices, jnp.zeros_like(indices)), axis=0)
    positions = (indices - first_index).astype(jnp.float32)
    half_width = HD // 2
    freqs = rope_theta ** (-(2.0 * jnp.arange(half_width, dtype=jnp.float32)) / HD)
    angles = positions[:, None] * freqs[None, :]
    cosine_table = jnp.concatenate([jnp.cos(angles), jnp.cos(angles)], axis=1)
    sine_table = jnp.concatenate([jnp.sin(angles), jnp.sin(angles)], axis=1)
    allowed = (indices[None, :] <= indices[:, None]) & (
        segment_row[None, :] == segment_row[:, None]
    )
    return (cosine_table, sine_table, allowed)


def rotate(values, cosine_table, sine_table):
    half_width = values.shape[-1] // 2
    turned = jnp.concatenate([-values[..., half_width:], values[..., :half_width]], axis=-1)
    return values * cosine_table + turned * sine_table


def softmax_weights(scores, allowed):
    masked = jnp.where(allowed, scores, -1e30)
    highest = jnp.max(masked, axis=-1, keepdims=True)
    raised = jnp.exp(masked - highest)
    return (raised / jnp.sum(raised, axis=-1, keepdims=True)).astype(jnp.bfloat16)


def apply_layer(
    activations,
    gain_row,
    query_weight,
    keyval_weight,
    output_weight,
    cosine_table,
    sine_table,
    allowed,
    mesh_index,
):
    floats = activations.astype(jnp.float32)
    gathered = whole_of(activations, MESH, (0, 1), 1)
    whole_floats = gathered.astype(jnp.float32)
    scale = lax.rsqrt(jnp.mean(whole_floats * whole_floats, axis=1, keepdims=True) + norm_epsilon)
    normed = (whole_floats * scale * gain_row.astype(jnp.float32)).astype(jnp.bfloat16)
    query_raw = jnp.dot(normed, query_weight, preferred_element_type=jnp.float32)
    keyval_raw = jnp.dot(normed, keyval_weight, preferred_element_type=jnp.float32)
    query = rotate(query_raw, cosine_table, sine_table).astype(jnp.bfloat16)
    keyval_part = keyval_raw.astype(jnp.bfloat16)
    for bit_index in range(GROUP.bit_length() - 1):
        partner = partner_2(keyval_part, MESH, bit_index)
        upper_half = mesh_index // (1 << bit_index) % 2 == 1
        keyval_part = jnp.where(
            upper_half,
            jnp.concatenate([partner, keyval_part], axis=1),
            jnp.concatenate([keyval_part, partner], axis=1),
        )
    keys = rotate(keyval_part[:, :HD].astype(jnp.float32), cosine_table, sine_table).astype(
        jnp.bfloat16
    )
    values = keyval_part[:, HD:]
    scores = jnp.dot(query, keys.T, preferred_element_type=jnp.float32) * HD ** (-0.5)
    probs = softmax_weights(scores, allowed)
    attended = jnp.dot(probs, values, preferred_element_type=jnp.float32).astype(jnp.bfloat16)
    mixed = jnp.dot(
        whole_of(attended, MESH, (0, 1), 1), output_weight, preferred_element_type=jnp.float32
    )
    return (floats + mixed).astype(jnp.bfloat16)


def shards(inputs, segments, gains, w_query, w_keyval, w_output):
    micro_count, row_count, local_cols = inputs.shape
    section_count = lax.axis_size("section")
    section_index = lax.axis_index("section")
    mesh_index = lax.axis_index(MESH)
    cosine_list, sine_list, allowed_list = ([], [], [])
    for micro_index in range(micro_count):
        cosine_table, sine_table, allowed = position_tables(segments[micro_index])
        cosine_list.append(cosine_table)
        sine_list.append(sine_table)
        allowed_list.append(allowed)
    cosine_all = jnp.stack(cosine_list)
    sine_all = jnp.stack(sine_list)
    allowed_all = jnp.stack(allowed_list)
    step_count = micro_count + section_count - 1
    received = jnp.zeros((row_count, local_cols), jnp.bfloat16)
    results = []
    for section_step in range(step_count):
        feed_slot = min(section_step, micro_count - 1)
        micro_here = jnp.clip(section_step - section_index, 0, micro_count - 1)
        cosine_table = lax.dynamic_index_in_dim(cosine_all, micro_here, 0, keepdims=False)
        sine_table = lax.dynamic_index_in_dim(sine_all, micro_here, 0, keepdims=False)
        allowed = lax.dynamic_index_in_dim(allowed_all, micro_here, 0, keepdims=False)
        current = jnp.where(section_index == 0, inputs[feed_slot], received)
        current = apply_layer(
            current,
            gains[0, 0],
            w_query[0, 0],
            w_keyval[0, 0],
            w_output[0, 0],
            cosine_table,
            sine_table,
            allowed,
            mesh_index,
        )
        results.append(current)
        if section_step + 1 < step_count:
            received = from_behind(current, "section", 1)
    stacked = jnp.stack(results)
    chosen = lax.dynamic_slice_in_dim(stacked, section_index, micro_count, 0)
    return chosen[None]


def solution(mesh):
    finer = Mesh(
        mesh.devices.reshape(mesh.shape["groups"], mesh.shape["section"], 8, 8),
        ("groups", "section", "mesh_0", "mesh_1"),
    )
    in_specs = (
        P("groups", None, MESH),
        P("groups", None),
        P("section", None, None),
        P("section", None, None, MESH),
        P("section", None, None, MESH),
        P("section", None, None, MESH),
    )
    out_specs = P("section", "groups", None, MESH)
    return jax.shard_map(
        shards, mesh=finer, in_specs=in_specs, out_specs=out_specs, check_vma=False
    )
```

profile of v0, /device:TPU:514, one launch (start us, length us, event | category | flops | bytes accessed | tf_op | source)
XLA Modules:
  0.0 562.5 jit_solution(12271159927433915738)
XLA Ops:
  6.6 0.9 slice_select_fusion
  7.5 43.0 %all_gather.36 = bf16[8,128,128]{2,1,0:T(8,128)(2,1)} all-gather(bf16[1,128,128]{2,1,0:T(8,128)(2,1)S(1)} %slice_select_fusion), channel_id=1, replica_groups=mesh['groups'=2,'section'=2,'mesh_0'=8,'mesh_1'=8] {'mesh_0'}, dimensions={0}, use_global_device_ids=true | all-gather | bytes 294912 | tf_op jit(solution)/shard_map/all_gather | solution.py:25
  50.6 0.8 convert_element_type.231
  51.4 0.9 compare_bitcast_fusion
  53.6 0.8 slice_bitcast_fusion
  54.5 40.1 %all-gather.12.cloned.1.call-done = bf16[64,128,128]{2,1,0:T(8,128)(2,1)} async-done(((bf16[8,128,128]{2,1,0:T(8,128)(2,1)}), bf16[64,128,128]{2,1,0:T(8,128)(2,1)}) %all-gather.12.cloned.1.call-update) | async-done | bytes 2097168 | tf_op jit(solution)/shard_map/all_gather | solution.py:25
  94.5 2.1 convert_bitcast_fusion.2
  96.7 0.5 copy.45
  97.5 2.2 fusion.8
  99.7 4.1 copy.46
  103.9 2.0 convolution_convert_fusion.5
  105.9 1.5 collective-permute-start
  107.4 2.3 collective-permute-done
  109.7 1.6 collective-permute-start.1
  111.3 2.4 fusion.19
  113.6 0.8 collective-permute-done.1
  114.4 3.2 collective-permute-start.2
  117.7 4.7 collective-permute-done.2
  122.9 27.0 %all-gather = bf16[1024,128]{1,0:T(8,128)(2,1)} all-gather(bf16[128,128]{1,0:T(8,128)(2,1)S(1)} %convolution_convert_fusion.2), channel_id=2, replica_groups=mesh['groups'=2,'section'=2,'mesh_0'=8,'mesh_1'=8] {'mesh_0'}, dimensions={0}, use_global_device_ids=true | all-gather | bytes 294912 | tf_op jit(solution)/shard_map/all_gather | solution.py:25
  150.0 41.0 %all-gather.14.cloned.1.call-done = bf16[64,128,128]{2,1,0:T(8,128)(2,1)} async-done(((bf16[8,128,128]{2,1,0:T(8,128)(2,1)}), bf16[64,128,128]{2,1,0:T(8,128)(2,1)}) %all-gather.14.cloned.1.call-update) | async-done | bytes 2097168 | tf_op jit(solution)/shard_map/all_gather | solution.py:25
  191.0 3.1 copy.49
  194.1 4.1 copy.50
  198.2 3.0 fusion.27
  201.2 1.3 collective-permute-start.3
  202.5 0.8 collective-permute-done.3
  203.4 27.0 %all-gather.1 = bf16[1024,128]{1,0:T(8,128)(2,1)} all-gather(bf16[128,128]{1,0:T(8,128)(2,1)S(1)} %bitcast_select_fusion.1), channel_id=3, replica_groups=mesh['groups'=2,'section'=2,'mesh_0'=8,'mesh_1'=8] {'mesh_0'}, dimensions={0}, use_global_device_ids=true | all-gather | bytes 294912 | tf_op jit(solution)/shard_map/all_gather | solution.py:25
  230.7 40.7 %all-gather.16.cloned.1.call-done = bf16[64,128,128]{2,1,0:T(8,128)(2,1)} async-done(((bf16[8,128,128]{2,1,0:T(8,128)(2,1)}), bf16[64,128,128]{2,1,0:T(8,128)(2,1)}) %all-gather.16.cloned.1.call-update) | async-done | bytes 2097168 | tf_op jit(solution)/shard_map/all_gather | solution.py:25
  271.4 2.1 convert_bitcast_fusion.1
  274.4 2.2 fusion.5
  276.6 4.1 copy.52
  280.7 2.0 convolution_convert_fusion.4
  282.7 1.5 collective-permute-start.4
  284.2 2.3 collective-permute-done.4
  286.5 1.6 collective-permute-start.5
  288.1 2.4 fusion.17
  290.4 0.8 collective-permute-done.5
  291.3 3.2 collective-permute-start.6
  294.5 4.7 collective-permute-done.6
  299.7 27.0 %all-gather.2 = bf16[1024,128]{1,0:T(8,128)(2,1)} all-gather(bf16[128,128]{1,0:T(8,128)(2,1)S(1)} %convolution_convert_fusion.1), channel_id=4, replica_groups=mesh['groups'=2,'section'=2,'mesh_0'=8,'mesh_1'=8] {'mesh_0'}, dimensions={0}, use_global_device_ids=true | all-gather | bytes 294912 | tf_op jit(solution)/shard_map/all_gather | solution.py:25
  326.8 41.0 %all-gather.18.cloned.1.call-done = bf16[64,128,128]{2,1,0:T(8,128)(2,1)} async-done(((bf16[8,128,128]{2,1,0:T(8,128)(2,1)}), bf16[64,128,128]{2,1,0:T(8,128)(2,1)}) %all-gather.18.cloned.1.call-update) | async-done | bytes 2097168 | tf_op jit(solution)/shard_map/all_gather | solution.py:25
  367.8 3.1 copy.53
  371.0 4.1 copy.54
  375.0 3.0 add_convert_fusion.1
  378.0 1.3 collective-permute-start.7
  379.3 0.8 collective-permute-done.7
  380.2 27.0 %all-gather.3 = bf16[1024,128]{1,0:T(8,128)(2,1)} all-gather(bf16[128,128]{1,0:T(8,128)(2,1)S(1)} %bitcast_select_fusion), channel_id=5, replica_groups=mesh['groups'=2,'section'=2,'mesh_0'=8,'mesh_1'=8] {'mesh_0'}, dimensions={0}, use_global_device_ids=true | all-gather | bytes 294912 | tf_op jit(solution)/shard_map/all_gather | solution.py:25
  407.3 40.9 %all-gather.20.cloned.1.call-done = bf16[64,128,128]{2,1,0:T(8,128)(2,1)} async-done(((bf16[8,128,128]{2,1,0:T(8,128)(2,1)}), bf16[64,128,128]{2,1,0:T(8,128)(2,1)}) %all-gather.20.cloned.1.call-update) | async-done | bytes 2097168 | tf_op jit(solution)/shard_map/all_gather | solution.py:25
  448.1 2.1 convert_bitcast_fusion
  451.1 2.2 fusion.2
  453.3 4.1 copy.56
  457.4 2.0 convolution_convert_fusion.3
  459.4 1.5 collective-permute-start.8
  460.9 2.3 collective-permute-done.8
  463.2 1.8 collective-permute-start.9
  465.0 2.4 fusion.15
  467.3 0.8 collective-permute-done.9
  468.2 3.2 collective-permute-start.10
  471.4 4.7 collective-permute-done.10
  476.7 27.0 %all-gather.4 = bf16[1024,128]{1,0:T(8,128)(2,1)} all-gather(bf16[128,128]{1,0:T(8,128)(2,1)S(1)} %convolution_convert_fusion), channel_id=6, replica_groups=mesh['groups'=2,'section'=2,'mesh_0'=8,'mesh_1'=8] {'mesh_0'}, dimensions={0}, use_global_device_ids=true | all-gather | bytes 294912 | tf_op jit(solution)/shard_map/all_gather | solution.py:25
  503.7 41.0 %all-gather.22.cloned.1.call-done = bf16[64,128,128]{2,1,0:T(8,128)(2,1)} async-done(((bf16[8,128,128]{2,1,0:T(8,128)(2,1)}), bf16[64,128,128]{2,1,0:T(8,128)(2,1)}) %all-gather.22.cloned.1.call-update) | async-done | bytes 2097168 | tf_op jit(solution)/shard_map/all_gather | solution.py:25
  544.7 3.1 copy.57
  547.9 4.1 copy.58
  551.9 3.0 fusion.71
  554.9 0.7 fusion.35
  (71 shorter events, 6.0 us)
Async XLA Ops:
  6.5 104.7 %copy-start = (bf16[1,1,8192,128]{3,2,1,0:T(8,128)(2,1)S(1)}, bf16[1,1,8192,128]{3,2,1,0:T(8,128)(2,1)}, u32[]{:S(2)}) copy-start(bf16[1,1,8192,128]{3,2,1,0:T(8,128)(2,1)} %param.9) | copy-start | bytes 6291460
  6.6 88.0 %all-gather.12.cloned.1.call-start = ((), (), s32[]{:S(2)}) async-start(), calls=%async_computation | async-start | bytes 2359296 | tf_op jit(solution)/shard_map/all_gather | solution.py:25
  50.6 140.4 %all-gather.14.cloned.1.call-start = ((), (), s32[]{:S(2)}) async-start(), calls=%async_computation.1 | async-start | bytes 2359296 | tf_op jit(solution)/shard_map/all_gather | solution.py:25
  99.7 4.1 copy-start.1
  105.9 3.8 collective-permute-start
  109.7 4.8 collective-permute-start.1
  114.4 7.9 %collective-permute-start.2 = (bf16[128,128]{0,1:T(8,128)(2,1)S(1)}, bf16[128,128]{0,1:T(8,128)(2,1)S(1)}, u32[]{:S(2)}, u32[]{:S(2)}) collective-permute-start(bf16[128,128]{0,1:T(8,128)(2,1)S(1)} %maximum_select_fusion.3), channel_id=1, source_target_pairs={{0,4},{1,5},{2,6},{3,7},{4,0},{5,1},{6,2},{7,3},{8,12},{9,13},{10,... | collective-permute-start | bytes 98312 | tf_op jit(solution)/shard_map/ppermute | solution.py:37
  150.0 121.4 %all-gather.16.cloned.1.call-start = ((), (), s32[]{:S(2)}) async-start(), calls=%async_computation.2 | async-start | bytes 2359296 | tf_op jit(solution)/shard_map/all_gather | solution.py:25
  198.2 5.2 copy-start.2
  201.2 2.2 collective-permute-start.3
  230.5 137.3 %all-gather.18.cloned.1.call-start = ((), (), s32[]{:S(2)}) async-start(), calls=%async_computation.3 | async-start | bytes 2359296 | tf_op jit(solution)/shard_map/all_gather | solution.py:25
  282.7 3.8 collective-permute-start.4
  286.5 4.8 collective-permute-start.5
  291.3 7.9 %collective-permute-start.6 = (bf16[128,128]{0,1:T(8,128)(2,1)S(1)}, bf16[128,128]{0,1:T(8,128)(2,1)S(1)}, u32[]{:S(2)}, u32[]{:S(2)}) collective-permute-start(bf16[128,128]{0,1:T(8,128)(2,1)S(1)} %maximum_select_fusion.4), channel_id=1, source_target_pairs={{0,4},{1,5},{2,6},{3,7},{4,0},{5,1},{6,2},{7,3},{8,12},{9,13},{10,... | collective-permute-start | bytes 98312 | tf_op jit(solution)/shard_map/ppermute | solution.py:37
  326.8 121.3 %all-gather.20.cloned.1.call-start = ((), (), s32[]{:S(2)}) async-start(), calls=%async_computation.4 | async-start | bytes 2359296 | tf_op jit(solution)/shard_map/all_gather | solution.py:25
  378.0 2.2 collective-permute-start.7
  407.2 137.5 %all-gather.22.cloned.1.call-start = ((), (), s32[]{:S(2)}) async-start(), calls=%async_computation.5 | async-start | bytes 2359296 | tf_op jit(solution)/shard_map/all_gather | solution.py:25
  459.4 3.8 collective-permute-start.8
  463.2 5.0 collective-permute-start.9
  468.2 7.9 %collective-permute-start.10 = (bf16[128,128]{0,1:T(8,128)(2,1)S(1)}, bf16[128,128]{0,1:T(8,128)(2,1)S(1)}, u32[]{:S(2)}, u32[]{:S(2)}) collective-permute-start(bf16[128,128]{0,1:T(8,128)(2,1)S(1)} %maximum_select_fusion.5), channel_id=1, source_target_pairs={{0,4},{1,5},{2,6},{3,7},{4,0},{5,1},{6,2},{7,3},{8,12},{9,13},{10,... | collective-permute-start | bytes 98312 | tf_op jit(solution)/shard_map/ppermute | solution.py:37
Sparse Core Ops, SparseCore 0:
  50.7 43.8 all-gather.11
  150.1 40.8 all-gather.13
  230.6 40.7 all-gather.15
  326.9 40.8 all-gather.17
  407.3 40.7 all-gather.19
  503.8 40.8 all-gather.21
where the time goes:
time: 564 us; the launch traced here: 562 us
  waiting for transfers between devices  270 us (48%)
  blocking collectives  178 us (32%)
  local copies, waits for them, and re-layouts  36.4 us (6%)
  matrix products  23.5 us (4%)
  starting transfers between devices  22.3 us (4%)
  other arithmetic  18.8 us (3%)
  between operations  13.8 us (2%)
    all_gather x6, waiting for transfers between devices, gather_in_order(): parts = lax.all_gather(parts, axes[k], axis=0, tiled=True)  245 us
    all_gather x6, blocking collectives, gather_in_order(): parts = lax.all_gather(parts, axes[k], axis=0, tiled=True)  178 us
    ppermute x9, waiting for transfers between devices, partner_2(): lax.ppermute(x, axis, [(i, i ^ 1 << distance) for i in range(lax.axis_siz...  23.4 us
    ppermute x9, starting transfers between devices, partner_2(): lax.ppermute(x, axis, [(i, i ^ 1 << distance) for i in range(lax.axis_siz...  19.2 us
    convert_element_type x3, local copies, waits for them, and re-layouts, apply_layer(): (whole_floats * scale * gain_row.astype(jnp.float32)).astype(jnp.bfloat16)  12.2 us
    transpose x3, local copies, waits for them, and re-layouts, joined_along(): return jnp.moveaxis(parts, 0, dim).reshape(lengths)  12.2 us
  transfers between devices with their start and end apart: 17, of which 17 were waited for; matrix products, arithmetic and copies ran while one was open for 2% of the time, Pallas kernels for 0%

commit v1 on v0

v1 whole, which is shorter than its diff:
```python
import functools

import jax
import jax.numpy as jnp
from jax import lax
from jax.experimental import pallas as pl
from jax.experimental.pallas import tpu as pltpu
from jax.sharding import Mesh
from jax.sharding import PartitionSpec as P

HD = 128
HALF = HD // 2
X = ("x2", "x1", "x0")
Y = ("y2", "y1", "y0")
MESH = X + Y
norm_epsilon = 1e-05
rope_theta = 500000.0
VMEM_LIMIT = 56 * 1024 * 1024


def position_tables(segment_row):
    row_length = segment_row.shape[0]
    indices = jnp.arange(row_length, dtype=jnp.int32)
    same = segment_row[None, :] == segment_row[:, None]
    first_index = jnp.min(jnp.where(same, indices[None, :], row_length), axis=1)
    positions = (indices - first_index).astype(jnp.float32)
    freqs = rope_theta ** (-(2.0 * jnp.arange(HALF, dtype=jnp.float32)) / HD)
    angles = positions[:, None] * freqs[None, :]
    cosine, sine = jnp.cos(angles), jnp.sin(angles)
    allowed = (indices[None, :] <= indices[:, None]) & same
    return (
        jnp.concatenate([cosine, cosine], axis=1),
        jnp.concatenate([-sine, sine], axis=1),
        allowed.astype(jnp.float32),
    )


def project_kernel(pick, blocks, gain, wq_a, wq_b, wkv_a, wkv_b, cosine, sine, query, keyval):
    count, rows, width = blocks.shape
    second = pick[0] == 1
    total = jnp.zeros((rows, width), jnp.float32)
    for d in range(count):
        part = blocks[d].astype(jnp.float32)
        total += part * part
    scale = lax.rsqrt(
        jnp.sum(total, axis=1, keepdims=True) / (count * width) + norm_epsilon
    )
    q_sum = jnp.zeros(query.shape, jnp.float32)
    kv_sum = jnp.zeros((rows, wkv_a.shape[1]), jnp.float32)
    for d in range(0, count, 2):
        pair = []
        for e in (d, d + 1):
            weight = gain[:, e * width : (e + 1) * width].astype(jnp.float32)
            pair.append((blocks[e].astype(jnp.float32) * scale * weight).astype(jnp.bfloat16))
        normed = jnp.concatenate(pair, axis=1)
        span = slice(d * width, (d + 2) * width)
        wq = jnp.where(second, wq_b[span, :], wq_a[span, :])
        wkv = jnp.where(second, wkv_b[span, :], wkv_a[span, :])
        q_sum += jnp.dot(normed, wq, preferred_element_type=jnp.float32)
        kv_sum += jnp.dot(normed, wkv, preferred_element_type=jnp.float32)
    turned = jnp.concatenate([q_sum[:, HALF:], q_sum[:, :HALF]], axis=1)
    query[...] = (q_sum * cosine[...] + turned * sine[...]).astype(query.dtype)
    flat = kv_sum.astype(jnp.bfloat16).astype(jnp.float32).T.astype(jnp.bfloat16)
    keyval[...] = jnp.broadcast_to(flat[None], keyval.shape)


def attend_kernel(query, keyval, cosine, sine, allowed, attended):
    keys = keyval[:HD, :].astype(jnp.float32)
    turned = jnp.concatenate([keys[HALF:], keys[:HALF]], axis=0)
    keys = (keys * cosine[...].T + turned * sine[...].T).astype(jnp.bfloat16)
    scores = jnp.dot(query[...], keys, preferred_element_type=jnp.float32) * HD ** (-0.5)
    masked = jnp.where(allowed[...] > 0.0, scores, -1e30)
    highest = jnp.max(masked, axis=1, keepdims=True)
    raised = jnp.exp(masked - highest)
    probs = (raised / jnp.sum(raised, axis=1, keepdims=True)).astype(jnp.bfloat16)
    out = lax.dot_general(
        probs, keyval[HD:, :], (((1,), (1,)), ((), ())), preferred_element_type=jnp.float32
    ).astype(jnp.bfloat16)
    attended[...] = jnp.broadcast_to(out[None], attended.shape)


def mix_kernel(pick, blocks, wo_a, wo_b, residual, result, copies=None):
    count, rows, width = blocks.shape
    second = pick[0] == 1
    mixed = residual[...].astype(jnp.float32)
    for d in range(0, count, 2):
        pair = jnp.concatenate([blocks[d], blocks[d + 1]], axis=1)
        span = slice(d * width, (d + 2) * width)
        wo = jnp.where(second, wo_b[span, :], wo_a[span, :])
        mixed += jnp.dot(pair, wo, preferred_element_type=jnp.float32)
    out = mixed.astype(result.dtype)
    result[...] = out
    if copies is not None:
        copies[...] = jnp.broadcast_to(out[None], copies.shape)


def call(kernel, outs, n_in, scalar_first):
    vmem = pl.BlockSpec(memory_space=pltpu.VMEM)
    specs = [pl.BlockSpec(memory_space=pltpu.SMEM)] if scalar_first else []
    specs += [vmem] * (n_in - len(specs))
    return pl.pallas_call(
        kernel,
        out_shape=outs,
        in_specs=specs,
        out_specs=jax.tree.map(lambda _: vmem, outs),
        compiler_params=pltpu.CompilerParams(vmem_limit_bytes=VMEM_LIMIT),
    )


def exchange(copies):
    return lax.all_to_all(copies, MESH, 0, 0, tiled=True)


def shards(inputs, segments, gains, w_query, w_keyval, w_output):
    _, rows, width = inputs.shape
    sections = lax.axis_size("section")
    devices = lax.axis_size(MESH)
    ring = lax.axis_size(Y)
    me = lax.axis_index("section")
    swap = [(0, 1), (1, 0)]
    own = [w[0, 0] for w in (w_query, w_keyval, w_output)]
    current = lax.dynamic_index_in_dim(inputs, me, 0, keepdims=False)
    segment_row = lax.dynamic_index_in_dim(segments, me, 0, keepdims=False)
    cosine, sine, allowed = position_tables(segment_row)
    other_gain = lax.ppermute(gains[0], "section", swap)
    other = [lax.ppermute(w, "section", swap) for w in own]
    copies = jnp.broadcast_to(current[None], (devices, rows, width))
    bf16 = functools.partial(jax.ShapeDtypeStruct, dtype=jnp.bfloat16)
    results = []
    for s in range(sections):
        pick = jnp.where(me == s, 0, 1).astype(jnp.int32).reshape(1)
        gain = jnp.where(me == s, gains[0], other_gain)
        blocks = exchange(copies)
        query, keyval = call(
            project_kernel, (bf16((rows, width)), bf16((ring, own[1].shape[1], rows))), 9, True
        )(pick, blocks, gain, own[0], other[0], own[1], other[1], cosine, sine)
        keyval = lax.all_to_all(keyval, Y, 0, 0, tiled=True).reshape(-1, rows)
        attended = call(attend_kernel, bf16((devices, rows, width)), 5, False)(
            query, keyval, cosine, sine, allowed
        )
        blocks = exchange(attended)
        outs = (bf16((rows, width)),)
        if s + 1 < sections:
            outs += (bf16((devices, rows, width)),)
        current, *copies = call(mix_kernel, outs, 5, True)(pick, blocks, own[2], other[2], current)
        copies = copies[0] if copies else None
        results.append(current)
    mine = jnp.where(me == 0, results[0], results[1])
    theirs = lax.ppermute(jnp.where(me == 0, results[1], results[0]), "section", swap)
    first = jnp.where(me == 0, mine, theirs)
    second = jnp.where(me == 0, theirs, mine)
    return jnp.stack([first, second])[None]


def solution(mesh):
    finer = Mesh(
        mesh.devices.reshape(mesh.shape["groups"], mesh.shape["section"], *([2] * 6)),
        ("groups", "section") + MESH,
    )
    in_specs = (
        P("groups", None, MESH),
        P("groups", None),
        P("section", None, None),
        P("section", None, None, MESH),
        P("section", None, None, MESH),
        P("section", None, None, MESH),
    )
    out_specs = P("section", "groups", None, MESH)
    return jax.shard_map(
        shards, mesh=finer, in_specs=in_specs, out_specs=out_specs, check_vma=False
    )
```

time: 564 us -> 332 us (0.59)
  the two profiles are of different devices: /device:TPU:514 before, /device:TPU:647 now
where the time goes in v1:
time: 332 us; the launch traced here: 331 us
  waiting for transfers between devices  159 us (48%)
  blocking collectives  77.7 us (23%)
  starting transfers between devices  51.6 us (16%)
  Pallas kernels  29 us (9%)
  local copies, waits for them, and re-layouts  9.63 us (3%)
  other arithmetic  4.06 us (1%)
    all_to_all x3, waiting for transfers between devices, exchange(): return lax.all_to_all(copies, MESH, 0, 0, tiled=True)  148 us
    all_to_all x1, blocking collectives, exchange(): return lax.all_to_all(copies, MESH, 0, 0, tiled=True)  66.4 us
    all_to_all x3, starting transfers between devices, exchange(): return lax.all_to_all(copies, MESH, 0, 0, tiled=True)  40.8 us
    pallas_call x2, Pallas kernels, shards(): call(project_kernel, (bf16((rows, width)), bf16((ring, own[1].shape[1], r...  13.5 us
    all_to_all x1, blocking collectives, shards(): keyval = lax.all_to_all(keyval, Y, 0, 0, tiled=True).reshape(-1, rows)  11.3 us
    pallas_call x2, Pallas kernels, shards(): call(mix_kernel, outs, 5, True)(pick, blocks, own[2], other[2], current)  9.47 us
  transfers between devices with their start and end apart: 9, of which 6 were waited for; matrix products, arithmetic and copies ran while one was open for 2% of the time, Pallas kernels for 0%

profile of v1, /device:TPU:647, one launch (start us, length us, event | category | flops | bytes accessed | tf_op | source)
XLA Modules:
  0.0 331.1 jit_solution(17733558781892879086)
XLA Ops:
  0.0 0.0 copy-start
  0.0 0.8 copy-done
  0.8 0.0 copy-start.5
  0.8 1.9 broadcast_in_dim.33
  2.7 0.0 copy-start.8
  2.7 0.0 copy-start.4
  2.8 0.0 copy-start.9
  2.8 0.0 copy-done.5
  2.8 19.7 %all-to-all-start = ((bf16[64,128,128]{2,1,0:T(8,128)(2,1)}), bf16[64,128,128]{2,1,0:T(8,128)(2,1)S(1)}, u32[]{:S(2)}, u32[]{:S(2)}) async-start(bf16[64,128,128]{2,1,0:T(8,128)(2,1)} %broadcast_in_dim.33), calls=%async_computation | async-start | bytes 4194304 | tf_op jit(solution)/shard_map/all_to_all | solution.py:111
  22.5 0.0 copy-done.8
  22.5 1.3 collective-permute-start
  23.8 0.0 copy-done.4
  23.8 0.2 collective-permute-start.2
  23.9 0.4 collective-permute-start.1
  24.3 0.0 copy-done.9
  24.3 0.2 fusion
  24.5 0.3 fusion.2
  24.8 0.7 pad_maximum_fusion
  25.6 1.7 copy.8
  27.3 0.0 collective-permute-done
  27.3 0.7 broadcast_select_fusion
  28.0 0.0 collective-permute-done.2
  28.0 1.8 copy.10.wkv_b
  29.7 0.0 collective-permute-done.1.wq_b
  29.7 48.0 %all-to-all-done.blocks = bf16[64,128,128]{2,1,0:T(8,128)(2,1)S(1)} async-done(((bf16[64,128,128]{2,1,0:T(8,128)(2,1)}), bf16[64,128,128]{2,1,0:T(8,128)(2,1)S(1)}, u32[]{:S(2)}, u32[]{:S(2)}) %all-to-all-start) | async-done | bytes 2097184 | tf_op jit(solution)/shard_map/all_to_all | solution.py:111
  77.7 0.0 copy-start.2
  77.7 1.4 copy-done.2
  79.1 6.7 %shard_map.64 = (bf16[128,128]{1,0:T(8,128)(2,1)}, bf16[8,32,128]{2,1,0:T(8,128)(2,1)}) custom-call(s32[1]{0:T(128)} %bitcast.pick, bf16[64,128,128]{2,1,0:T(8,128)(2,1)} %copy-done.2, bf16[1,8192]{1,0:T(2,128)(2,1)} %get-tuple-element.20.gain, bf16[8192,128]{1,0:T(8,128)(2,1)} %bitcast.27, bf16[8192,128]{1,0:T(8,128)(2,1)} %collective-permute-done.1.wq_b, ...), custom_call_target="tpu_custom_call" | custom-call | tf_op jit(solution)/shard_map/pallas_call | solution.py:134
  85.8 3.6 %all-to-all-start.1 = ((bf16[8,32,128]{2,1,0:T(8,128)(2,1)}), bf16[8,32,128]{2,1,0:T(8,128)(2,1)S(1)}, u32[]{:S(2)}, u32[]{:S(2)}) async-start(bf16[8,32,128]{2,1,0:T(8,128)(2,1)} %get-tuple-element.12), calls=%async_computation.1 | async-start | bytes 131072 | tf_op jit(solution)/shard_map/all_to_all | solution.py:137
  89.4 0.7 fusion.1.allowed
  90.1 6.6 %all-to-all-done.1 = bf16[8,32,128]{2,1,0:T(8,128)(2,1)S(1)} async-done(((bf16[8,32,128]{2,1,0:T(8,128)(2,1)}), bf16[8,32,128]{2,1,0:T(8,128)(2,1)S(1)}, u32[]{:S(2)}, u32[]{:S(2)}) %all-to-all-start.1) | async-done | bytes 65568 | tf_op jit(solution)/shard_map/all_to_all | solution.py:137
  96.7 0.0 copy-start.7
  96.7 0.6 copy-done.7
  97.3 3.0 shard_map.65
  100.4 0.0 copy-start.1
  100.4 8.2 %all-to-all-start.2 = ((bf16[64,128,128]{2,1,0:T(8,128)(2,1)}), bf16[64,128,128]{2,1,0:T(8,128)(2,1)}, u32[]{:S(2)}, u32[]{:S(2)}) async-start(bf16[64,128,128]{2,1,0:T(8,128)(2,1)} %shard_map.65), calls=%async_computation.2 | async-start | bytes 4194304 | tf_op jit(solution)/shard_map/all_to_all | solution.py:111
  108.6 0.0 copy-done.1
  108.6 3.2 collective-permute-start.3
  111.9 3.9 %collective-permute-done.3.wo_b = bf16[8192,128]{1,0:T(8,128)(2,1)} collective-permute-done((bf16[8192,128]{1,0:T(8,128)(2,1)S(1)}, bf16[8192,128]{1,0:T(8,128)(2,1)}, u32[]{:S(2)}, u32[]{:S(2)}) %collective-permute-start.3) | collective-permute-done | bytes 2097184 | tf_op jit(solution)/shard_map/ppermute | solution.py:126
  115.8 46.0 %all-to-all-done.2.blocks = bf16[64,128,128]{2,1,0:T(8,128)(2,1)} async-done(((bf16[64,128,128]{2,1,0:T(8,128)(2,1)}), bf16[64,128,128]{2,1,0:T(8,128)(2,1)}, u32[]{:S(2)}, u32[]{:S(2)}) %all-to-all-start.2) | async-done | bytes 2097184 | tf_op jit(solution)/shard_map/all_to_all | solution.py:111
  161.8 5.2 %shard_map.66 = (bf16[128,128]{1,0:T(8,128)(2,1)}, bf16[64,128,128]{2,1,0:T(8,128)(2,1)}) custom-call(s32[1]{0:T(128)} %bitcast.pick, bf16[64,128,128]{2,1,0:T(8,128)(2,1)} %all-to-all-done.2.blocks, bf16[8192,128]{1,0:T(8,128)(2,1)} %bitcast.23, bf16[8192,128]{1,0:T(8,128)(2,1)} %collective-permute-done.3.wo_b, bf16[128,128]{1,0:T(8,128)(2,1)} %copy-done.5), custom_call_target="tpu_custom_call" | custom-call | tf_op jit(solution)/shard_map/pallas_call | solution.py:145
  167.0 12.8 %all-to-all-start.3 = ((bf16[64,128,128]{2,1,0:T(8,128)(2,1)}), bf16[64,128,128]{2,1,0:T(8,128)(2,1)S(1)}, u32[]{:S(2)}, u32[]{:S(2)}) async-start(bf16[64,128,128]{2,1,0:T(8,128)(2,1)} %get-tuple-element.14), calls=%async_computation.3 | async-start | bytes 4194304 | tf_op jit(solution)/shard_map/all_to_all | solution.py:111
  179.8 53.5 %all-to-all-done.3.blocks = bf16[64,128,128]{2,1,0:T(8,128)(2,1)S(1)} async-done(((bf16[64,128,128]{2,1,0:T(8,128)(2,1)}), bf16[64,128,128]{2,1,0:T(8,128)(2,1)S(1)}, u32[]{:S(2)}, u32[]{:S(2)}) %all-to-all-start.3) | async-done | bytes 2097184 | tf_op jit(solution)/shard_map/all_to_all | solution.py:111
  233.4 0.0 copy-start.3
  233.4 1.4 copy-done.3
  234.7 6.7 %shard_map.67 = (bf16[128,128]{1,0:T(8,128)(2,1)}, bf16[8,32,128]{2,1,0:T(8,128)(2,1)}) custom-call(s32[1]{0:T(128)} %bitcast.9.pick, bf16[64,128,128]{2,1,0:T(8,128)(2,1)} %copy-done.3, bf16[1,8192]{1,0:T(2,128)(2,1)} %get-tuple-element.19.gain, bf16[8192,128]{1,0:T(8,128)(2,1)} %bitcast.28, bf16[8192,128]{1,0:T(8,128)(2,1)} %collective-permute-done.1.wq_b, ...), custom_call_target="tpu_custom_call" | custom-call | tf_op jit(solution)/shard_map/pallas_call | solution.py:134
  241.5 11.3 %all_to_all.30 = bf16[8,32,128]{2,1,0:T(8,128)(2,1)} all-to-all(bf16[8,32,128]{2,1,0:T(8,128)(2,1)} %get-tuple-element.16), channel_id=1, replica_groups=mesh['groups'=2,'section'=2,'x2'=2,'x1'=2,'x0'=2,'y2'=2,'y1'=2,'y0'=2] {..., dimensions={0} | all-to-all | bytes 131072 | tf_op jit(solution)/shard_map/all_to_all | solution.py:137
  252.8 3.0 shard_map.68
  255.8 66.4 %all_to_all.31.blocks = bf16[64,128,128]{2,1,0:T(8,128)(2,1)} all-to-all(bf16[64,128,128]{2,1,0:T(8,128)(2,1)} %shard_map.68), channel_id=1, replica_groups=mesh['groups'=2,'section'=2,'x2'=2,'x1'=2,'x0'=2,'y2'=2,'y1'=2,'y0'=2] {..., dimensions={0} | all-to-all | bytes 4194304 | tf_op jit(solution)/shard_map/all_to_all | solution.py:111
  322.3 0.0 copy-start.6
  322.3 4.3 %shard_map.69 = bf16[128,128]{1,0:T(8,128)(2,1)} custom-call(s32[1]{0:T(128)} %bitcast.9.pick, bf16[64,128,128]{2,1,0:T(8,128)(2,1)} %all_to_all.31.blocks, bf16[8192,128]{1,0:T(8,128)(2,1)} %bitcast.24, bf16[8192,128]{1,0:T(8,128)(2,1)} %collective-permute-done.3.wo_b, bf16[128,128]{1,0:T(8,128)(2,1)} %get-tuple-element.13.residual), custom_call_target="tpu_custom_call" | custom-call | tf_op jit(solution)/shard_map/pallas_call | solution.py:145
  326.5 0.0 copy-done.6
  326.5 2.3 collective-permute-start.4
  328.8 0.9 collective-permute-done.4
  329.7 0.8 select_bitcast_fusion.1
  330.4 0.6 maximum_bitcast_fusion
  (5 shorter events, 0.0 us)
Async XLA Ops:
  0.0 0.8 copy-start
  0.8 1.9 copy-start.5
  2.7 19.7 %copy-start.8 = (bf16[1,1,8192]{2,1,0:T(2,128)(2,1)S(1)}, bf16[1,1,8192]{2,1,0:T(2,128)(2,1)}, u32[]{:S(2)}) copy-start(bf16[1,1,8192]{2,1,0:T(2,128)(2,1)} %param.8) | copy-start | bytes 49156
  2.7 21.0 %copy-start.4 = (bf16[1,1,8192,32]{2,3,1,0:T(8,128)(2,1)S(1)}, bf16[1,1,8192,32]{2,3,1,0:T(8,128)(2,1)}, u32[]{:S(2)}) copy-start(bf16[1,1,8192,32]{2,3,1,0:T(8,128)(2,1)} %param.10) | copy-start | bytes 1572868
  2.8 21.6 %copy-start.9 = (s32[2,128]{1,0:T(2,128)S(1)}, s32[2,128]{1,0:T(2,128)}, u32[]{:S(2)}) copy-start(s32[2,128]{1,0:T(2,128)} %param.7) | copy-start | bytes 3076
  2.8 74.9 %all-to-all-start = ((bf16[64,128,128]{2,1,0:T(8,128)(2,1)}), bf16[64,128,128]{2,1,0:T(8,128)(2,1)S(1)}, u32[]{:S(2)}, u32[]{:S(2)}) async-start(bf16[64,128,128]{2,1,0:T(8,128)(2,1)} %broadcast_in_dim.33), calls=%async_computation | async-start | bytes 4194304 | tf_op jit(solution)/shard_map/all_to_all | solution.py:111
  22.5 4.8 %collective-permute-start = (bf16[1,8192]{1,0:T(2,128)(2,1)S(1)}, bf16[1,8192]{1,0:T(2,128)(2,1)S(1)}, u32[]{:S(2)}, u32[]{:S(2)}) collective-permute-start(bf16[1,8192]{1,0:T(2,128)(2,1)S(1)} %bitcast.32), channel_id=1, source_target_pairs={{0,64},{64,0},{1,65},{65,1},{2,66},{66,2},{3,67},{67,3},{4,68},{68... | collective-permute-start | bytes 49160 | tf_op jit(solution)/shard_map/ppermute | solution.py:125
  23.8 4.2 %collective-permute-start.2 = (bf16[8192,32]{0,1:T(8,128)(2,1)S(1)}, bf16[8192,32]{0,1:T(8,128)(2,1)S(1)}, u32[]{:S(2)}, u32[]{:S(2)}) collective-permute-start(bf16[8192,32]{0,1:T(8,128)(2,1)S(1)} %bitcast.29), channel_id=1, source_target_pairs={{0,64},{64,0},{1,65},{65,1},{2,66},{66,2},{3,67},{67,3},{4,68},{68... | collective-permute-start | bytes 1572872 | tf_op jit(solution)/shard_map/ppermute | solution.py:126
  23.9 5.8 %collective-permute-start.1 = (bf16[8192,128]{1,0:T(8,128)(2,1)}, bf16[8192,128]{1,0:T(8,128)(2,1)}, u32[]{:S(2)}, u32[]{:S(2)}) collective-permute-start(bf16[8192,128]{1,0:T(8,128)(2,1)} %bitcast.26), channel_id=1, source_target_pairs={{0,64},{64,0},{1,65},{65,1},{2,66},{66,2},{3,67},{67,3},{4,68},{68... | collective-permute-start | bytes 6291464 | tf_op jit(solution)/shard_map/ppermute | solution.py:126
  77.7 1.4 copy-start.2
  85.8 10.9 %all-to-all-start.1 = ((bf16[8,32,128]{2,1,0:T(8,128)(2,1)}), bf16[8,32,128]{2,1,0:T(8,128)(2,1)S(1)}, u32[]{:S(2)}, u32[]{:S(2)}) async-start(bf16[8,32,128]{2,1,0:T(8,128)(2,1)} %get-tuple-element.12), calls=%async_computation.1 | async-start | bytes 131072 | tf_op jit(solution)/shard_map/all_to_all | solution.py:137
  96.7 0.6 copy-start.7
  100.4 8.2 %copy-start.1 = (bf16[1,1,8192,128]{3,2,1,0:T(8,128)(2,1)S(1)}, bf16[1,1,8192,128]{3,2,1,0:T(8,128)(2,1)}, u32[]{:S(2)}) copy-start(bf16[1,1,8192,128]{3,2,1,0:T(8,128)(2,1)} %param.11) | copy-start | bytes 6291460
  100.4 61.4 %all-to-all-start.2 = ((bf16[64,128,128]{2,1,0:T(8,128)(2,1)}), bf16[64,128,128]{2,1,0:T(8,128)(2,1)}, u32[]{:S(2)}, u32[]{:S(2)}) async-start(bf16[64,128,128]{2,1,0:T(8,128)(2,1)} %shard_map.65), calls=%async_computation.2 | async-start | bytes 4194304 | tf_op jit(solution)/shard_map/all_to_all | solution.py:111
  108.6 7.2 %collective-permute-start.3 = (bf16[8192,128]{1,0:T(8,128)(2,1)S(1)}, bf16[8192,128]{1,0:T(8,128)(2,1)}, u32[]{:S(2)}, u32[]{:S(2)}) collective-permute-start(bf16[8192,128]{1,0:T(8,128)(2,1)S(1)} %bitcast.25), channel_id=1, source_target_pairs={{0,64},{64,0},{1,65},{65,1},{2,66},{66,2},{3,67},{67,3},{4,68},{68... | collective-permute-start | bytes 6291464 | tf_op jit(solution)/shard_map/ppermute | solution.py:126
  167.0 66.4 %all-to-all-start.3 = ((bf16[64,128,128]{2,1,0:T(8,128)(2,1)}), bf16[64,128,128]{2,1,0:T(8,128)(2,1)S(1)}, u32[]{:S(2)}, u32[]{:S(2)}) async-start(bf16[64,128,128]{2,1,0:T(8,128)(2,1)} %get-tuple-element.14), calls=%async_computation.3 | async-start | bytes 4194304 | tf_op jit(solution)/shard_map/all_to_all | solution.py:111
  233.4 1.4 copy-start.3
  322.3 4.3 %copy-start.6 = (bf16[128,128]{1,0:T(8,128)(2,1)S(1)}, bf16[128,128]{1,0:T(8,128)(2,1)}, u32[]{:S(2)}) copy-start(bf16[128,128]{1,0:T(8,128)(2,1)} %get-tuple-element.13.residual) | copy-start | bytes 98308
  326.5 3.1 collective-permute-start.4

commit v2 on v1

v2 whole, which is shorter than its diff:
```python
import functools

import jax
import jax.numpy as jnp
from jax import lax
from jax.experimental import pallas as pl
from jax.experimental.pallas import tpu as pltpu
from jax.sharding import Mesh
from jax.sharding import PartitionSpec as P

HD = 128
HALF = HD // 2
X = ("x2", "x1", "x0")
Y = ("y2", "y1", "y0")
MESH = X + Y
FAR = ("x2", "x1", "y2", "y1")
SIDE = 8
FAR_COUNT = 16
norm_epsilon = 1e-05
rope_theta = 500000.0
MIB = 1024 * 1024


def position_tables(segment_row):
    row_length = segment_row.shape[0]
    indices = jnp.arange(row_length, dtype=jnp.int32)
    same = segment_row[None, :] == segment_row[:, None]
    first_index = jnp.min(jnp.where(same, indices[None, :], row_length), axis=1)
    positions = (indices - first_index).astype(jnp.float32)
    freqs = rope_theta ** (-(2.0 * jnp.arange(HALF, dtype=jnp.float32)) / HD)
    angles = positions[:, None] * freqs[None, :]
    cosine, sine = jnp.cos(angles), jnp.sin(angles)
    allowed = (indices[None, :] <= indices[:, None]) & same
    return (
        jnp.concatenate([cosine, cosine], axis=1),
        jnp.concatenate([-sine, sine], axis=1),
        allowed.astype(jnp.float32),
    )


STAGES = (
    ((0, 0, 0),),
    ((1, 0, 0), (1, 0, 8), (0, 1, 0), (0, 1, 8)),
    ((1, 1, 0), (1, 1, 8)),
)
STEP = 4


def for_chunks(buffers, layout, body, carry):
    px, py = lax.axis_index("x0"), lax.axis_index("y0")
    for ref, (turn_x, turn_y, first) in zip(buffers, layout, strict=True):
        base = SIDE * jnp.where(turn_x == 1, 1 - px, px) + jnp.where(turn_y == 1, 1 - py, py)
        base += 2 * SIDE * (first // STEP)

        def chunk(i, carry, ref=ref, base=base):
            place = base + 2 * SIDE * i
            return body([(ref[i * STEP + k], place + 2 * k) for k in range(STEP)], carry)

        count = ref.shape[0] // STEP
        carry = chunk(0, carry) if count == 1 else lax.fori_loop(0, count, chunk, carry)
    return carry


def at(place, width):
    return pl.ds(pl.multiple_of(place * width, width), width)


def is_other(section):
    return lax.axis_index("section") != section


def weight_rows(second, own, other, chunk, width):
    parts = []
    for _, place in chunk:
        parts.append(jnp.where(second, other[at(place, width), :], own[at(place, width), :]))
    return jnp.concatenate(parts, axis=0)


def project_kernel(
    section, layout, first, last, gain_own, gain_other, own, other, kv_own, kv_other, *rest
):
    before = () if first else rest[:3]
    rest = rest[len(before) :]
    tables = rest[:2] if last else ()
    rest = rest[len(tables) :]
    buffers, outs = rest[: len(layout)], rest[len(layout) :]
    second = is_other(section)
    rows, width = buffers[0].shape[1:]
    columns = kv_own.shape[0]

    def body(chunk, carry):
        q_sum, kv_sum, squares = carry
        scaled, kv_parts = [], []
        for part, place in chunk:
            gain = jnp.where(second, gain_other[place], gain_own[place])
            wide = part.astype(jnp.float32)
            squares += wide * wide
            scaled.append((wide * gain).astype(jnp.bfloat16))
            span = at(place, width)
            kv_parts.append(jnp.where(second, kv_other[:, span], kv_own[:, span]))
        scaled = jnp.concatenate(scaled, axis=1)
        weight = weight_rows(second, own, other, chunk, width)
        q_sum += jnp.dot(scaled, weight, preferred_element_type=jnp.float32)
        kv_sum += lax.dot_general(
            jnp.concatenate(kv_parts, axis=1),
            scaled,
            (((1,), (1,)), ((), ())),
            preferred_element_type=jnp.float32,
        )
        return q_sum, kv_sum, squares

    if first:
        carry = tuple(
            jnp.zeros(shape, jnp.float32) for shape in ((rows, width), (columns, rows), (rows, width))
        )
    else:
        carry = tuple(ref[...] for ref in before)
    carry = for_chunks(buffers, layout, body, carry)
    if not last:
        for out, value in zip(outs, carry, strict=True):
            out[...] = value
        return
    q_sum, kv_sum, squares = carry
    cosine, sine = tables
    query, keyval = outs
    features = width * gain_own.shape[0]
    scale = lax.rsqrt(jnp.sum(squares, axis=1, keepdims=True) / features + norm_epsilon)
    q_sum *= scale
    turned = jnp.concatenate([q_sum[:, HALF:], q_sum[:, :HALF]], axis=1)
    query[...] = (q_sum * cosine[...] + turned * sine[...]).astype(query.dtype)
    across = jnp.broadcast_to(scale, (rows, width)).T[:columns, :]
    flat = (kv_sum * across).astype(keyval.dtype)
    keyval[...] = jnp.broadcast_to(flat[None], keyval.shape)


def attend_kernel(query, keyval, cosine, sine, allowed, attended):
    keys = keyval[:HD, :].astype(jnp.float32)
    turned = jnp.concatenate([keys[HALF:], keys[:HALF]], axis=0)
    keys = (keys * cosine[...].T + turned * sine[...].T).astype(jnp.bfloat16)
    scores = jnp.dot(query[...], keys, preferred_element_type=jnp.float32) * HD ** (-0.5)
    masked = jnp.where(allowed[...] > 0.0, scores, -1e30)
    highest = jnp.max(masked, axis=1, keepdims=True)
    raised = jnp.exp(masked - highest)
    probs = (raised / jnp.sum(raised, axis=1, keepdims=True)).astype(jnp.bfloat16)
    out = lax.dot_general(
        probs, keyval[HD:, :], (((1,), (1,)), ((), ())), preferred_element_type=jnp.float32
    ).astype(jnp.bfloat16)
    attended[...] = jnp.broadcast_to(out[None], attended.shape)


def mix_kernel(section, layout, earlier, own, other, before, *rest):
    past, rest = rest[:earlier], rest[earlier:]
    buffers, outs = rest[: len(layout)], rest[len(layout) :]
    second = is_other(section)
    width = before.shape[1]

    def body(chunk, mixed):
        weight = weight_rows(second, own, other, chunk, width)
        joined = jnp.concatenate([part for part, _ in chunk], axis=1)
        return mixed + jnp.dot(joined, weight, preferred_element_type=jnp.float32)

    mixed = for_chunks(buffers, layout, body, before[...].astype(jnp.float32))
    out = mixed.astype(outs[0].dtype)
    if past:
        lower = lax.axis_index("section") == 0
        outs[0][...] = jnp.where(lower, past[0][...], out)
        outs[1][...] = jnp.where(lower, out, past[0][...])
        return
    outs[0][...] = out
    if len(outs) > 1:
        outs[1][...] = jnp.broadcast_to(out[None], outs[1].shape)


def place_kernel(mine, theirs, result):
    me = lax.axis_index("section")
    result[me] = mine[...]
    result[1 - me] = theirs[...]


def call(kernel, outs, limit, *args):
    vmem = pl.BlockSpec(memory_space=pltpu.VMEM)
    return pl.pallas_call(
        kernel,
        out_shape=outs,
        in_specs=[vmem] * len(args),
        out_specs=jax.tree.map(lambda _: vmem, outs),
        compiler_params=pltpu.CompilerParams(vmem_limit_bytes=limit * MIB),
    )(*args)


def from_neighbour(block, dx, dy):
    pairs = []
    for x in range(SIDE):
        for y in range(SIDE):
            there = (x + dx) % SIDE * SIDE + (y + dy) % SIDE
            pairs.append((there, x * SIDE + y))
    return lax.ppermute(block, MESH, pairs)


def far_stage(copies):
    return lax.all_to_all(copies, FAR, 0, 0, tiled=True)


def near_stage(own):
    low, high = own[:8], own[8:]
    xa, xb = from_neighbour(low, 1, 0), from_neighbour(high, -1, 0)
    ya, yb = from_neighbour(low, 0, 1), from_neighbour(high, 0, -1)
    da, db = from_neighbour(xa, 0, 1), from_neighbour(xb, 0, -1)
    return (own,), (xa, xb, ya, yb), (da, db)


def shards(inputs, segments, gains, w_query, w_keyval, w_output):
    _, rows, width = inputs.shape
    sections = lax.axis_size("section")
    ring = lax.axis_size(Y)
    me = lax.axis_index("section")
    swap = [(0, 1), (1, 0)]
    own = [w_query[0, 0], w_keyval[0, 0].T, w_output[0, 0]]
    gain = gains[0].astype(jnp.float32).reshape(-1, 1, width)
    current = lax.dynamic_index_in_dim(inputs, me, 0, keepdims=False)
    segment_row = lax.dynamic_index_in_dim(segments, me, 0, keepdims=False)
    cosine, sine, allowed = position_tables(segment_row)
    copies = jnp.broadcast_to(current[None], (FAR_COUNT, rows, width))
    copies, cosine, sine, allowed, gain = lax.optimization_barrier(
        (copies, cosine, sine, allowed, gain)
    )
    shape = jax.ShapeDtypeStruct
    bf16 = functools.partial(shape, dtype=jnp.bfloat16)
    f32 = functools.partial(shape, dtype=jnp.float32)
    columns = own[1].shape[0]
    stages = len(STAGES)
    for s in range(sections):
        far = far_stage(copies)
        if s == 0:
            far, gain, *own = lax.optimization_barrier((far, gain, *own))
            other_gain = lax.ppermute(gain, "section", swap)
            other = [lax.ppermute(w, "section", swap) for w in own]
        near = near_stage(far)
        sums = ()
        for k, (group, layout) in enumerate(zip(near, STAGES, strict=True)):
            last = k == stages - 1
            outs = (f32((rows, width)), f32((columns, rows)), f32((rows, width)))
            if last:
                outs = (bf16((rows, width)), bf16((ring, columns, rows)))
            kernel = functools.partial(project_kernel, s, layout, k == 0, last)
            tables = (cosine, sine) if last else ()
            weights = (gain, other_gain, own[0], other[0], own[1], other[1])
            sums = call(kernel, outs, 10, *weights, *sums, *tables, *group)
        query, keyval = sums
        keyval = lax.all_to_all(keyval, Y, 0, 0, tiled=True).reshape(-1, rows)
        attended = call(
            attend_kernel, bf16((FAR_COUNT, rows, width)), 4, query, keyval, cosine, sine, allowed
        )
        near = near_stage(far_stage(attended))
        partial, end = current, s + 1 == sections
        for k, (group, layout) in enumerate(zip(near, STAGES, strict=True)):
            outs, past = (f32((rows, width)),), ()
            if k == stages - 1:
                outs = (bf16((rows, width)),)
                past = (current,) if end else ()
                outs += (bf16((rows, width)),) if end else (bf16((FAR_COUNT, rows, width)),)
            kernel = functools.partial(mix_kernel, s, layout, len(past))
            partial, *extra = call(kernel, outs, 10, own[2], other[2], partial, *past, *group)
        current, copies = partial, extra[0]
    theirs = lax.ppermute(copies, "section", swap)
    return call(place_kernel, bf16((sections, rows, width)), 4, current, theirs)[None]


def solution(mesh):
    finer = Mesh(
        mesh.devices.reshape(mesh.shape["groups"], mesh.shape["section"], *([2] * 6)),
        ("groups", "section") + MESH,
    )
    in_specs = (
        P("groups", None, MESH),
        P("groups", None),
        P("section", None, None),
        P("section", None, None, MESH),
        P("section", None, None, MESH),
        P("section", None, None, MESH),
    )
    out_specs = P("section", "groups", None, MESH)
    return jax.shard_map(
        shards, mesh=finer, in_specs=in_specs, out_specs=out_specs, check_vma=False
    )
```

time: 332 us -> 215 us (0.65)
  waiting for transfers between devices: 159 us -> 33.2 us
  blocking collectives: 77.7 us -> 121 us
  Pallas kernels: 29 us -> 15.1 us
  starting transfers between devices: 51.6 us -> 40.9 us
  local copies, waits for them, and re-layouts: 9.63 us -> 1.12 us
    all_to_all x4 -> x0, waiting for transfers between devices: 154 us -> none  [the longest x3 148 us: exchange(): return lax.all_to_all(copies, MESH, 0, 0, tiled=True)]
    all_to_all x4 -> x0, starting transfers between devices: 44.3 us -> none  [the longest x3 40.8 us: exchange(): return lax.all_to_all(copies, MESH, 0, 0, tiled=True)]
    all_to_all x1 -> x4, blocking collectives: 66.4 us -> 100 us  [far_stage(): return lax.all_to_all(copies, FAR, 0, 0, tiled=True)]
    ppermute x2 -> x26, starting transfers between devices: 3.56 us -> 37.5 us  [the longest x24 28.9 us: from_neighbour(): return lax.ppermute(block, MESH, pairs)]
    ppermute x2 -> x26, waiting for transfers between devices: 0.86 us -> 33.2 us  [the longest x24 31.5 us: from_neighbour(): return lax.ppermute(block, MESH, pairs)]
    pallas_call x6 -> x15, Pallas kernels: 29 us -> 15.1 us  [call(): pl.pallas_call(kernel, out_shape=outs, in_specs=[vmem] * len(args), out_s...]
    all_to_all x1 -> x2, blocking collectives: 11.3 us -> 20.7 us  [shards(): keyval = lax.all_to_all(keyval, Y, 0, 0, tiled=True).reshape(-1, rows)]
    unnamed x21 -> x8, local copies, waits for them, and re-layouts: 5.97 us -> 0.02 us
  transfers between devices with their start and end apart: 9 -> 29, of which waited for: 6 -> 16; matrix products, arithmetic and copies ran while one was open for 2% -> 0% of each run, Pallas kernels for 0% -> 5%
where the time goes in v2:
time: 215 us; the launch traced here: 213 us
  blocking collectives  121 us (56%)
  starting transfers between devices  40.9 us (19%)
  waiting for transfers between devices  33.2 us (15%)
  Pallas kernels  15.1 us (7%)
    all_to_all x4, blocking collectives, far_stage(): return lax.all_to_all(copies, FAR, 0, 0, tiled=True)  100 us
    ppermute x24, waiting for transfers between devices, from_neighbour(): return lax.ppermute(block, MESH, pairs)  31.5 us
    ppermute x24, starting transfers between devices, from_neighbour(): return lax.ppermute(block, MESH, pairs)  28.9 us
    all_to_all x2, blocking collectives, shards(): keyval = lax.all_to_all(keyval, Y, 0, 0, tiled=True).reshape(-1, rows)  20.7 us
    pallas_call x15, Pallas kernels, call(): pl.pallas_call(kernel, out_shape=outs, in_specs=[vmem] * len(args), out_s...  15.1 us
    ppermute x1, starting transfers between devices, shards(): theirs = lax.ppermute(copies, 'section', swap)  7.75 us
  transfers between devices with their start and end apart: 29, of which 16 were waited for; matrix products, arithmetic and copies ran while one was open for 0% of the time, Pallas kernels for 5%

profile of v2, /device:TPU:647, one launch (start us, length us, event | category | flops | bytes accessed | tf_op | source)
XLA Modules:
  0.0 213.2 jit_solution(1924130680903928379)
XLA Ops:
  0.0 0.8 dynamic-slice_bitcast_fusion.1
  0.9 0.2 fusion
  1.2 0.8 bitcast_convert_fusion.gain_own
  2.0 0.3 fusion.2
  2.5 32.2 %all_to_all.30.rest_0_ = bf16[16,128,128]{2,1,0:T(8,128)(2,1)S(1)} all-to-all(bf16[16,128,128]{2,1,0:T(8,128)(2,1)S(1)} %broadcast_in_dim.33), channel_id=1, replica_groups=mesh['groups'=2,'section'=2,'x2'=2,'x1'=2,'x0'=2,'y2'=2,'y1'=2,'y0'=2] {..., dimensions={0} | all-to-all | bytes 1048576 | tf_op jit(solution)/shard_map/all_to_all | solution.py:201
  34.7 1.5 collective-permute-start.2
  36.3 4.1 %collective-permute-start.4 = (bf16[8,128,128]{2,1,0:T(8,128)(2,1)S(1)}, bf16[8,128,128]{2,1,0:T(8,128)(2,1)S(1)}, u32[]{:S(2)}, u32[]{:S(2)}) collective-permute-start(bf16[8,128,128]{2,1,0:T(8,128)(2,1)S(1)} %get-tuple-element.72), channel_id=1, source_target_pairs={{8,0},{9,1},{10,2},{11,3},{12,4},{13,5},{14,6},{15,7},{16,8},{17,9... | collective-permute-start | bytes 786440 | tf_op jit(solution)/shard_map/ppermute | solution.py:197
  40.4 0.5 collective-permute-start.5
  40.9 0.8 collective-permute-start.1
  41.7 0.9 collective-permute-done.1.gain_other
  42.6 2.0 collective-permute-start.6
  44.5 2.4 %collective-permute-done.4.rest_3_ = bf16[8,128,128]{2,1,0:T(8,128)(2,1)S(1)} collective-permute-done((bf16[8,128,128]{2,1,0:T(8,128)(2,1)S(1)}, bf16[8,128,128]{2,1,0:T(8,128)(2,1)S(1)}, u32[]{:S(2)}, u32[]{:S(2)}) %collective-permute-start.4) | collective-permute-done | bytes 262176 | tf_op jit(solution)/shard_map/ppermute | solution.py:197
  47.0 2.3 %collective-permute-start.7 = (bf16[8,128,128]{2,1,0:T(8,128)(2,1)S(1)}, bf16[8,128,128]{2,1,0:T(8,128)(2,1)S(1)}, u32[]{:S(2)}, u32[]{:S(2)}) collective-permute-start(bf16[8,128,128]{2,1,0:T(8,128)(2,1)S(1)} %get-tuple-element.71), channel_id=1, source_target_pairs={{7,0},{0,1},{1,2},{2,3},{3,4},{4,5},{5,6},{6,7},{15,8},{8,9},{9,10... | collective-permute-start | bytes 786440 | tf_op jit(solution)/shard_map/ppermute | solution.py:197
  49.3 0.7 collective-permute-start.8
  50.0 0.8 collective-permute-start.9
  50.7 1.9 collective-permute-start
  52.7 0.9 shard_map.64
  53.5 1.4 collective-permute-done.7.rest_6_
  54.9 1.7 shard_map.65
  56.7 3.9 %collective-permute-done.9.rest_6_ = bf16[8,128,128]{2,1,0:T(8,128)(2,1)S(1)} collective-permute-done((bf16[8,128,128]{2,1,0:T(8,128)(2,1)S(1)}, bf16[8,128,128]{2,1,0:T(8,128)(2,1)S(1)}, u32[]{:S(2)}, u32[]{:S(2)}) %collective-permute-start.9) | collective-permute-done | bytes 262176 | tf_op jit(solution)/shard_map/ppermute | solution.py:197
  60.6 1.1 shard_map.66
  61.6 11.0 %all_to_all.31 = bf16[8,32,128]{2,1,0:T(8,128)(2,1)S(1)} all-to-all(bf16[8,32,128]{2,1,0:T(8,128)(2,1)S(1)} %get-tuple-element.51), channel_id=1, replica_groups=mesh['groups'=2,'section'=2,'x2'=2,'x1'=2,'x0'=2,'y2'=2,'y1'=2,'y0'=2] {..., dimensions={0} | all-to-all | bytes 131072 | tf_op jit(solution)/shard_map/all_to_all | solution.py:250
  72.6 0.5 shard_map.67
  73.2 21.7 %all_to_all.32.rest_0_ = bf16[16,128,128]{2,1,0:T(8,128)(2,1)S(1)} all-to-all(bf16[16,128,128]{2,1,0:T(8,128)(2,1)S(1)} %shard_map.67), channel_id=1, replica_groups=mesh['groups'=2,'section'=2,'x2'=2,'x1'=2,'x0'=2,'y2'=2,'y1'=2,'y0'=2] {..., dimensions={0} | all-to-all | bytes 1048576 | tf_op jit(solution)/shard_map/all_to_all | solution.py:201
  94.9 0.1 collective-permute-start.10
  95.1 2.6 %collective-permute-start.11 = (bf16[8,128,128]{2,1,0:T(8,128)(2,1)S(1)}, bf16[8,128,128]{2,1,0:T(8,128)(2,1)S(1)}, u32[]{:S(2)}, u32[]{:S(2)}) collective-permute-start(bf16[8,128,128]{2,1,0:T(8,128)(2,1)S(1)} %get-tuple-element.69), channel_id=1, source_target_pairs={{56,0},{57,1},{58,2},{59,3},{60,4},{61,5},{62,6},{63,7},{0,8},{1,9... | collective-permute-start | bytes 786440 | tf_op jit(solution)/shard_map/ppermute | solution.py:197
  97.7 1.5 collective-permute-start.12
  99.3 0.2 collective-permute-start.13
  99.5 2.3 %collective-permute-done.10.rest_0_ = bf16[8,128,128]{2,1,0:T(8,128)(2,1)S(1)} collective-permute-done((bf16[8,128,128]{2,1,0:T(8,128)(2,1)S(1)}, bf16[8,128,128]{2,1,0:T(8,128)(2,1)S(1)}, u32[]{:S(2)}, u32[]{:S(2)}) %collective-permute-start.10) | collective-permute-done | bytes 262176 | tf_op jit(solution)/shard_map/ppermute | solution.py:197
  101.8 1.2 collective-permute-start.14
  103.0 0.5 collective-permute-done.11.rest_1_
  103.6 2.8 %collective-permute-start.15 = (bf16[8,128,128]{2,1,0:T(8,128)(2,1)S(1)}, bf16[8,128,128]{2,1,0:T(8,128)(2,1)S(1)}, u32[]{:S(2)}, u32[]{:S(2)}) collective-permute-start(bf16[8,128,128]{2,1,0:T(8,128)(2,1)S(1)} %collective-permute-done.11.rest_1_), channel_id=1, source_target_pairs={{7,0},{0,1},{1,2},{2,3},{3,4},{4,5},{5,6},{6,7},{15,8},{8,9},{9,10... | collective-permute-start | bytes 786440 | tf_op jit(solution)/shard_map/ppermute | solution.py:197
  106.4 0.8 shard_map.68.before
  107.2 1.5 shard_map.69.before
  108.7 1.4 collective-permute-done.14.rest_0_
  110.1 3.0 %collective-permute-done.15.rest_1_ = bf16[8,128,128]{2,1,0:T(8,128)(2,1)S(1)} collective-permute-done((bf16[8,128,128]{2,1,0:T(8,128)(2,1)S(1)}, bf16[8,128,128]{2,1,0:T(8,128)(2,1)S(1)}, u32[]{:S(2)}, u32[]{:S(2)}) %collective-permute-start.15) | collective-permute-done | bytes 262176 | tf_op jit(solution)/shard_map/ppermute | solution.py:197
  113.1 0.8 shard_map.70
  113.9 25.7 %all_to_all.33.rest_0_ = bf16[16,128,128]{2,1,0:T(8,128)(2,1)S(1)} all-to-all(bf16[16,128,128]{2,1,0:T(8,128)(2,1)S(1)} %get-tuple-element.54), channel_id=1, replica_groups=mesh['groups'=2,'section'=2,'x2'=2,'x1'=2,'x0'=2,'y2'=2,'y1'=2,'y0'=2] {..., dimensions={0} | all-to-all | bytes 1048576 | tf_op jit(solution)/shard_map/all_to_all | solution.py:201
  139.7 0.1 collective-permute-start.16
  139.8 2.6 %collective-permute-start.17 = (bf16[8,128,128]{2,1,0:T(8,128)(2,1)S(1)}, bf16[8,128,128]{2,1,0:T(8,128)(2,1)S(1)}, u32[]{:S(2)}, u32[]{:S(2)}) collective-permute-start(bf16[8,128,128]{2,1,0:T(8,128)(2,1)S(1)} %get-tuple-element.67), channel_id=1, source_target_pairs={{56,0},{57,1},{58,2},{59,3},{60,4},{61,5},{62,6},{63,7},{0,8},{1,9... | collective-permute-start | bytes 786440 | tf_op jit(solution)/shard_map/ppermute | solution.py:197
  142.5 1.5 collective-permute-start.19
  143.9 3.9 %collective-permute-done.16.rest_3_ = bf16[8,128,128]{2,1,0:T(8,128)(2,1)S(1)} collective-permute-done((bf16[8,128,128]{2,1,0:T(8,128)(2,1)S(1)}, bf16[8,128,128]{2,1,0:T(8,128)(2,1)S(1)}, u32[]{:S(2)}, u32[]{:S(2)}) %collective-permute-start.16) | collective-permute-done | bytes 262176 | tf_op jit(solution)/shard_map/ppermute | solution.py:197
  147.8 1.5 collective-permute-done.17.rest_4_
  149.3 0.9 shard_map.71
  150.2 1.7 shard_map.72
  151.9 2.4 %collective-permute-done.20.rest_5_ = bf16[8,128,128]{2,1,0:T(8,128)(2,1)S(1)} collective-permute-done((bf16[8,128,128]{2,1,0:T(8,128)(2,1)S(1)}, bf16[8,128,128]{2,1,0:T(8,128)(2,1)S(1)}, u32[]{:S(2)}, u32[]{:S(2)}) %collective-permute-start.20) | collective-permute-done | bytes 262176 | tf_op jit(solution)/shard_map/ppermute | solution.py:197
  154.3 2.4 %collective-permute-done.21.rest_6_ = bf16[8,128,128]{2,1,0:T(8,128)(2,1)S(1)} collective-permute-done((bf16[8,128,128]{2,1,0:T(8,128)(2,1)S(1)}, bf16[8,128,128]{2,1,0:T(8,128)(2,1)S(1)}, u32[]{:S(2)}, u32[]{:S(2)}) %collective-permute-start.21) | collective-permute-done | bytes 262176 | tf_op jit(solution)/shard_map/ppermute | solution.py:197
  156.7 1.1 shard_map.73
  157.7 9.7 %all_to_all.34 = bf16[8,32,128]{2,1,0:T(8,128)(2,1)S(1)} all-to-all(bf16[8,32,128]{2,1,0:T(8,128)(2,1)S(1)} %get-tuple-element.62), channel_id=1, replica_groups=mesh['groups'=2,'section'=2,'x2'=2,'x1'=2,'x0'=2,'y2'=2,'y1'=2,'y0'=2] {..., dimensions={0} | all-to-all | bytes 131072 | tf_op jit(solution)/shard_map/all_to_all | solution.py:250
  167.4 0.5 shard_map.74
  168.0 20.7 %all_to_all.35.rest_0_ = bf16[16,128,128]{2,1,0:T(8,128)(2,1)S(1)} all-to-all(bf16[16,128,128]{2,1,0:T(8,128)(2,1)S(1)} %shard_map.74), channel_id=1, replica_groups=mesh['groups'=2,'section'=2,'x2'=2,'x1'=2,'x0'=2,'y2'=2,'y1'=2,'y0'=2] {..., dimensions={0} | all-to-all | bytes 1048576 | tf_op jit(solution)/shard_map/all_to_all | solution.py:201
  188.8 0.1 collective-permute-start.22
  188.9 2.6 %collective-permute-start.23 = (bf16[8,128,128]{2,1,0:T(8,128)(2,1)S(1)}, bf16[8,128,128]{2,1,0:T(8,128)(2,1)S(1)}, u32[]{:S(2)}, u32[]{:S(2)}) collective-permute-start(bf16[8,128,128]{2,1,0:T(8,128)(2,1)S(1)} %get-tuple-element.65), channel_id=1, source_target_pairs={{56,0},{57,1},{58,2},{59,3},{60,4},{61,5},{62,6},{63,7},{0,8},{1,9... | collective-permute-start | bytes 786440 | tf_op jit(solution)/shard_map/ppermute | solution.py:197
  191.6 1.4 collective-permute-start.25
  193.0 2.3 %collective-permute-done.22.rest_0_ = bf16[8,128,128]{2,1,0:T(8,128)(2,1)S(1)} collective-permute-done((bf16[8,128,128]{2,1,0:T(8,128)(2,1)S(1)}, bf16[8,128,128]{2,1,0:T(8,128)(2,1)S(1)}, u32[]{:S(2)}, u32[]{:S(2)}) %collective-permute-start.22) | collective-permute-done | bytes 262176 | tf_op jit(solution)/shard_map/ppermute | solution.py:197
  195.4 1.4 collective-permute-start.27
  196.8 0.8 shard_map.75.before
  197.5 0.8 collective-permute-done.25.rest_3_
  198.3 1.5 shard_map.76.before
  199.9 3.3 %collective-permute-done.26.rest_1_ = bf16[8,128,128]{2,1,0:T(8,128)(2,1)S(1)} collective-permute-done((bf16[8,128,128]{2,1,0:T(8,128)(2,1)S(1)}, bf16[8,128,128]{2,1,0:T(8,128)(2,1)S(1)}, u32[]{:S(2)}, u32[]{:S(2)}) %collective-permute-start.26) | collective-permute-done | bytes 262176 | tf_op jit(solution)/shard_map/ppermute | solution.py:197
  203.2 0.8 shard_map.77
  203.9 7.7 %collective-permute-start.28 = (bf16[128,128]{1,0:T(8,128)(2,1)S(1)}, bf16[128,128]{1,0:T(8,128)(2,1)S(1)}, u32[]{:S(2)}, u32[]{:S(2)}) collective-permute-start(bf16[128,128]{1,0:T(8,128)(2,1)S(1)} %get-tuple-element.64), channel_id=1, source_target_pairs={{0,64},{64,0},{1,65},{65,1},{2,66},{66,2},{3,67},{67,3},{4,68},{68... | collective-permute-start | bytes 98312 | tf_op jit(solution)/shard_map/ppermute | solution.py:265
  211.7 0.9 collective-permute-done.28.theirs
  212.5 0.6 shard_map.78
  (37 shorter events, 0.7 us)
Async XLA Ops:
  0.0 1.2 copy-start
  0.0 34.7 %copy-start.1 = (bf16[1,1,8192,128]{3,2,1,0:T(8,128)(2,1)S(1)}, bf16[1,1,8192,128]{3,2,1,0:T(8,128)(2,1)}, u32[]{:S(2)}) copy-start(bf16[1,1,8192,128]{3,2,1,0:T(8,128)(2,1)} %param.9) | copy-start | bytes 6291460
  0.0 52.7 %copy-start.3 = (bf16[1,1,8192,32]{2,3,1,0:T(8,128)(2,1)S(1)}, bf16[1,1,8192,32]{2,3,1,0:T(8,128)(2,1)}, u32[]{:S(2)}) copy-start(bf16[1,1,8192,32]{2,3,1,0:T(8,128)(2,1)} %param.10) | copy-start | bytes 1572868
  34.7 16.0 %collective-permute-start.2 = (bf16[8192,128]{1,0:T(8,128)(2,1)S(1)}, bf16[8192,128]{1,0:T(8,128)(2,1)S(1)}, u32[]{:S(2)}, u32[]{:S(2)}) collective-permute-start(bf16[8192,128]{1,0:T(8,128)(2,1)S(1)} %bitcast.15), channel_id=1, source_target_pairs={{0,64},{64,0},{1,65},{65,1},{2,66},{66,2},{3,67},{67,3},{4,68},{68... | collective-permute-start | bytes 6291464 | tf_op jit(solution)/shard_map/ppermute | solution.py:237
  36.2 13.7 %collective-permute-start.3 = (bf16[32,8192]{1,0:T(8,128)(2,1)}, bf16[32,8192]{1,0:T(8,128)(2,1)S(1)}, u32[]{:S(2)}, u32[]{:S(2)}) collective-permute-start(bf16[32,8192]{1,0:T(8,128)(2,1)} %bitcast.29), channel_id=1, source_target_pairs={{0,64},{64,0},{1,65},{65,1},{2,66},{66,2},{3,67},{67,3},{4,68},{68... | collective-permute-start | bytes 1572872 | tf_op jit(solution)/shard_map/ppermute | solution.py:237
  36.3 10.7 %collective-permute-start.4 = (bf16[8,128,128]{2,1,0:T(8,128)(2,1)S(1)}, bf16[8,128,128]{2,1,0:T(8,128)(2,1)S(1)}, u32[]{:S(2)}, u32[]{:S(2)}) collective-permute-start(bf16[8,128,128]{2,1,0:T(8,128)(2,1)S(1)} %get-tuple-element.72), channel_id=1, source_target_pairs={{8,0},{9,1},{10,2},{11,3},{12,4},{13,5},{14,6},{15,7},{16,8},{17,9... | collective-permute-start | bytes 786440 | tf_op jit(solution)/shard_map/ppermute | solution.py:197
  40.4 8.9 %collective-permute-start.5 = (bf16[8,128,128]{2,1,0:T(8,128)(2,1)S(1)}, bf16[8,128,128]{2,1,0:T(8,128)(2,1)S(1)}, u32[]{:S(2)}, u32[]{:S(2)}) collective-permute-start(bf16[8,128,128]{2,1,0:T(8,128)(2,1)S(1)} %get-tuple-element.71), channel_id=1, source_target_pairs={{56,0},{57,1},{58,2},{59,3},{60,4},{61,5},{62,6},{63,7},{0,8},{1,9... | collective-permute-start | bytes 786440 | tf_op jit(solution)/shard_map/ppermute | solution.py:197
  40.9 1.6 collective-permute-start.1
  42.6 11.0 %collective-permute-start.6 = (bf16[8,128,128]{2,1,0:T(8,128)(2,1)S(1)}, bf16[8,128,128]{2,1,0:T(8,128)(2,1)S(1)}, u32[]{:S(2)}, u32[]{:S(2)}) collective-permute-start(bf16[8,128,128]{2,1,0:T(8,128)(2,1)S(1)} %get-tuple-element.72), channel_id=1, source_target_pairs={{1,0},{2,1},{3,2},{4,3},{5,4},{6,5},{7,6},{0,7},{9,8},{10,9},{11,1... | collective-permute-start | bytes 786440 | tf_op jit(solution)/shard_map/ppermute | solution.py:197
  47.0 8.0 %collective-permute-start.7 = (bf16[8,128,128]{2,1,0:T(8,128)(2,1)S(1)}, bf16[8,128,128]{2,1,0:T(8,128)(2,1)S(1)}, u32[]{:S(2)}, u32[]{:S(2)}) collective-permute-start(bf16[8,128,128]{2,1,0:T(8,128)(2,1)S(1)} %get-tuple-element.71), channel_id=1, source_target_pairs={{7,0},{0,1},{1,2},{2,3},{3,4},{4,5},{5,6},{6,7},{15,8},{8,9},{9,10... | collective-permute-start | bytes 786440 | tf_op jit(solution)/shard_map/ppermute | solution.py:197
  49.3 7.4 %collective-permute-start.8 = (bf16[8,128,128]{2,1,0:T(8,128)(2,1)S(1)}, bf16[8,128,128]{2,1,0:T(8,128)(2,1)S(1)}, u32[]{:S(2)}, u32[]{:S(2)}) collective-permute-start(bf16[8,128,128]{2,1,0:T(8,128)(2,1)S(1)} %collective-permute-done.4.rest_3_), channel_id=1, source_target_pairs={{1,0},{2,1},{3,2},{4,3},{5,4},{6,5},{7,6},{0,7},{9,8},{10,9},{11,1... | collective-permute-start | bytes 786440 | tf_op jit(solution)/shard_map/ppermute | solution.py:197
  50.0 10.6 %collective-permute-start.9 = (bf16[8,128,128]{2,1,0:T(8,128)(2,1)S(1)}, bf16[8,128,128]{2,1,0:T(8,128)(2,1)S(1)}, u32[]{:S(2)}, u32[]{:S(2)}) collective-permute-start(bf16[8,128,128]{2,1,0:T(8,128)(2,1)S(1)} %collective-permute-done.5.rest_4_), channel_id=1, source_target_pairs={{7,0},{0,1},{1,2},{2,3},{3,4},{4,5},{5,6},{6,7},{15,8},{8,9},{9,10... | collective-permute-start | bytes 786440 | tf_op jit(solution)/shard_map/ppermute | solution.py:197
  50.7 55.7 %collective-permute-start = (bf16[8192,128]{1,0:T(8,128)(2,1)}, bf16[8192,128]{1,0:T(8,128)(2,1)S(1)}, u32[]{:S(2)}, u32[]{:S(2)}) collective-permute-start(bf16[8192,128]{1,0:T(8,128)(2,1)} %bitcast.22), channel_id=1, source_target_pairs={{0,64},{64,0},{1,65},{65,1},{2,66},{66,2},{3,67},{67,3},{4,68},{68... | collective-permute-start | bytes 6291464 | tf_op jit(solution)/shard_map/ppermute | solution.py:237
  61.6 44.8 %copy-start.2 = (bf16[1,1,8192,128]{3,2,1,0:T(8,128)(2,1)S(1)}, bf16[1,1,8192,128]{3,2,1,0:T(8,128)(2,1)}, u32[]{:S(2)}) copy-start(bf16[1,1,8192,128]{3,2,1,0:T(8,128)(2,1)} %param.11) | copy-start | bytes 6291460
  94.9 6.9 %collective-permute-start.10 = (bf16[8,128,128]{2,1,0:T(8,128)(2,1)S(1)}, bf16[8,128,128]{2,1,0:T(8,128)(2,1)S(1)}, u32[]{:S(2)}, u32[]{:S(2)}) collective-permute-start(bf16[8,128,128]{2,1,0:T(8,128)(2,1)S(1)} %get-tuple-element.70), channel_id=1, source_target_pairs={{8,0},{9,1},{10,2},{11,3},{12,4},{13,5},{14,6},{15,7},{16,8},{17,9... | collective-permute-start | bytes 786440 | tf_op jit(solution)/shard_map/ppermute | solution.py:197
  95.1 8.5 %collective-permute-start.11 = (bf16[8,128,128]{2,1,0:T(8,128)(2,1)S(1)}, bf16[8,128,128]{2,1,0:T(8,128)(2,1)S(1)}, u32[]{:S(2)}, u32[]{:S(2)}) collective-permute-start(bf16[8,128,128]{2,1,0:T(8,128)(2,1)S(1)} %get-tuple-element.69), channel_id=1, source_target_pairs={{56,0},{57,1},{58,2},{59,3},{60,4},{61,5},{62,6},{63,7},{0,8},{1,9... | collective-permute-start | bytes 786440 | tf_op jit(solution)/shard_map/ppermute | solution.py:197
  97.7 9.5 %collective-permute-start.12 = (bf16[8,128,128]{2,1,0:T(8,128)(2,1)S(1)}, bf16[8,128,128]{2,1,0:T(8,128)(2,1)S(1)}, u32[]{:S(2)}, u32[]{:S(2)}) collective-permute-start(bf16[8,128,128]{2,1,0:T(8,128)(2,1)S(1)} %get-tuple-element.70), channel_id=1, source_target_pairs={{1,0},{2,1},{3,2},{4,3},{5,4},{6,5},{7,6},{0,7},{9,8},{10,9},{11,1... | collective-permute-start | bytes 786440 | tf_op jit(solution)/shard_map/ppermute | solution.py:197
  99.3 7.9 %collective-permute-start.13 = (bf16[8,128,128]{2,1,0:T(8,128)(2,1)S(1)}, bf16[8,128,128]{2,1,0:T(8,128)(2,1)S(1)}, u32[]{:S(2)}, u32[]{:S(2)}) collective-permute-start(bf16[8,128,128]{2,1,0:T(8,128)(2,1)S(1)} %get-tuple-element.69), channel_id=1, source_target_pairs={{7,0},{0,1},{1,2},{2,3},{3,4},{4,5},{5,6},{6,7},{15,8},{8,9},{9,10... | collective-permute-start | bytes 786440 | tf_op jit(solution)/shard_map/ppermute | solution.py:197
  101.8 8.3 %collective-permute-start.14 = (bf16[8,128,128]{2,1,0:T(8,128)(2,1)S(1)}, bf16[8,128,128]{2,1,0:T(8,128)(2,1)S(1)}, u32[]{:S(2)}, u32[]{:S(2)}) collective-permute-start(bf16[8,128,128]{2,1,0:T(8,128)(2,1)S(1)} %collective-permute-done.10.rest_0_), channel_id=1, source_target_pairs={{1,0},{2,1},{3,2},{4,3},{5,4},{6,5},{7,6},{0,7},{9,8},{10,9},{11,1... | collective-permute-start | bytes 786440 | tf_op jit(solution)/shard_map/ppermute | solution.py:197
  103.6 9.5 %collective-permute-start.15 = (bf16[8,128,128]{2,1,0:T(8,128)(2,1)S(1)}, bf16[8,128,128]{2,1,0:T(8,128)(2,1)S(1)}, u32[]{:S(2)}, u32[]{:S(2)}) collective-permute-start(bf16[8,128,128]{2,1,0:T(8,128)(2,1)S(1)} %collective-permute-done.11.rest_1_), channel_id=1, source_target_pairs={{7,0},{0,1},{1,2},{2,3},{3,4},{4,5},{5,6},{6,7},{15,8},{8,9},{9,10... | collective-permute-start | bytes 786440 | tf_op jit(solution)/shard_map/ppermute | solution.py:197
  139.7 8.1 %collective-permute-start.16 = (bf16[8,128,128]{2,1,0:T(8,128)(2,1)S(1)}, bf16[8,128,128]{2,1,0:T(8,128)(2,1)S(1)}, u32[]{:S(2)}, u32[]{:S(2)}) collective-permute-start(bf16[8,128,128]{2,1,0:T(8,128)(2,1)S(1)} %get-tuple-element.68), channel_id=1, source_target_pairs={{8,0},{9,1},{10,2},{11,3},{12,4},{13,5},{14,6},{15,7},{16,8},{17,9... | collective-permute-start | bytes 786440 | tf_op jit(solution)/shard_map/ppermute | solution.py:197
  139.8 9.5 %collective-permute-start.17 = (bf16[8,128,128]{2,1,0:T(8,128)(2,1)S(1)}, bf16[8,128,128]{2,1,0:T(8,128)(2,1)S(1)}, u32[]{:S(2)}, u32[]{:S(2)}) collective-permute-start(bf16[8,128,128]{2,1,0:T(8,128)(2,1)S(1)} %get-tuple-element.67), channel_id=1, source_target_pairs={{56,0},{57,1},{58,2},{59,3},{60,4},{61,5},{62,6},{63,7},{0,8},{1,9... | collective-permute-start | bytes 786440 | tf_op jit(solution)/shard_map/ppermute | solution.py:197
  142.5 7.7 %collective-permute-start.18 = (bf16[8,128,128]{2,1,0:T(8,128)(2,1)S(1)}, bf16[8,128,128]{2,1,0:T(8,128)(2,1)S(1)}, u32[]{:S(2)}, u32[]{:S(2)}) collective-permute-start(bf16[8,128,128]{2,1,0:T(8,128)(2,1)S(1)} %get-tuple-element.68), channel_id=1, source_target_pairs={{1,0},{2,1},{3,2},{4,3},{5,4},{6,5},{7,6},{0,7},{9,8},{10,9},{11,1... | collective-permute-start | bytes 786440 | tf_op jit(solution)/shard_map/ppermute | solution.py:197
  142.5 7.7 %collective-permute-start.19 = (bf16[8,128,128]{2,1,0:T(8,128)(2,1)S(1)}, bf16[8,128,128]{2,1,0:T(8,128)(2,1)S(1)}, u32[]{:S(2)}, u32[]{:S(2)}) collective-permute-start(bf16[8,128,128]{2,1,0:T(8,128)(2,1)S(1)} %get-tuple-element.67), channel_id=1, source_target_pairs={{7,0},{0,1},{1,2},{2,3},{3,4},{4,5},{5,6},{6,7},{15,8},{8,9},{9,10... | collective-permute-start | bytes 786440 | tf_op jit(solution)/shard_map/ppermute | solution.py:197
  147.8 6.5 %collective-permute-start.20 = (bf16[8,128,128]{2,1,0:T(8,128)(2,1)S(1)}, bf16[8,128,128]{2,1,0:T(8,128)(2,1)S(1)}, u32[]{:S(2)}, u32[]{:S(2)}) collective-permute-start(bf16[8,128,128]{2,1,0:T(8,128)(2,1)S(1)} %collective-permute-done.16.rest_3_), channel_id=1, source_target_pairs={{1,0},{2,1},{3,2},{4,3},{5,4},{6,5},{7,6},{0,7},{9,8},{10,9},{11,1... | collective-permute-start | bytes 786440 | tf_op jit(solution)/shard_map/ppermute | solution.py:197
  149.3 7.4 %collective-permute-start.21 = (bf16[8,128,128]{2,1,0:T(8,128)(2,1)S(1)}, bf16[8,128,128]{2,1,0:T(8,128)(2,1)S(1)}, u32[]{:S(2)}, u32[]{:S(2)}) collective-permute-start(bf16[8,128,128]{2,1,0:T(8,128)(2,1)S(1)} %collective-permute-done.17.rest_4_), channel_id=1, source_target_pairs={{7,0},{0,1},{1,2},{2,3},{3,4},{4,5},{5,6},{6,7},{15,8},{8,9},{9,10... | collective-permute-start | bytes 786440 | tf_op jit(solution)/shard_map/ppermute | solution.py:197
  188.8 6.5 %collective-permute-start.22 = (bf16[8,128,128]{2,1,0:T(8,128)(2,1)S(1)}, bf16[8,128,128]{2,1,0:T(8,128)(2,1)S(1)}, u32[]{:S(2)}, u32[]{:S(2)}) collective-permute-start(bf16[8,128,128]{2,1,0:T(8,128)(2,1)S(1)} %get-tuple-element.66), channel_id=1, source_target_pairs={{8,0},{9,1},{10,2},{11,3},{12,4},{13,5},{14,6},{15,7},{16,8},{17,9... | collective-permute-start | bytes 786440 | tf_op jit(solution)/shard_map/ppermute | solution.py:197
  188.9 6.5 %collective-permute-start.23 = (bf16[8,128,128]{2,1,0:T(8,128)(2,1)S(1)}, bf16[8,128,128]{2,1,0:T(8,128)(2,1)S(1)}, u32[]{:S(2)}, u32[]{:S(2)}) collective-permute-start(bf16[8,128,128]{2,1,0:T(8,128)(2,1)S(1)} %get-tuple-element.65), channel_id=1, source_target_pairs={{56,0},{57,1},{58,2},{59,3},{60,4},{61,5},{62,6},{63,7},{0,8},{1,9... | collective-permute-start | bytes 786440 | tf_op jit(solution)/shard_map/ppermute | solution.py:197
  191.5 6.0 %collective-permute-start.24 = (bf16[8,128,128]{2,1,0:T(8,128)(2,1)S(1)}, bf16[8,128,128]{2,1,0:T(8,128)(2,1)S(1)}, u32[]{:S(2)}, u32[]{:S(2)}) collective-permute-start(bf16[8,128,128]{2,1,0:T(8,128)(2,1)S(1)} %get-tuple-element.66), channel_id=1, source_target_pairs={{1,0},{2,1},{3,2},{4,3},{5,4},{6,5},{7,6},{0,7},{9,8},{10,9},{11,1... | collective-permute-start | bytes 786440 | tf_op jit(solution)/shard_map/ppermute | solution.py:197
  191.6 6.7 %collective-permute-start.25 = (bf16[8,128,128]{2,1,0:T(8,128)(2,1)S(1)}, bf16[8,128,128]{2,1,0:T(8,128)(2,1)S(1)}, u32[]{:S(2)}, u32[]{:S(2)}) collective-permute-start(bf16[8,128,128]{2,1,0:T(8,128)(2,1)S(1)} %get-tuple-element.65), channel_id=1, source_target_pairs={{7,0},{0,1},{1,2},{2,3},{3,4},{4,5},{5,6},{6,7},{15,8},{8,9},{9,10... | collective-permute-start | bytes 786440 | tf_op jit(solution)/shard_map/ppermute | solution.py:197
  195.3 7.8 %collective-permute-start.26 = (bf16[8,128,128]{2,1,0:T(8,128)(2,1)S(1)}, bf16[8,128,128]{2,1,0:T(8,128)(2,1)S(1)}, u32[]{:S(2)}, u32[]{:S(2)}) collective-permute-start(bf16[8,128,128]{2,1,0:T(8,128)(2,1)S(1)} %collective-permute-done.22.rest_0_), channel_id=1, source_target_pairs={{1,0},{2,1},{3,2},{4,3},{5,4},{6,5},{7,6},{0,7},{9,8},{10,9},{11,1... | collective-permute-start | bytes 786440 | tf_op jit(solution)/shard_map/ppermute | solution.py:197
  195.4 7.8 %collective-permute-start.27 = (bf16[8,128,128]{2,1,0:T(8,128)(2,1)S(1)}, bf16[8,128,128]{2,1,0:T(8,128)(2,1)S(1)}, u32[]{:S(2)}, u32[]{:S(2)}) collective-permute-start(bf16[8,128,128]{2,1,0:T(8,128)(2,1)S(1)} %collective-permute-done.23.rest_1_), channel_id=1, source_target_pairs={{7,0},{0,1},{1,2},{2,3},{3,4},{4,5},{5,6},{6,7},{15,8},{8,9},{9,10... | collective-permute-start | bytes 786440 | tf_op jit(solution)/shard_map/ppermute | solution.py:197
  203.9 8.6 %collective-permute-start.28 = (bf16[128,128]{1,0:T(8,128)(2,1)S(1)}, bf16[128,128]{1,0:T(8,128)(2,1)S(1)}, u32[]{:S(2)}, u32[]{:S(2)}) collective-permute-start(bf16[128,128]{1,0:T(8,128)(2,1)S(1)} %get-tuple-element.64), channel_id=1, source_target_pairs={{0,64},{64,0},{1,65},{65,1},{2,66},{66,2},{3,67},{67,3},{4,68},{68... | collective-permute-start | bytes 98312 | tf_op jit(solution)/shard_map/ppermute | solution.py:265

commit v3 on v2

--- a/solution.py
+++ b/solution.py
@@ -21,13 +21,16 @@
 MIB = 1024 * 1024
 
 
-def position_tables(segment_row):
+def frequencies():
+    return rope_theta ** (-(2.0 * jnp.arange(HALF, dtype=jnp.float32)) / HD)
+
+
+def position_tables(segment_row, freqs):
     row_length = segment_row.shape[0]
     indices = jnp.arange(row_length, dtype=jnp.int32)
     same = segment_row[None, :] == segment_row[:, None]
     first_index = jnp.min(jnp.where(same, indices[None, :], row_length), axis=1)
     positions = (indices - first_index).astype(jnp.float32)
-    freqs = rope_theta ** (-(2.0 * jnp.arange(HALF, dtype=jnp.float32)) / HD)
     angles = positions[:, None] * freqs[None, :]
     cosine, sine = jnp.cos(angles), jnp.sin(angles)
     allowed = (indices[None, :] <= indices[:, None]) & same
@@ -46,7 +49,7 @@
 STEP = 4
 
 
-def for_chunks(buffers, layout, body, carry):
+def for_chunks(buffers, layout, body, carry, unrolled=False):
     px, py = lax.axis_index("x0"), lax.axis_index("y0")
     for ref, (turn_x, turn_y, first) in zip(buffers, layout, strict=True):
         base = SIDE * jnp.where(turn_x == 1, 1 - px, px) + jnp.where(turn_y == 1, 1 - py, py)
@@ -57,7 +60,11 @@
             return body([(ref[i * STEP + k], place + 2 * k) for k in range(STEP)], carry)
 
         count = ref.shape[0] // STEP
-        carry = chunk(0, carry) if count == 1 else lax.fori_loop(0, count, chunk, carry)
+        if unrolled:
+            for i in range(count):
+                carry = chunk(i, carry)
+        else:
+            carry = lax.fori_loop(0, count, chunk, carry)
     return carry
 
 
@@ -76,60 +83,53 @@
     return jnp.concatenate(parts, axis=0)
 
 
-def project_kernel(
-    section, layout, first, last, gain_own, gain_other, own, other, kv_own, kv_other, *rest
-):
-    before = () if first else rest[:3]
-    rest = rest[len(before) :]
-    tables = rest[:2] if last else ()
-    rest = rest[len(tables) :]
-    buffers, outs = rest[: len(layout)], rest[len(layout) :]
+def squares_of(buffers, total):
+    for ref in buffers:
+        for j in range(ref.shape[0]):
+            part = ref[j].astype(jnp.float32)
+            total += part * part
+    return total
+
+
+def squares_kernel(*refs):
+    buffers, total = refs[:-1], refs[-1]
+    total[...] = squares_of(buffers, jnp.zeros(total.shape, jnp.float32))
+
+
+def project_kernel(section, layout, late, squares, *rest):
+    gain_own, gain_other, own, other, kv_own, kv_other, cosine, sine = rest[:8]
+    buffers, (query, keyval) = rest[8:-2], rest[-2:]
     second = is_other(section)
-    rows, width = buffers[0].shape[1:]
+    rows, width = query.shape
     columns = kv_own.shape[0]
+    features = width * gain_own.shape[0]
+    total = squares_of(buffers[-late:], squares[...])
+    scale = lax.rsqrt(jnp.sum(total, axis=1, keepdims=True) / features + norm_epsilon)
 
     def body(chunk, carry):
-        q_sum, kv_sum, squares = carry
-        scaled, kv_parts = [], []
+        q_sum, kv_sum = carry
+        normed, kv_parts = [], []
         for part, place in chunk:
             gain = jnp.where(second, gain_other[place], gain_own[place])
-            wide = part.astype(jnp.float32)
-            squares += wide * wide
-            scaled.append((wide * gain).astype(jnp.bfloat16))
+            normed.append((part.astype(jnp.float32) * scale * gain).astype(jnp.bfloat16))
             span = at(place, width)
             kv_parts.append(jnp.where(second, kv_other[:, span], kv_own[:, span]))
-        scaled = jnp.concatenate(scaled, axis=1)
+        normed = jnp.concatenate(normed, axis=1)
         weight = weight_rows(second, own, other, chunk, width)
-        q_sum += jnp.dot(scaled, weight, preferred_element_type=jnp.float32)
+        q_sum += jnp.dot(normed, weight, preferred_element_type=jnp.float32)
         kv_sum += lax.dot_general(
+            normed,
             jnp.concatenate(kv_parts, axis=1),
-            scaled,
             (((1,), (1,)), ((), ())),
             preferred_element_type=jnp.float32,
         )
-        return q_sum, kv_sum, squares
-
-    if first:
-        carry = tuple(
-            jnp.zeros(shape, jnp.float32) for shape in ((rows, width), (columns, rows), (rows, width))
-        )
-    else:
-        carry = tuple(ref[...] for ref in before)
-    carry = for_chunks(buffers, layout, body, carry)
-    if not last:
-        for out, value in zip(outs, carry, strict=True):
-            out[...] = value
-        return
-    q_sum, kv_sum, squares = carry
-    cosine, sine = tables
-    query, keyval = outs
-    features = width * gain_own.shape[0]
-    scale = lax.rsqrt(jnp.sum(squares, axis=1, keepdims=True) / features + norm_epsilon)
-    q_sum *= scale
+        return q_sum, kv_sum
+
+    zero = jnp.zeros((rows, width), jnp.float32), jnp.zeros((rows, columns), jnp.float32)
+    q_sum, kv_sum = for_chunks(buffers, layout, body, zero, unrolled=True)
     turned = jnp.concatenate([q_sum[:, HALF:], q_sum[:, :HALF]], axis=1)
     query[...] = (q_sum * cosine[...] + turned * sine[...]).astype(query.dtype)
-    across = jnp.broadcast_to(scale, (rows, width)).T[:columns, :]
-    flat = (kv_sum * across).astype(keyval.dtype)
+    flat = kv_sum.T.astype(keyval.dtype)
     keyval[...] = jnp.broadcast_to(flat[None], keyval.shape)
 
 
@@ -171,6 +171,14 @@
         outs[1][...] = jnp.broadcast_to(out[None], outs[1].shape)
 
 
+def start_kernel(inputs, segments, current, copies, segment_row):
+    me = lax.axis_index("section")
+    block = inputs[me]
+    current[...] = block
+    copies[...] = jnp.broadcast_to(block[None], copies.shape)
+    segment_row[...] = jnp.where(me == 0, segments[0:1, :], segments[1:2, :])
+
+
 def place_kernel(mine, theirs, result):
     me = lax.axis_index("section")
     result[me] = mine[...]
@@ -213,40 +221,35 @@
     _, rows, width = inputs.shape
     sections = lax.axis_size("section")
     ring = lax.axis_size(Y)
-    me = lax.axis_index("section")
     swap = [(0, 1), (1, 0)]
     own = [w_query[0, 0], w_keyval[0, 0].T, w_output[0, 0]]
     gain = gains[0].astype(jnp.float32).reshape(-1, 1, width)
-    current = lax.dynamic_index_in_dim(inputs, me, 0, keepdims=False)
-    segment_row = lax.dynamic_index_in_dim(segments, me, 0, keepdims=False)
-    cosine, sine, allowed = position_tables(segment_row)
-    copies = jnp.broadcast_to(current[None], (FAR_COUNT, rows, width))
-    copies, cosine, sine, allowed, gain = lax.optimization_barrier(
-        (copies, cosine, sine, allowed, gain)
-    )
+    other = []
+    for w in own:
+        other.append(lax.ppermute(w, "section", swap))
+    other_gain = lax.ppermute(gain, "section", swap)
     shape = jax.ShapeDtypeStruct
     bf16 = functools.partial(shape, dtype=jnp.bfloat16)
     f32 = functools.partial(shape, dtype=jnp.float32)
     columns = own[1].shape[0]
+    outs = (bf16((rows, width)), bf16((FAR_COUNT, rows, width)), shape((1, rows), jnp.int32))
+    current, copies, segment_row = call(start_kernel, outs, 4, inputs, segments)
+    copies, segment_row, freqs = lax.optimization_barrier((copies, segment_row, frequencies()))
     stages = len(STAGES)
     for s in range(sections):
         far = far_stage(copies)
         if s == 0:
-            far, gain, *own = lax.optimization_barrier((far, gain, *own))
-            other_gain = lax.ppermute(gain, "section", swap)
-            other = [lax.ppermute(w, "section", swap) for w in own]
+            far, segment_row = lax.optimization_barrier((far, segment_row))
+            cosine, sine, allowed = position_tables(segment_row[0], freqs)
         near = near_stage(far)
-        sums = ()
-        for k, (group, layout) in enumerate(zip(near, STAGES, strict=True)):
-            last = k == stages - 1
-            outs = (f32((rows, width)), f32((columns, rows)), f32((rows, width)))
-            if last:
-                outs = (bf16((rows, width)), bf16((ring, columns, rows)))
-            kernel = functools.partial(project_kernel, s, layout, k == 0, last)
-            tables = (cosine, sine) if last else ()
-            weights = (gain, other_gain, own[0], other[0], own[1], other[1])
-            sums = call(kernel, outs, 10, *weights, *sums, *tables, *group)
-        query, keyval = sums
+        squares = call(squares_kernel, f32((rows, width)), 4, *near[0], *near[1])
+        squares, cosine, sine, allowed = lax.optimization_barrier(
+            (squares, cosine, sine, allowed)
+        )
+        weights = (gain, other_gain, own[0], other[0], own[1], other[1])
+        kernel = functools.partial(project_kernel, s, sum(STAGES, ()), len(STAGES[-1]))
+        outs = (bf16((rows, width)), bf16((ring, columns, rows)))
+        query, keyval = call(kernel, outs, 10, squares, *weights, cosine, sine, *sum(near, ()))
         keyval = lax.all_to_all(keyval, Y, 0, 0, tiled=True).reshape(-1, rows)
         attended = call(
             attend_kernel, bf16((FAR_COUNT, rows, width)), 4, query, keyval, cosine, sine, allowed
@@ -280,6 +283,7 @@
         P("section", None, None, MESH),
     )
     out_specs = P("section", "groups", None, MESH)
+
     return jax.shard_map(
         shards, mesh=finer, in_specs=in_specs, out_specs=out_specs, check_vma=False
     )

time: 215 us -> 216 us (level)
  blocking collectives: 121 us -> 79.7 us
  starting transfers between devices: 40.9 us -> 68.5 us
  waiting for transfers between devices: 33.2 us -> 44.3 us
    all_to_all x4 -> x3, blocking collectives: 100 us -> 57.3 us  [far_stage(): return lax.all_to_all(copies, FAR, 0, 0, tiled=True)]
    all_to_all x0 -> x1, starting transfers between devices: none -> 17 us  [far_stage(): return lax.all_to_all(copies, FAR, 0, 0, tiled=True)]
    all_to_all x0 -> x1, waiting for transfers between devices: none -> 13.3 us  [far_stage(): return lax.all_to_all(copies, FAR, 0, 0, tiled=True)]
    ppermute x24, starting transfers between devices: 28.9 us -> 42.2 us  [from_neighbour(): return lax.ppermute(block, MESH, pairs)]
    ppermute x1, starting transfers between devices: 7.75 us -> 4.02 us  [shards(): theirs = lax.ppermute(copies, 'section', swap)]
    unnamed x8 -> x12, local copies, waits for them, and re-layouts: 0.02 us -> 2.72 us
    pallas_call x15 -> x14, Pallas kernels: 15.1 us -> 15.4 us  [call(): pl.pallas_call(kernel, out_shape=outs, in_specs=[vmem] * len(args), out_s...]
  transfers between devices with their start and end apart: 29 -> 30, of which waited for: 16 -> 17; matrix products, arithmetic and copies ran while one was open for 0% -> 1% of each run, Pallas kernels for 5% -> 4%
where the time goes in v3:
time: 216 us; the launch traced here: 212 us
  blocking collectives  79.7 us (37%)
  starting transfers between devices  68.5 us (32%)
  waiting for transfers between devices  44.3 us (21%)
  Pallas kernels  15.4 us (7%)
  local copies, waits for them, and re-layouts  2.86 us (1%)
    all_to_all x3, blocking collectives, far_stage(): return lax.all_to_all(copies, FAR, 0, 0, tiled=True)  57.3 us
    ppermute x24, starting transfers between devices, from_neighbour(): return lax.ppermute(block, MESH, pairs)  42.2 us
    ppermute x24, waiting for transfers between devices, from_neighbour(): return lax.ppermute(block, MESH, pairs)  30.1 us
    all_to_all x2, blocking collectives, shards(): keyval = lax.all_to_all(keyval, Y, 0, 0, tiled=True).reshape(-1, rows)  22.3 us
    all_to_all x1, starting transfers between devices, far_stage(): return lax.all_to_all(copies, FAR, 0, 0, tiled=True)  17 us
    pallas_call x14, Pallas kernels, call(): pl.pallas_call(kernel, out_shape=outs, in_specs=[vmem] * len(args), out_s...  15.4 us
    all_to_all x1, waiting for transfers between devices, far_stage(): return lax.all_to_all(copies, FAR, 0, 0, tiled=True)  13.3 us
    ppermute x3, starting transfers between devices, shards(): other.append(lax.ppermute(w, 'section', swap))  5.15 us
  transfers between devices with their start and end apart: 30, of which 17 were waited for; matrix products, arithmetic and copies ran while one was open for 1% of the time, Pallas kernels for 4%

profile of v3, /device:TPU:647, one launch (start us, length us, event | category | flops | bytes accessed | tf_op | source)
XLA Modules:
  0.0 212.4 jit_solution(16201065390924360426)
XLA Ops:
  0.0 1.0 copy-done.4
  1.0 0.7 copy-done.5
  1.7 0.9 shard_map.64
  2.6 17.0 %all-to-all-start = ((bf16[16,128,128]{2,1,0:T(8,128)(2,1)}), bf16[16,128,128]{2,1,0:T(8,128)(2,1)S(1)}, u32[]{:S(2)}, u32[]{:S(2)}) async-start(bf16[16,128,128]{2,1,0:T(8,128)(2,1)} %get-tuple-element.32), calls=%async_computation | async-start | bytes 1048576 | tf_op jit(solution)/shard_map/all_to_all | solution.py:209
  19.6 1.2 collective-permute-start.6
  20.8 0.8 bitcast_convert_fusion.rest_0_
  21.7 13.3 %all-to-all-done.refs_0_.rest_8_ = bf16[16,128,128]{2,1,0:T(8,128)(2,1)S(1)} async-done(((bf16[16,128,128]{2,1,0:T(8,128)(2,1)}), bf16[16,128,128]{2,1,0:T(8,128)(2,1)S(1)}, u32[]{:S(2)}, u32[]{:S(2)}) %all-to-all-start) | async-done | bytes 524320 | tf_op jit(solution)/shard_map/all_to_all | solution.py:209
  35.0 1.5 collective-permute-start.4
  36.6 4.1 %collective-permute-start.2 = (bf16[8,128,128]{2,1,0:T(8,128)(2,1)S(1)}, bf16[8,128,128]{2,1,0:T(8,128)(2,1)S(1)}, u32[]{:S(2)}, u32[]{:S(2)}) collective-permute-start(bf16[8,128,128]{2,1,0:T(8,128)(2,1)S(1)} %get-tuple-element.59), channel_id=1, source_target_pairs={{56,0},{57,1},{58,2},{59,3},{60,4},{61,5},{62,6},{63,7},{0,8},{1,9... | collective-permute-start | bytes 786440 | tf_op jit(solution)/shard_map/ppermute | solution.py:205
  40.7 0.2 fusion
  40.9 1.8 collective-permute-start.3
  42.7 1.0 collective-permute-done.4.refs_4_.rest_12_
  43.7 2.0 collective-permute-start.7
  45.7 0.3 fusion.2
  46.1 2.0 collective-permute-start
  48.1 0.4 collective-permute-start.9
  48.4 1.2 collective-permute-done.1.refs_1_.rest_9_
  49.6 1.1 collective-permute-start.8
  50.9 0.2 shard_map.65.squares
  51.1 3.3 %collective-permute-done.9.rest_14_ = bf16[8,128,128]{2,1,0:T(8,128)(2,1)S(1)} collective-permute-done((bf16[8,128,128]{2,1,0:T(8,128)(2,1)S(1)}, bf16[8,128,128]{2,1,0:T(8,128)(2,1)S(1)}, u32[]{:S(2)}, u32[]{:S(2)}) %collective-permute-start.9) | collective-permute-done | bytes 262176 | tf_op jit(solution)/shard_map/ppermute | solution.py:205
  54.5 0.7 collective-permute-done.8.rest_13_
  55.2 1.0 copy-done.2
  56.2 3.1 %shard_map.66 = (bf16[128,128]{1,0:T(8,128)(2,1)S(1)}, bf16[8,32,128]{2,1,0:T(8,128)(2,1)S(1)}) custom-call(f32[128,128]{1,0:T(8,128)S(1)} %shard_map.65.squares, f32[64,1,128]{2,1,0:T(1,128)S(1)} %bitcast_convert_fusion.rest_0_, f32[64,1,128]{2,1,0:T(1,128)S(1)} %collective-permute-done.5.rest_1_, bf16[8192,128]{1,0:T(8,128)(2,1)S(1)} %bitcast.20, ...), custom_call_target="tpu_custom_call" | custom-call | tf_op jit(solution)/shard_map/pallas_call | solution.py:190
  59.3 11.7 %all_to_all.30 = bf16[8,32,128]{2,1,0:T(8,128)(2,1)S(1)} all-to-all(bf16[8,32,128]{2,1,0:T(8,128)(2,1)S(1)} %get-tuple-element.41), channel_id=1, replica_groups=mesh['groups'=2,'section'=2,'x2'=2,'x1'=2,'x0'=2,'y2'=2,'y1'=2,'y0'=2] {..., dimensions={0} | all-to-all | bytes 131072 | tf_op jit(solution)/shard_map/all_to_all | solution.py:253
  71.0 0.5 shard_map.67
  71.5 16.9 %all_to_all.31.rest_0_ = bf16[16,128,128]{2,1,0:T(8,128)(2,1)S(1)} all-to-all(bf16[16,128,128]{2,1,0:T(8,128)(2,1)S(1)} %shard_map.67), channel_id=1, replica_groups=mesh['groups'=2,'section'=2,'x2'=2,'x1'=2,'x0'=2,'y2'=2,'y1'=2,'y0'=2] {..., dimensions={0} | all-to-all | bytes 1048576 | tf_op jit(solution)/shard_map/all_to_all | solution.py:209
  88.5 8.1 %collective-permute-start.11 = (bf16[8,128,128]{2,1,0:T(8,128)(2,1)S(1)}, bf16[8,128,128]{2,1,0:T(8,128)(2,1)S(1)}, u32[]{:S(2)}, u32[]{:S(2)}) collective-permute-start(bf16[8,128,128]{2,1,0:T(8,128)(2,1)S(1)} %get-tuple-element.57), channel_id=1, source_target_pairs={{56,0},{57,1},{58,2},{59,3},{60,4},{61,5},{62,6},{63,7},{0,8},{1,9... | collective-permute-start | bytes 786440 | tf_op jit(solution)/shard_map/ppermute | solution.py:205
  96.6 1.1 collective-permute-start.13
  97.7 1.6 collective-permute-start.12
  99.3 0.6 collective-permute-done.11.rest_1_
  99.9 1.1 collective-permute-start.15
  101.0 2.0 collective-permute-done.10.rest_0_
  103.0 0.3 collective-permute-start.14
  103.4 0.8 shard_map.68.before
  104.2 1.5 shard_map.69.before
  105.7 2.5 %collective-permute-done.15.rest_1_ = bf16[8,128,128]{2,1,0:T(8,128)(2,1)S(1)} collective-permute-done((bf16[8,128,128]{2,1,0:T(8,128)(2,1)S(1)}, bf16[8,128,128]{2,1,0:T(8,128)(2,1)S(1)}, u32[]{:S(2)}, u32[]{:S(2)}) %collective-permute-start.15) | collective-permute-done | bytes 262176 | tf_op jit(solution)/shard_map/ppermute | solution.py:205
  108.2 2.1 collective-permute-done.14.rest_0_
  110.2 0.8 shard_map.70
  111.1 21.1 %all_to_all.32.refs_0_.rest_8_ = bf16[16,128,128]{2,1,0:T(8,128)(2,1)S(1)} all-to-all(bf16[16,128,128]{2,1,0:T(8,128)(2,1)S(1)} %get-tuple-element.44), channel_id=1, replica_groups=mesh['groups'=2,'section'=2,'x2'=2,'x1'=2,'x0'=2,'y2'=2,'y1'=2,'y0'=2] {..., dimensions={0} | all-to-all | bytes 1048576 | tf_op jit(solution)/shard_map/all_to_all | solution.py:209
  132.2 7.0 %collective-permute-start.17 = (bf16[8,128,128]{2,1,0:T(8,128)(2,1)S(1)}, bf16[8,128,128]{2,1,0:T(8,128)(2,1)S(1)}, u32[]{:S(2)}, u32[]{:S(2)}) collective-permute-start(bf16[8,128,128]{2,1,0:T(8,128)(2,1)S(1)} %get-tuple-element.55), channel_id=1, source_target_pairs={{56,0},{57,1},{58,2},{59,3},{60,4},{61,5},{62,6},{63,7},{0,8},{1,9... | collective-permute-start | bytes 786440 | tf_op jit(solution)/shard_map/ppermute | solution.py:205
  139.2 0.8 collective-permute-start.16
  140.1 2.6 %collective-permute-start.18 = (bf16[8,128,128]{2,1,0:T(8,128)(2,1)S(1)}, bf16[8,128,128]{2,1,0:T(8,128)(2,1)S(1)}, u32[]{:S(2)}, u32[]{:S(2)}) collective-permute-start(bf16[8,128,128]{2,1,0:T(8,128)(2,1)S(1)} %get-tuple-element.56), channel_id=1, source_target_pairs={{1,0},{2,1},{3,2},{4,3},{5,4},{6,5},{7,6},{0,7},{9,8},{10,9},{11,1... | collective-permute-start | bytes 786440 | tf_op jit(solution)/shard_map/ppermute | solution.py:205
  142.7 3.1 %collective-permute-done.17.refs_2_.rest_10_ = bf16[8,128,128]{2,1,0:T(8,128)(2,1)S(1)} collective-permute-done((bf16[8,128,128]{2,1,0:T(8,128)(2,1)S(1)}, bf16[8,128,128]{2,1,0:T(8,128)(2,1)S(1)}, u32[]{:S(2)}, u32[]{:S(2)}) %collective-permute-start.17) | collective-permute-done | bytes 262176 | tf_op jit(solution)/shard_map/ppermute | solution.py:205
  145.9 2.6 %collective-permute-start.20 = (bf16[8,128,128]{2,1,0:T(8,128)(2,1)S(1)}, bf16[8,128,128]{2,1,0:T(8,128)(2,1)S(1)}, u32[]{:S(2)}, u32[]{:S(2)}) collective-permute-start(bf16[8,128,128]{2,1,0:T(8,128)(2,1)S(1)} %collective-permute-done.16.refs_1_.rest_9_), channel_id=1, source_target_pairs={{1,0},{2,1},{3,2},{4,3},{5,4},{6,5},{7,6},{0,7},{9,8},{10,9},{11,1... | collective-permute-start | bytes 786440 | tf_op jit(solution)/shard_map/ppermute | solution.py:205
  148.4 0.2 shard_map.71.squares
  148.6 4.8 %collective-permute-done.21.rest_14_ = bf16[8,128,128]{2,1,0:T(8,128)(2,1)S(1)} collective-permute-done((bf16[8,128,128]{2,1,0:T(8,128)(2,1)S(1)}, bf16[8,128,128]{2,1,0:T(8,128)(2,1)S(1)}, u32[]{:S(2)}, u32[]{:S(2)}) %collective-permute-start.21) | collective-permute-done | bytes 262176 | tf_op jit(solution)/shard_map/ppermute | solution.py:205
  153.4 3.1 %shard_map.72 = (bf16[128,128]{1,0:T(8,128)(2,1)S(1)}, bf16[8,32,128]{2,1,0:T(8,128)(2,1)S(1)}) custom-call(f32[128,128]{1,0:T(8,128)S(1)} %shard_map.71.squares, f32[64,1,128]{2,1,0:T(1,128)S(1)} %bitcast_convert_fusion.rest_0_, f32[64,1,128]{2,1,0:T(1,128)S(1)} %collective-permute-done.5.rest_1_, bf16[8192,128]{1,0:T(8,128)(2,1)S(1)} %bitcast.21, ...), custom_call_target="tpu_custom_call" | custom-call | tf_op jit(solution)/shard_map/pallas_call | solution.py:190
  156.5 10.7 %all_to_all.33 = bf16[8,32,128]{2,1,0:T(8,128)(2,1)S(1)} all-to-all(bf16[8,32,128]{2,1,0:T(8,128)(2,1)S(1)} %get-tuple-element.49), channel_id=1, replica_groups=mesh['groups'=2,'section'=2,'x2'=2,'x1'=2,'x0'=2,'y2'=2,'y1'=2,'y0'=2] {..., dimensions={0} | all-to-all | bytes 131072 | tf_op jit(solution)/shard_map/all_to_all | solution.py:253
  167.2 0.5 shard_map.73
  167.8 19.4 %all_to_all.34.rest_0_ = bf16[16,128,128]{2,1,0:T(8,128)(2,1)S(1)} all-to-all(bf16[16,128,128]{2,1,0:T(8,128)(2,1)S(1)} %shard_map.73), channel_id=1, replica_groups=mesh['groups'=2,'section'=2,'x2'=2,'x1'=2,'x0'=2,'y2'=2,'y1'=2,'y0'=2] {..., dimensions={0} | all-to-all | bytes 1048576 | tf_op jit(solution)/shard_map/all_to_all | solution.py:209
  187.2 4.7 %collective-permute-start.23 = (bf16[8,128,128]{2,1,0:T(8,128)(2,1)S(1)}, bf16[8,128,128]{2,1,0:T(8,128)(2,1)S(1)}, u32[]{:S(2)}, u32[]{:S(2)}) collective-permute-start(bf16[8,128,128]{2,1,0:T(8,128)(2,1)S(1)} %get-tuple-element.53), channel_id=1, source_target_pairs={{56,0},{57,1},{58,2},{59,3},{60,4},{61,5},{62,6},{63,7},{0,8},{1,9... | collective-permute-start | bytes 786440 | tf_op jit(solution)/shard_map/ppermute | solution.py:205
  191.8 0.4 collective-permute-start.25
  192.3 2.2 %collective-permute-start.24 = (bf16[8,128,128]{2,1,0:T(8,128)(2,1)S(1)}, bf16[8,128,128]{2,1,0:T(8,128)(2,1)S(1)}, u32[]{:S(2)}, u32[]{:S(2)}) collective-permute-start(bf16[8,128,128]{2,1,0:T(8,128)(2,1)S(1)} %get-tuple-element.54), channel_id=1, source_target_pairs={{1,0},{2,1},{3,2},{4,3},{5,4},{6,5},{7,6},{0,7},{9,8},{10,9},{11,1... | collective-permute-start | bytes 786440 | tf_op jit(solution)/shard_map/ppermute | solution.py:205
  194.5 0.6 collective-permute-done.23.rest_1_
  195.2 0.4 collective-permute-start.27
  195.6 2.7 %collective-permute-done.22.rest_0_ = bf16[8,128,128]{2,1,0:T(8,128)(2,1)S(1)} collective-permute-done((bf16[8,128,128]{2,1,0:T(8,128)(2,1)S(1)}, bf16[8,128,128]{2,1,0:T(8,128)(2,1)S(1)}, u32[]{:S(2)}, u32[]{:S(2)}) %collective-permute-start.22) | collective-permute-done | bytes 262176 | tf_op jit(solution)/shard_map/ppermute | solution.py:205
  198.3 0.8 shard_map.74.before
  199.1 1.5 shard_map.75.before
  200.6 2.8 %collective-permute-done.27.rest_2_ = bf16[8,128,128]{2,1,0:T(8,128)(2,1)S(1)} collective-permute-done((bf16[8,128,128]{2,1,0:T(8,128)(2,1)S(1)}, bf16[8,128,128]{2,1,0:T(8,128)(2,1)S(1)}, u32[]{:S(2)}, u32[]{:S(2)}) %collective-permute-start.27) | collective-permute-done | bytes 262176 | tf_op jit(solution)/shard_map/ppermute | solution.py:205
  203.4 2.7 %collective-permute-done.26.rest_1_ = bf16[8,128,128]{2,1,0:T(8,128)(2,1)S(1)} collective-permute-done((bf16[8,128,128]{2,1,0:T(8,128)(2,1)S(1)}, bf16[8,128,128]{2,1,0:T(8,128)(2,1)S(1)}, u32[]{:S(2)}, u32[]{:S(2)}) %collective-permute-start.26) | collective-permute-done | bytes 262176 | tf_op jit(solution)/shard_map/ppermute | solution.py:205
  206.1 0.8 shard_map.76
  206.8 4.0 %collective-permute-start.28 = (bf16[128,128]{1,0:T(8,128)(2,1)S(1)}, bf16[128,128]{1,0:T(8,128)(2,1)S(1)}, u32[]{:S(2)}, u32[]{:S(2)}) collective-permute-start(bf16[128,128]{1,0:T(8,128)(2,1)S(1)} %get-tuple-element.52), channel_id=1, source_target_pairs={{0,64},{64,0},{1,65},{65,1},{2,66},{66,2},{3,67},{67,3},{4,68},{68... | collective-permute-start | bytes 98312 | tf_op jit(solution)/shard_map/ppermute | solution.py:268
  210.9 0.9 collective-permute-done.28.theirs
  211.7 0.6 shard_map.77
  (38 shorter events, 0.9 us)
Async XLA Ops:
  0.0 46.1 %copy-start = (bf16[1,1,8192,128]{3,2,1,0:T(8,128)(2,1)S(1)}, bf16[1,1,8192,128]{3,2,1,0:T(8,128)(2,1)}, u32[]{:S(2)}) copy-start(bf16[1,1,8192,128]{3,2,1,0:T(8,128)(2,1)} %param.11) | copy-start | bytes 6291460
  0.0 1.0 copy-start.4
  1.0 0.7 copy-start.5
  2.6 32.4 %all-to-all-start = ((bf16[16,128,128]{2,1,0:T(8,128)(2,1)}), bf16[16,128,128]{2,1,0:T(8,128)(2,1)S(1)}, u32[]{:S(2)}, u32[]{:S(2)}) async-start(bf16[16,128,128]{2,1,0:T(8,128)(2,1)} %get-tuple-element.32), calls=%async_computation | async-start | bytes 1048576 | tf_op jit(solution)/shard_map/all_to_all | solution.py:209
  19.6 35.6 %collective-permute-start.6 = (bf16[8192,128]{1,0:T(8,128)(2,1)}, bf16[8192,128]{1,0:T(8,128)(2,1)}, u32[]{:S(2)}, u32[]{:S(2)}) collective-permute-start(bf16[8192,128]{1,0:T(8,128)(2,1)} %bitcast.19), channel_id=1, source_target_pairs={{0,64},{64,0},{1,65},{65,1},{2,66},{66,2},{3,67},{67,3},{4,68},{68... | collective-permute-start | bytes 6291464 | tf_op jit(solution)/shard_map/ppermute | solution.py:229
  21.6 21.1 %collective-permute-start.5 = (f32[64,1,128]{2,1,0:T(1,128)S(1)}, f32[64,1,128]{2,1,0:T(1,128)S(1)}, u32[]{:S(2)}, u32[]{:S(2)}) collective-permute-start(f32[64,1,128]{2,1,0:T(1,128)S(1)} %bitcast_convert_fusion.rest_0_), channel_id=1, source_target_pairs={{0,64},{64,0},{1,65},{65,1},{2,66},{66,2},{3,67},{67,3},{4,68},{68... | collective-permute-start | bytes 98312 | tf_op jit(solution)/shard_map/ppermute | solution.py:230
  35.0 20.2 %copy-start.1 = (bf16[1,1,8192,128]{3,2,1,0:T(8,128)(2,1)S(1)}, bf16[1,1,8192,128]{3,2,1,0:T(8,128)(2,1)}, u32[]{:S(2)}) copy-start(bf16[1,1,8192,128]{3,2,1,0:T(8,128)(2,1)} %param.9) | copy-start | bytes 6291460
  35.0 8.7 %collective-permute-start.4 = (bf16[8,128,128]{2,1,0:T(8,128)(2,1)S(1)}, bf16[8,128,128]{2,1,0:T(8,128)(2,1)S(1)}, u32[]{:S(2)}, u32[]{:S(2)}) collective-permute-start(bf16[8,128,128]{2,1,0:T(8,128)(2,1)S(1)} %get-tuple-element.59), channel_id=1, source_target_pairs={{7,0},{0,1},{1,2},{2,3},{3,4},{4,5},{5,6},{6,7},{15,8},{8,9},{9,10... | collective-permute-start | bytes 786440 | tf_op jit(solution)/shard_map/ppermute | solution.py:205
  36.6 9.5 %collective-permute-start.2 = (bf16[8,128,128]{2,1,0:T(8,128)(2,1)S(1)}, bf16[8,128,128]{2,1,0:T(8,128)(2,1)S(1)}, u32[]{:S(2)}, u32[]{:S(2)}) collective-permute-start(bf16[8,128,128]{2,1,0:T(8,128)(2,1)S(1)} %get-tuple-element.59), channel_id=1, source_target_pairs={{56,0},{57,1},{58,2},{59,3},{60,4},{61,5},{62,6},{63,7},{0,8},{1,9... | collective-permute-start | bytes 786440 | tf_op jit(solution)/shard_map/ppermute | solution.py:205
  40.9 7.1 %collective-permute-start.3 = (bf16[8,128,128]{2,1,0:T(8,128)(2,1)S(1)}, bf16[8,128,128]{2,1,0:T(8,128)(2,1)S(1)}, u32[]{:S(2)}, u32[]{:S(2)}) collective-permute-start(bf16[8,128,128]{2,1,0:T(8,128)(2,1)S(1)} %get-tuple-element.60), channel_id=1, source_target_pairs={{1,0},{2,1},{3,2},{4,3},{5,4},{6,5},{7,6},{0,7},{9,8},{10,9},{11,1... | collective-permute-start | bytes 786440 | tf_op jit(solution)/shard_map/ppermute | solution.py:205
  42.7 6.9 %collective-permute-start.1 = (bf16[8,128,128]{2,1,0:T(8,128)(2,1)S(1)}, bf16[8,128,128]{2,1,0:T(8,128)(2,1)S(1)}, u32[]{:S(2)}, u32[]{:S(2)}) collective-permute-start(bf16[8,128,128]{2,1,0:T(8,128)(2,1)S(1)} %get-tuple-element.60), channel_id=1, source_target_pairs={{8,0},{9,1},{10,2},{11,3},{12,4},{13,5},{14,6},{15,7},{16,8},{17,9... | collective-permute-start | bytes 786440 | tf_op jit(solution)/shard_map/ppermute | solution.py:205
  43.7 7.4 %collective-permute-start.7 = (bf16[32,8192]{1,0:T(8,128)(2,1)}, bf16[32,8192]{1,0:T(8,128)(2,1)S(1)}, u32[]{:S(2)}, u32[]{:S(2)}) collective-permute-start(bf16[32,8192]{1,0:T(8,128)(2,1)} %bitcast.22), channel_id=1, source_target_pairs={{0,64},{64,0},{1,65},{65,1},{2,66},{66,2},{3,67},{67,3},{4,68},{68... | collective-permute-start | bytes 1572872 | tf_op jit(solution)/shard_map/ppermute | solution.py:229
  46.1 57.3 %collective-permute-start = (bf16[8192,128]{1,0:T(8,128)(2,1)S(1)}, bf16[8192,128]{1,0:T(8,128)(2,1)S(1)}, u32[]{:S(2)}, u32[]{:S(2)}) collective-permute-start(bf16[8192,128]{1,0:T(8,128)(2,1)S(1)} %bitcast.12), channel_id=1, source_target_pairs={{0,64},{64,0},{1,65},{65,1},{2,66},{66,2},{3,67},{67,3},{4,68},{68... | collective-permute-start | bytes 6291464 | tf_op jit(solution)/shard_map/ppermute | solution.py:229
  48.1 6.4 %collective-permute-start.9 = (bf16[8,128,128]{2,1,0:T(8,128)(2,1)S(1)}, bf16[8,128,128]{2,1,0:T(8,128)(2,1)S(1)}, u32[]{:S(2)}, u32[]{:S(2)}) collective-permute-start(bf16[8,128,128]{2,1,0:T(8,128)(2,1)S(1)} %collective-permute-done.2.refs_2_.rest_10_), channel_id=1, source_target_pairs={{7,0},{0,1},{1,2},{2,3},{3,4},{4,5},{5,6},{6,7},{15,8},{8,9},{9,10... | collective-permute-start | bytes 786440 | tf_op jit(solution)/shard_map/ppermute | solution.py:205
  49.6 5.5 %collective-permute-start.8 = (bf16[8,128,128]{2,1,0:T(8,128)(2,1)S(1)}, bf16[8,128,128]{2,1,0:T(8,128)(2,1)S(1)}, u32[]{:S(2)}, u32[]{:S(2)}) collective-permute-start(bf16[8,128,128]{2,1,0:T(8,128)(2,1)S(1)} %collective-permute-done.1.refs_1_.rest_9_), channel_id=1, source_target_pairs={{1,0},{2,1},{3,2},{4,3},{5,4},{6,5},{7,6},{0,7},{9,8},{10,9},{11,1... | collective-permute-start | bytes 786440 | tf_op jit(solution)/shard_map/ppermute | solution.py:205
  55.2 1.0 copy-start.2
  88.5 11.4 %collective-permute-start.11 = (bf16[8,128,128]{2,1,0:T(8,128)(2,1)S(1)}, bf16[8,128,128]{2,1,0:T(8,128)(2,1)S(1)}, u32[]{:S(2)}, u32[]{:S(2)}) collective-permute-start(bf16[8,128,128]{2,1,0:T(8,128)(2,1)S(1)} %get-tuple-element.57), channel_id=1, source_target_pairs={{56,0},{57,1},{58,2},{59,3},{60,4},{61,5},{62,6},{63,7},{0,8},{1,9... | collective-permute-start | bytes 786440 | tf_op jit(solution)/shard_map/ppermute | solution.py:205
  96.6 6.4 %collective-permute-start.10 = (bf16[8,128,128]{2,1,0:T(8,128)(2,1)S(1)}, bf16[8,128,128]{2,1,0:T(8,128)(2,1)S(1)}, u32[]{:S(2)}, u32[]{:S(2)}) collective-permute-start(bf16[8,128,128]{2,1,0:T(8,128)(2,1)S(1)} %get-tuple-element.58), channel_id=1, source_target_pairs={{8,0},{9,1},{10,2},{11,3},{12,4},{13,5},{14,6},{15,7},{16,8},{17,9... | collective-permute-start | bytes 786440 | tf_op jit(solution)/shard_map/ppermute | solution.py:205
  96.6 7.5 %collective-permute-start.13 = (bf16[8,128,128]{2,1,0:T(8,128)(2,1)S(1)}, bf16[8,128,128]{2,1,0:T(8,128)(2,1)S(1)}, u32[]{:S(2)}, u32[]{:S(2)}) collective-permute-start(bf16[8,128,128]{2,1,0:T(8,128)(2,1)S(1)} %get-tuple-element.57), channel_id=1, source_target_pairs={{7,0},{0,1},{1,2},{2,3},{3,4},{4,5},{5,6},{6,7},{15,8},{8,9},{9,10... | collective-permute-start | bytes 786440 | tf_op jit(solution)/shard_map/ppermute | solution.py:205
  97.7 6.5 %collective-permute-start.12 = (bf16[8,128,128]{2,1,0:T(8,128)(2,1)S(1)}, bf16[8,128,128]{2,1,0:T(8,128)(2,1)S(1)}, u32[]{:S(2)}, u32[]{:S(2)}) collective-permute-start(bf16[8,128,128]{2,1,0:T(8,128)(2,1)S(1)} %get-tuple-element.58), channel_id=1, source_target_pairs={{1,0},{2,1},{3,2},{4,3},{5,4},{6,5},{7,6},{0,7},{9,8},{10,9},{11,1... | collective-permute-start | bytes 786440 | tf_op jit(solution)/shard_map/ppermute | solution.py:205
  99.9 8.3 %collective-permute-start.15 = (bf16[8,128,128]{2,1,0:T(8,128)(2,1)S(1)}, bf16[8,128,128]{2,1,0:T(8,128)(2,1)S(1)}, u32[]{:S(2)}, u32[]{:S(2)}) collective-permute-start(bf16[8,128,128]{2,1,0:T(8,128)(2,1)S(1)} %collective-permute-done.11.rest_1_), channel_id=1, source_target_pairs={{7,0},{0,1},{1,2},{2,3},{3,4},{4,5},{5,6},{6,7},{15,8},{8,9},{9,10... | collective-permute-start | bytes 786440 | tf_op jit(solution)/shard_map/ppermute | solution.py:205
  103.0 7.2 %collective-permute-start.14 = (bf16[8,128,128]{2,1,0:T(8,128)(2,1)S(1)}, bf16[8,128,128]{2,1,0:T(8,128)(2,1)S(1)}, u32[]{:S(2)}, u32[]{:S(2)}) collective-permute-start(bf16[8,128,128]{2,1,0:T(8,128)(2,1)S(1)} %collective-permute-done.10.rest_0_), channel_id=1, source_target_pairs={{1,0},{2,1},{3,2},{4,3},{5,4},{6,5},{7,6},{0,7},{9,8},{10,9},{11,1... | collective-permute-start | bytes 786440 | tf_op jit(solution)/shard_map/ppermute | solution.py:205
  111.0 42.4 %copy-start.3 = (bf16[1,1,8192,32]{2,3,1,0:T(8,128)(2,1)S(1)}, bf16[1,1,8192,32]{2,3,1,0:T(8,128)(2,1)}, u32[]{:S(2)}) copy-start(bf16[1,1,8192,32]{2,3,1,0:T(8,128)(2,1)} %param.10) | copy-start | bytes 1572868
  132.2 13.6 %collective-permute-start.17 = (bf16[8,128,128]{2,1,0:T(8,128)(2,1)S(1)}, bf16[8,128,128]{2,1,0:T(8,128)(2,1)S(1)}, u32[]{:S(2)}, u32[]{:S(2)}) collective-permute-start(bf16[8,128,128]{2,1,0:T(8,128)(2,1)S(1)} %get-tuple-element.55), channel_id=1, source_target_pairs={{56,0},{57,1},{58,2},{59,3},{60,4},{61,5},{62,6},{63,7},{0,8},{1,9... | collective-permute-start | bytes 786440 | tf_op jit(solution)/shard_map/ppermute | solution.py:205
  139.2 6.7 %collective-permute-start.16 = (bf16[8,128,128]{2,1,0:T(8,128)(2,1)S(1)}, bf16[8,128,128]{2,1,0:T(8,128)(2,1)S(1)}, u32[]{:S(2)}, u32[]{:S(2)}) collective-permute-start(bf16[8,128,128]{2,1,0:T(8,128)(2,1)S(1)} %get-tuple-element.56), channel_id=1, source_target_pairs={{8,0},{9,1},{10,2},{11,3},{12,4},{13,5},{14,6},{15,7},{16,8},{17,9... | collective-permute-start | bytes 786440 | tf_op jit(solution)/shard_map/ppermute | solution.py:205
  140.0 8.4 %collective-permute-start.19 = (bf16[8,128,128]{2,1,0:T(8,128)(2,1)S(1)}, bf16[8,128,128]{2,1,0:T(8,128)(2,1)S(1)}, u32[]{:S(2)}, u32[]{:S(2)}) collective-permute-start(bf16[8,128,128]{2,1,0:T(8,128)(2,1)S(1)} %get-tuple-element.55), channel_id=1, source_target_pairs={{7,0},{0,1},{1,2},{2,3},{3,4},{4,5},{5,6},{6,7},{15,8},{8,9},{9,10... | collective-permute-start | bytes 786440 | tf_op jit(solution)/shard_map/ppermute | solution.py:205
  140.1 8.3 %collective-permute-start.18 = (bf16[8,128,128]{2,1,0:T(8,128)(2,1)S(1)}, bf16[8,128,128]{2,1,0:T(8,128)(2,1)S(1)}, u32[]{:S(2)}, u32[]{:S(2)}) collective-permute-start(bf16[8,128,128]{2,1,0:T(8,128)(2,1)S(1)} %get-tuple-element.56), channel_id=1, source_target_pairs={{1,0},{2,1},{3,2},{4,3},{5,4},{6,5},{7,6},{0,7},{9,8},{10,9},{11,1... | collective-permute-start | bytes 786440 | tf_op jit(solution)/shard_map/ppermute | solution.py:205
  145.7 7.7 %collective-permute-start.21 = (bf16[8,128,128]{2,1,0:T(8,128)(2,1)S(1)}, bf16[8,128,128]{2,1,0:T(8,128)(2,1)S(1)}, u32[]{:S(2)}, u32[]{:S(2)}) collective-permute-start(bf16[8,128,128]{2,1,0:T(8,128)(2,1)S(1)} %collective-permute-done.17.refs_2_.rest_10_), channel_id=1, source_target_pairs={{7,0},{0,1},{1,2},{2,3},{3,4},{4,5},{5,6},{6,7},{15,8},{8,9},{9,10... | collective-permute-start | bytes 786440 | tf_op jit(solution)/shard_map/ppermute | solution.py:205
  145.9 7.6 %collective-permute-start.20 = (bf16[8,128,128]{2,1,0:T(8,128)(2,1)S(1)}, bf16[8,128,128]{2,1,0:T(8,128)(2,1)S(1)}, u32[]{:S(2)}, u32[]{:S(2)}) collective-permute-start(bf16[8,128,128]{2,1,0:T(8,128)(2,1)S(1)} %collective-permute-done.16.refs_1_.rest_9_), channel_id=1, source_target_pairs={{1,0},{2,1},{3,2},{4,3},{5,4},{6,5},{7,6},{0,7},{9,8},{10,9},{11,1... | collective-permute-start | bytes 786440 | tf_op jit(solution)/shard_map/ppermute | solution.py:205
  187.2 8.0 %collective-permute-start.23 = (bf16[8,128,128]{2,1,0:T(8,128)(2,1)S(1)}, bf16[8,128,128]{2,1,0:T(8,128)(2,1)S(1)}, u32[]{:S(2)}, u32[]{:S(2)}) collective-permute-start(bf16[8,128,128]{2,1,0:T(8,128)(2,1)S(1)} %get-tuple-element.53), channel_id=1, source_target_pairs={{56,0},{57,1},{58,2},{59,3},{60,4},{61,5},{62,6},{63,7},{0,8},{1,9... | collective-permute-start | bytes 786440 | tf_op jit(solution)/shard_map/ppermute | solution.py:205
  191.8 6.4 %collective-permute-start.22 = (bf16[8,128,128]{2,1,0:T(8,128)(2,1)S(1)}, bf16[8,128,128]{2,1,0:T(8,128)(2,1)S(1)}, u32[]{:S(2)}, u32[]{:S(2)}) collective-permute-start(bf16[8,128,128]{2,1,0:T(8,128)(2,1)S(1)} %get-tuple-element.54), channel_id=1, source_target_pairs={{8,0},{9,1},{10,2},{11,3},{12,4},{13,5},{14,6},{15,7},{16,8},{17,9... | collective-permute-start | bytes 786440 | tf_op jit(solution)/shard_map/ppermute | solution.py:205
  191.8 7.2 %collective-permute-start.25 = (bf16[8,128,128]{2,1,0:T(8,128)(2,1)S(1)}, bf16[8,128,128]{2,1,0:T(8,128)(2,1)S(1)}, u32[]{:S(2)}, u32[]{:S(2)}) collective-permute-start(bf16[8,128,128]{2,1,0:T(8,128)(2,1)S(1)} %get-tuple-element.53), channel_id=1, source_target_pairs={{7,0},{0,1},{1,2},{2,3},{3,4},{4,5},{5,6},{6,7},{15,8},{8,9},{9,10... | collective-permute-start | bytes 786440 | tf_op jit(solution)/shard_map/ppermute | solution.py:205
  192.3 6.8 %collective-permute-start.24 = (bf16[8,128,128]{2,1,0:T(8,128)(2,1)S(1)}, bf16[8,128,128]{2,1,0:T(8,128)(2,1)S(1)}, u32[]{:S(2)}, u32[]{:S(2)}) collective-permute-start(bf16[8,128,128]{2,1,0:T(8,128)(2,1)S(1)} %get-tuple-element.54), channel_id=1, source_target_pairs={{1,0},{2,1},{3,2},{4,3},{5,4},{6,5},{7,6},{0,7},{9,8},{10,9},{11,1... | collective-permute-start | bytes 786440 | tf_op jit(solution)/shard_map/ppermute | solution.py:205
  195.2 8.2 %collective-permute-start.27 = (bf16[8,128,128]{2,1,0:T(8,128)(2,1)S(1)}, bf16[8,128,128]{2,1,0:T(8,128)(2,1)S(1)}, u32[]{:S(2)}, u32[]{:S(2)}) collective-permute-start(bf16[8,128,128]{2,1,0:T(8,128)(2,1)S(1)} %collective-permute-done.23.rest_1_), channel_id=1, source_target_pairs={{7,0},{0,1},{1,2},{2,3},{3,4},{4,5},{5,6},{6,7},{15,8},{8,9},{9,10... | collective-permute-start | bytes 786440 | tf_op jit(solution)/shard_map/ppermute | solution.py:205
  198.3 7.8 %collective-permute-start.26 = (bf16[8,128,128]{2,1,0:T(8,128)(2,1)S(1)}, bf16[8,128,128]{2,1,0:T(8,128)(2,1)S(1)}, u32[]{:S(2)}, u32[]{:S(2)}) collective-permute-start(bf16[8,128,128]{2,1,0:T(8,128)(2,1)S(1)} %collective-permute-done.22.rest_0_), channel_id=1, source_target_pairs={{1,0},{2,1},{3,2},{4,3},{5,4},{6,5},{7,6},{0,7},{9,8},{10,9},{11,1... | collective-permute-start | bytes 786440 | tf_op jit(solution)/shard_map/ppermute | solution.py:205
  206.8 4.9 %collective-permute-start.28 = (bf16[128,128]{1,0:T(8,128)(2,1)S(1)}, bf16[128,128]{1,0:T(8,128)(2,1)S(1)}, u32[]{:S(2)}, u32[]{:S(2)}) collective-permute-start(bf16[128,128]{1,0:T(8,128)(2,1)S(1)} %get-tuple-element.52), channel_id=1, source_target_pairs={{0,64},{64,0},{1,65},{65,1},{2,66},{66,2},{3,67},{67,3},{4,68},{68... | collective-permute-start | bytes 98312 | tf_op jit(solution)/shard_map/ppermute | solution.py:268

commit v4 on v3

--- a/solution.py
+++ b/solution.py
@@ -102,7 +102,7 @@
     second = is_other(section)
     rows, width = query.shape
     columns = kv_own.shape[0]
-    features = width * gain_own.shape[0]
+    features = gain_own.shape[1]
     total = squares_of(buffers[-late:], squares[...])
     scale = lax.rsqrt(jnp.sum(total, axis=1, keepdims=True) / features + norm_epsilon)
 
@@ -110,9 +110,9 @@
         q_sum, kv_sum = carry
         normed, kv_parts = [], []
         for part, place in chunk:
-            gain = jnp.where(second, gain_other[place], gain_own[place])
+            span = at(place, width)
+            gain = jnp.where(second, gain_other[:, span], gain_own[:, span]).astype(jnp.float32)
             normed.append((part.astype(jnp.float32) * scale * gain).astype(jnp.bfloat16))
-            span = at(place, width)
             kv_parts.append(jnp.where(second, kv_other[:, span], kv_own[:, span]))
         normed = jnp.concatenate(normed, axis=1)
         weight = weight_rows(second, own, other, chunk, width)
@@ -171,12 +171,16 @@
         outs[1][...] = jnp.broadcast_to(out[None], outs[1].shape)
 
 
-def start_kernel(inputs, segments, current, copies, segment_row):
+def start_kernel(inputs, segments, current, copies, segment_row, both, sems):
     me = lax.axis_index("section")
-    block = inputs[me]
-    current[...] = block
-    copies[...] = jnp.broadcast_to(block[None], copies.shape)
-    segment_row[...] = jnp.where(me == 0, segments[0:1, :], segments[1:2, :])
+    fetch = pltpu.make_async_copy(inputs.at[me], current, sems.at[0])
+    fetch_rows = pltpu.make_async_copy(segments, both, sems.at[1])
+    fetch.start()
+    fetch_rows.start()
+    fetch_rows.wait()
+    segment_row[...] = jnp.where(me == 0, both[0:1, :], both[1:2, :])
+    fetch.wait()
+    copies[...] = jnp.broadcast_to(current[...][None], copies.shape)
 
 
 def place_kernel(mine, theirs, result):
@@ -211,6 +215,7 @@
 
 def near_stage(own):
     low, high = own[:8], own[8:]
+
     xa, xb = from_neighbour(low, 1, 0), from_neighbour(high, -1, 0)
     ya, yb = from_neighbour(low, 0, 1), from_neighbour(high, 0, -1)
     da, db = from_neighbour(xa, 0, 1), from_neighbour(xb, 0, -1)
@@ -223,17 +228,27 @@
     ring = lax.axis_size(Y)
     swap = [(0, 1), (1, 0)]
     own = [w_query[0, 0], w_keyval[0, 0].T, w_output[0, 0]]
-    gain = gains[0].astype(jnp.float32).reshape(-1, 1, width)
     other = []
     for w in own:
         other.append(lax.ppermute(w, "section", swap))
-    other_gain = lax.ppermute(gain, "section", swap)
+    other_gain = lax.ppermute(gains[0], "section", swap)
     shape = jax.ShapeDtypeStruct
     bf16 = functools.partial(shape, dtype=jnp.bfloat16)
     f32 = functools.partial(shape, dtype=jnp.float32)
     columns = own[1].shape[0]
     outs = (bf16((rows, width)), bf16((FAR_COUNT, rows, width)), shape((1, rows), jnp.int32))
-    current, copies, segment_row = call(start_kernel, outs, 4, inputs, segments)
+    anywhere, vmem = pl.BlockSpec(memory_space=pltpu.HBM), pl.BlockSpec(memory_space=pltpu.VMEM)
+    current, copies, segment_row = pl.pallas_call(
+        start_kernel,
+        out_shape=outs,
+        in_specs=[anywhere, anywhere],
+        out_specs=(vmem,) * len(outs),
+        scratch_shapes=[
+            pltpu.VMEM(segments.shape, segments.dtype),
+            pltpu.SemaphoreType.DMA((2,)),
+        ],
+        compiler_params=pltpu.CompilerParams(vmem_limit_bytes=2 * MIB),
+    )(*(pltpu.with_memory_space_constraint(a, pltpu.HBM) for a in (inputs, segments)))
     copies, segment_row, freqs = lax.optimization_barrier((copies, segment_row, frequencies()))
     stages = len(STAGES)
     for s in range(sections):
@@ -246,7 +261,7 @@
         squares, cosine, sine, allowed = lax.optimization_barrier(
             (squares, cosine, sine, allowed)
         )
-        weights = (gain, other_gain, own[0], other[0], own[1], other[1])
+        weights = (gains[0], other_gain, own[0], other[0], own[1], other[1])
         kernel = functools.partial(project_kernel, s, sum(STAGES, ()), len(STAGES[-1]))
         outs = (bf16((rows, width)), bf16((ring, columns, rows)))
         query, keyval = call(kernel, outs, 10, squares, *weights, cosine, sine, *sum(near, ()))

time: 216 us -> 215 us (level)
    pallas_call x14 -> x13, Pallas kernels: 15.4 us -> 14.5 us  [call(): pl.pallas_call(kernel, out_shape=outs, in_specs=[vmem] * len(args), out_s...]
  transfers between devices with their start and end apart: 30 -> 30, of which waited for: 17 -> 17; matrix products, arithmetic and copies ran while one was open for 1% -> 0% of each run, Pallas kernels for 4% -> 4%
where the time goes in v4:
time: 215 us; the launch traced here: 212 us
  blocking collectives  81.1 us (38%)
  starting transfers between devices  67.4 us (31%)
  waiting for transfers between devices  44.6 us (21%)
  Pallas kernels  16.3 us (8%)
    all_to_all x3, blocking collectives, far_stage(): return lax.all_to_all(copies, FAR, 0, 0, tiled=True)  58.8 us
    ppermute x24, starting transfers between devices, from_neighbour(): return lax.ppermute(block, MESH, pairs)  41 us
    ppermute x24, waiting for transfers between devices, from_neighbour(): return lax.ppermute(block, MESH, pairs)  29.7 us
    all_to_all x2, blocking collectives, shards(): keyval = lax.all_to_all(keyval, Y, 0, 0, tiled=True).reshape(-1, rows)  22.3 us
    all_to_all x1, starting transfers between devices, far_stage(): return lax.all_to_all(copies, FAR, 0, 0, tiled=True)  17 us
    pallas_call x13, Pallas kernels, call(): pl.pallas_call(kernel, out_shape=outs, in_specs=[vmem] * len(args), out_s...  14.5 us
    all_to_all x1, waiting for transfers between devices, far_stage(): return lax.all_to_all(copies, FAR, 0, 0, tiled=True)  14.1 us
    ppermute x3, starting transfers between devices, shards(): other.append(lax.ppermute(w, 'section', swap))  5.15 us
  transfers between devices with their start and end apart: 30, of which 17 were waited for; matrix products, arithmetic and copies ran while one was open for 0% of the time, Pallas kernels for 4%

profile of v4, /device:TPU:647, one launch (start us, length us, event | category | flops | bytes accessed | tf_op | source)
XLA Modules:
  0.0 211.5 jit_solution(11694300431089277407)
XLA Ops:
  0.0 1.8 shard_map.64
  1.9 17.0 %all-to-all-start = ((bf16[16,128,128]{2,1,0:T(8,128)(2,1)}), bf16[16,128,128]{2,1,0:T(8,128)(2,1)S(1)}, u32[]{:S(2)}, u32[]{:S(2)}) async-start(bf16[16,128,128]{2,1,0:T(8,128)(2,1)} %get-tuple-element.32), calls=%async_computation | async-start | bytes 1048576 | tf_op jit(solution)/shard_map/all_to_all | solution.py:213
  18.9 1.2 collective-permute-start.6
  20.1 0.1 collective-permute-start.5
  20.2 14.1 %all-to-all-done.refs_0_.rest_8_ = bf16[16,128,128]{2,1,0:T(8,128)(2,1)S(1)} async-done(((bf16[16,128,128]{2,1,0:T(8,128)(2,1)}), bf16[16,128,128]{2,1,0:T(8,128)(2,1)S(1)}, u32[]{:S(2)}, u32[]{:S(2)}) %all-to-all-start) | async-done | bytes 524320 | tf_op jit(solution)/shard_map/all_to_all | solution.py:213
  34.3 1.5 collective-permute-start.4
  35.9 4.1 %collective-permute-start.2 = (bf16[8,128,128]{2,1,0:T(8,128)(2,1)S(1)}, bf16[8,128,128]{2,1,0:T(8,128)(2,1)S(1)}, u32[]{:S(2)}, u32[]{:S(2)}) collective-permute-start(bf16[8,128,128]{2,1,0:T(8,128)(2,1)S(1)} %get-tuple-element.59), channel_id=1, source_target_pairs={{56,0},{57,1},{58,2},{59,3},{60,4},{61,5},{62,6},{63,7},{0,8},{1,9... | collective-permute-start | bytes 786440 | tf_op jit(solution)/shard_map/ppermute | solution.py:209
  40.0 0.2 fusion
  40.2 1.8 collective-permute-start.3
  42.0 1.0 collective-permute-done.4.refs_4_.rest_12_
  43.0 2.0 collective-permute-start.7
  45.0 0.3 fusion.2
  45.3 2.0 collective-permute-start
  47.3 0.4 collective-permute-start.9
  47.7 1.2 collective-permute-done.1.refs_1_.rest_9_
  48.9 1.1 collective-permute-start.8
  50.2 0.2 shard_map.65.squares
  50.4 3.3 %collective-permute-done.9.rest_14_ = bf16[8,128,128]{2,1,0:T(8,128)(2,1)S(1)} collective-permute-done((bf16[8,128,128]{2,1,0:T(8,128)(2,1)S(1)}, bf16[8,128,128]{2,1,0:T(8,128)(2,1)S(1)}, u32[]{:S(2)}, u32[]{:S(2)}) %collective-permute-start.9) | collective-permute-done | bytes 262176 | tf_op jit(solution)/shard_map/ppermute | solution.py:209
  53.8 0.7 collective-permute-done.8.rest_13_
  54.5 1.0 copy-done.2
  55.5 3.1 %shard_map.66 = (bf16[128,128]{1,0:T(8,128)(2,1)S(1)}, bf16[8,32,128]{2,1,0:T(8,128)(2,1)S(1)}) custom-call(f32[128,128]{1,0:T(8,128)S(1)} %shard_map.65.squares, bf16[1,8192]{1,0:T(2,128)(2,1)S(1)} %bitcast.26, bf16[1,8192]{1,0:T(2,128)(2,1)S(1)} %collective-permute-done.5.rest_1_, bf16[8192,128]{1,0:T(8,128)(2,1)S(1)} %bitcast.18, ...), custom_call_target="tpu_custom_call" | custom-call | tf_op jit(solution)/shard_map/pallas_call | solution.py:194
  58.6 11.7 %all_to_all.30 = bf16[8,32,128]{2,1,0:T(8,128)(2,1)S(1)} all-to-all(bf16[8,32,128]{2,1,0:T(8,128)(2,1)S(1)} %get-tuple-element.41), channel_id=1, replica_groups=mesh['groups'=2,'section'=2,'x2'=2,'x1'=2,'x0'=2,'y2'=2,'y1'=2,'y0'=2] {..., dimensions={0} | all-to-all | bytes 131072 | tf_op jit(solution)/shard_map/all_to_all | solution.py:268
  70.3 0.5 shard_map.67
  70.8 16.9 %all_to_all.31.rest_0_ = bf16[16,128,128]{2,1,0:T(8,128)(2,1)S(1)} all-to-all(bf16[16,128,128]{2,1,0:T(8,128)(2,1)S(1)} %shard_map.67), channel_id=1, replica_groups=mesh['groups'=2,'section'=2,'x2'=2,'x1'=2,'x0'=2,'y2'=2,'y1'=2,'y0'=2] {..., dimensions={0} | all-to-all | bytes 1048576 | tf_op jit(solution)/shard_map/all_to_all | solution.py:213
  87.8 7.9 %collective-permute-start.11 = (bf16[8,128,128]{2,1,0:T(8,128)(2,1)S(1)}, bf16[8,128,128]{2,1,0:T(8,128)(2,1)S(1)}, u32[]{:S(2)}, u32[]{:S(2)}) collective-permute-start(bf16[8,128,128]{2,1,0:T(8,128)(2,1)S(1)} %get-tuple-element.57), channel_id=1, source_target_pairs={{56,0},{57,1},{58,2},{59,3},{60,4},{61,5},{62,6},{63,7},{0,8},{1,9... | collective-permute-start | bytes 786440 | tf_op jit(solution)/shard_map/ppermute | solution.py:209
  95.6 1.2 collective-permute-start.13
  96.9 1.4 collective-permute-start.12
  98.3 0.6 collective-permute-done.11.rest_1_
  98.9 1.2 collective-permute-start.15
  100.2 1.9 collective-permute-done.10.rest_0_
  102.1 0.7 collective-permute-start.14
  102.7 0.8 shard_map.68.before
  103.5 1.5 shard_map.69.before
  105.0 1.9 collective-permute-done.15.rest_1_
  106.9 2.4 %collective-permute-done.14.rest_0_ = bf16[8,128,128]{2,1,0:T(8,128)(2,1)S(1)} collective-permute-done((bf16[8,128,128]{2,1,0:T(8,128)(2,1)S(1)}, bf16[8,128,128]{2,1,0:T(8,128)(2,1)S(1)}, u32[]{:S(2)}, u32[]{:S(2)}) %collective-permute-start.14) | collective-permute-done | bytes 262176 | tf_op jit(solution)/shard_map/ppermute | solution.py:209
  109.3 0.8 shard_map.70
  110.1 21.3 %all_to_all.32.refs_0_.rest_8_ = bf16[16,128,128]{2,1,0:T(8,128)(2,1)S(1)} all-to-all(bf16[16,128,128]{2,1,0:T(8,128)(2,1)S(1)} %get-tuple-element.44), channel_id=1, replica_groups=mesh['groups'=2,'section'=2,'x2'=2,'x1'=2,'x0'=2,'y2'=2,'y1'=2,'y0'=2] {..., dimensions={0} | all-to-all | bytes 1048576 | tf_op jit(solution)/shard_map/all_to_all | solution.py:213
  131.5 7.1 %collective-permute-start.17 = (bf16[8,128,128]{2,1,0:T(8,128)(2,1)S(1)}, bf16[8,128,128]{2,1,0:T(8,128)(2,1)S(1)}, u32[]{:S(2)}, u32[]{:S(2)}) collective-permute-start(bf16[8,128,128]{2,1,0:T(8,128)(2,1)S(1)} %get-tuple-element.55), channel_id=1, source_target_pairs={{56,0},{57,1},{58,2},{59,3},{60,4},{61,5},{62,6},{63,7},{0,8},{1,9... | collective-permute-start | bytes 786440 | tf_op jit(solution)/shard_map/ppermute | solution.py:209
  138.5 0.7 collective-permute-start.16
  139.2 0.3 collective-permute-start.19
  139.5 2.4 %collective-permute-start.18 = (bf16[8,128,128]{2,1,0:T(8,128)(2,1)S(1)}, bf16[8,128,128]{2,1,0:T(8,128)(2,1)S(1)}, u32[]{:S(2)}, u32[]{:S(2)}) collective-permute-start(bf16[8,128,128]{2,1,0:T(8,128)(2,1)S(1)} %get-tuple-element.56), channel_id=1, source_target_pairs={{1,0},{2,1},{3,2},{4,3},{5,4},{6,5},{7,6},{0,7},{9,8},{10,9},{11,1... | collective-permute-start | bytes 786440 | tf_op jit(solution)/shard_map/ppermute | solution.py:209
  141.9 3.1 %collective-permute-done.17.refs_2_.rest_10_ = bf16[8,128,128]{2,1,0:T(8,128)(2,1)S(1)} collective-permute-done((bf16[8,128,128]{2,1,0:T(8,128)(2,1)S(1)}, bf16[8,128,128]{2,1,0:T(8,128)(2,1)S(1)}, u32[]{:S(2)}, u32[]{:S(2)}) %collective-permute-start.17) | collective-permute-done | bytes 262176 | tf_op jit(solution)/shard_map/ppermute | solution.py:209
  144.9 0.3 collective-permute-start.21
  145.2 2.4 %collective-permute-start.20 = (bf16[8,128,128]{2,1,0:T(8,128)(2,1)S(1)}, bf16[8,128,128]{2,1,0:T(8,128)(2,1)S(1)}, u32[]{:S(2)}, u32[]{:S(2)}) collective-permute-start(bf16[8,128,128]{2,1,0:T(8,128)(2,1)S(1)} %collective-permute-done.16.refs_1_.rest_9_), channel_id=1, source_target_pairs={{1,0},{2,1},{3,2},{4,3},{5,4},{6,5},{7,6},{0,7},{9,8},{10,9},{11,1... | collective-permute-start | bytes 786440 | tf_op jit(solution)/shard_map/ppermute | solution.py:209
  147.6 0.2 shard_map.71.squares
  147.8 4.8 %collective-permute-done.21.rest_14_ = bf16[8,128,128]{2,1,0:T(8,128)(2,1)S(1)} collective-permute-done((bf16[8,128,128]{2,1,0:T(8,128)(2,1)S(1)}, bf16[8,128,128]{2,1,0:T(8,128)(2,1)S(1)}, u32[]{:S(2)}, u32[]{:S(2)}) %collective-permute-start.21) | collective-permute-done | bytes 262176 | tf_op jit(solution)/shard_map/ppermute | solution.py:209
  152.6 3.1 %shard_map.72 = (bf16[128,128]{1,0:T(8,128)(2,1)S(1)}, bf16[8,32,128]{2,1,0:T(8,128)(2,1)S(1)}) custom-call(f32[128,128]{1,0:T(8,128)S(1)} %shard_map.71.squares, bf16[1,8192]{1,0:T(2,128)(2,1)S(1)} %bitcast.27, bf16[1,8192]{1,0:T(2,128)(2,1)S(1)} %collective-permute-done.5.rest_1_, bf16[8192,128]{1,0:T(8,128)(2,1)S(1)} %bitcast.19, ...), custom_call_target="tpu_custom_call" | custom-call | tf_op jit(solution)/shard_map/pallas_call | solution.py:194
  155.7 10.7 %all_to_all.33 = bf16[8,32,128]{2,1,0:T(8,128)(2,1)S(1)} all-to-all(bf16[8,32,128]{2,1,0:T(8,128)(2,1)S(1)} %get-tuple-element.49), channel_id=1, replica_groups=mesh['groups'=2,'section'=2,'x2'=2,'x1'=2,'x0'=2,'y2'=2,'y1'=2,'y0'=2] {..., dimensions={0} | all-to-all | bytes 131072 | tf_op jit(solution)/shard_map/all_to_all | solution.py:268
  166.4 0.5 shard_map.73
  166.9 20.6 %all_to_all.34.rest_0_ = bf16[16,128,128]{2,1,0:T(8,128)(2,1)S(1)} all-to-all(bf16[16,128,128]{2,1,0:T(8,128)(2,1)S(1)} %shard_map.73), channel_id=1, replica_groups=mesh['groups'=2,'section'=2,'x2'=2,'x1'=2,'x0'=2,'y2'=2,'y1'=2,'y0'=2] {..., dimensions={0} | all-to-all | bytes 1048576 | tf_op jit(solution)/shard_map/all_to_all | solution.py:213
  187.6 3.5 %collective-permute-start.23 = (bf16[8,128,128]{2,1,0:T(8,128)(2,1)S(1)}, bf16[8,128,128]{2,1,0:T(8,128)(2,1)S(1)}, u32[]{:S(2)}, u32[]{:S(2)}) collective-permute-start(bf16[8,128,128]{2,1,0:T(8,128)(2,1)S(1)} %get-tuple-element.53), channel_id=1, source_target_pairs={{56,0},{57,1},{58,2},{59,3},{60,4},{61,5},{62,6},{63,7},{0,8},{1,9... | collective-permute-start | bytes 786440 | tf_op jit(solution)/shard_map/ppermute | solution.py:209
  191.1 0.3 collective-permute-start.25
  191.4 2.4 %collective-permute-start.24 = (bf16[8,128,128]{2,1,0:T(8,128)(2,1)S(1)}, bf16[8,128,128]{2,1,0:T(8,128)(2,1)S(1)}, u32[]{:S(2)}, u32[]{:S(2)}) collective-permute-start(bf16[8,128,128]{2,1,0:T(8,128)(2,1)S(1)} %get-tuple-element.54), channel_id=1, source_target_pairs={{1,0},{2,1},{3,2},{4,3},{5,4},{6,5},{7,6},{0,7},{9,8},{10,9},{11,1... | collective-permute-start | bytes 786440 | tf_op jit(solution)/shard_map/ppermute | solution.py:209
  193.8 0.6 collective-permute-done.23.rest_1_
  194.4 0.3 collective-permute-start.27
  194.7 2.8 %collective-permute-done.22.rest_0_ = bf16[8,128,128]{2,1,0:T(8,128)(2,1)S(1)} collective-permute-done((bf16[8,128,128]{2,1,0:T(8,128)(2,1)S(1)}, bf16[8,128,128]{2,1,0:T(8,128)(2,1)S(1)}, u32[]{:S(2)}, u32[]{:S(2)}) %collective-permute-start.22) | collective-permute-done | bytes 262176 | tf_op jit(solution)/shard_map/ppermute | solution.py:209
  197.5 0.8 shard_map.74.before
  198.3 1.5 shard_map.75.before
  199.9 2.9 %collective-permute-done.27.rest_2_ = bf16[8,128,128]{2,1,0:T(8,128)(2,1)S(1)} collective-permute-done((bf16[8,128,128]{2,1,0:T(8,128)(2,1)S(1)}, bf16[8,128,128]{2,1,0:T(8,128)(2,1)S(1)}, u32[]{:S(2)}, u32[]{:S(2)}) %collective-permute-start.27) | collective-permute-done | bytes 262176 | tf_op jit(solution)/shard_map/ppermute | solution.py:209
  202.7 2.5 %collective-permute-done.26.rest_1_ = bf16[8,128,128]{2,1,0:T(8,128)(2,1)S(1)} collective-permute-done((bf16[8,128,128]{2,1,0:T(8,128)(2,1)S(1)}, bf16[8,128,128]{2,1,0:T(8,128)(2,1)S(1)}, u32[]{:S(2)}, u32[]{:S(2)}) %collective-permute-start.26) | collective-permute-done | bytes 262176 | tf_op jit(solution)/shard_map/ppermute | solution.py:209
  205.2 0.8 shard_map.76
  206.0 4.1 %collective-permute-start.28 = (bf16[128,128]{1,0:T(8,128)(2,1)S(1)}, bf16[128,128]{1,0:T(8,128)(2,1)S(1)}, u32[]{:S(2)}, u32[]{:S(2)}) collective-permute-start(bf16[128,128]{1,0:T(8,128)(2,1)S(1)} %get-tuple-element.52), channel_id=1, source_target_pairs={{0,64},{64,0},{1,65},{65,1},{2,66},{66,2},{3,67},{67,3},{4,68},{68... | collective-permute-start | bytes 98312 | tf_op jit(solution)/shard_map/ppermute | solution.py:283
  210.1 0.9 collective-permute-done.28.theirs
  210.9 0.6 shard_map.77
  (35 shorter events, 0.5 us)
Async XLA Ops:
  0.0 45.3 %copy-start = (bf16[1,1,8192,128]{3,2,1,0:T(8,128)(2,1)S(1)}, bf16[1,1,8192,128]{3,2,1,0:T(8,128)(2,1)}, u32[]{:S(2)}) copy-start(bf16[1,1,8192,128]{3,2,1,0:T(8,128)(2,1)} %param.11) | copy-start | bytes 6291460
  1.9 52.6 %copy-start.4 = (bf16[1,1,8192]{2,1,0:T(2,128)(2,1)S(1)}, bf16[1,1,8192]{2,1,0:T(2,128)(2,1)}, u32[]{:S(2)}) copy-start(bf16[1,1,8192]{2,1,0:T(2,128)(2,1)} %param.8) | copy-start | bytes 49156
  1.9 32.4 %all-to-all-start = ((bf16[16,128,128]{2,1,0:T(8,128)(2,1)}), bf16[16,128,128]{2,1,0:T(8,128)(2,1)S(1)}, u32[]{:S(2)}, u32[]{:S(2)}) async-start(bf16[16,128,128]{2,1,0:T(8,128)(2,1)} %get-tuple-element.32), calls=%async_computation | async-start | bytes 1048576 | tf_op jit(solution)/shard_map/all_to_all | solution.py:213
  18.9 35.6 %collective-permute-start.6 = (bf16[8192,128]{1,0:T(8,128)(2,1)}, bf16[8192,128]{1,0:T(8,128)(2,1)}, u32[]{:S(2)}, u32[]{:S(2)}) collective-permute-start(bf16[8192,128]{1,0:T(8,128)(2,1)} %bitcast.17), channel_id=1, source_target_pairs={{0,64},{64,0},{1,65},{65,1},{2,66},{66,2},{3,67},{67,3},{4,68},{68... | collective-permute-start | bytes 6291464 | tf_op jit(solution)/shard_map/ppermute | solution.py:233
  20.1 21.9 %collective-permute-start.5 = (bf16[1,8192]{1,0:T(2,128)(2,1)}, bf16[1,8192]{1,0:T(2,128)(2,1)S(1)}, u32[]{:S(2)}, u32[]{:S(2)}) collective-permute-start(bf16[1,8192]{1,0:T(2,128)(2,1)} %bitcast.25), channel_id=1, source_target_pairs={{0,64},{64,0},{1,65},{65,1},{2,66},{66,2},{3,67},{67,3},{4,68},{68... | collective-permute-start | bytes 49160 | tf_op jit(solution)/shard_map/ppermute | solution.py:234
  34.3 20.2 %copy-start.1 = (bf16[1,1,8192,128]{3,2,1,0:T(8,128)(2,1)S(1)}, bf16[1,1,8192,128]{3,2,1,0:T(8,128)(2,1)}, u32[]{:S(2)}) copy-start(bf16[1,1,8192,128]{3,2,1,0:T(8,128)(2,1)} %param.9) | copy-start | bytes 6291460
  34.3 8.7 %collective-permute-start.4 = (bf16[8,128,128]{2,1,0:T(8,128)(2,1)S(1)}, bf16[8,128,128]{2,1,0:T(8,128)(2,1)S(1)}, u32[]{:S(2)}, u32[]{:S(2)}) collective-permute-start(bf16[8,128,128]{2,1,0:T(8,128)(2,1)S(1)} %get-tuple-element.59), channel_id=1, source_target_pairs={{7,0},{0,1},{1,2},{2,3},{3,4},{4,5},{5,6},{6,7},{15,8},{8,9},{9,10... | collective-permute-start | bytes 786440 | tf_op jit(solution)/shard_map/ppermute | solution.py:209
  35.9 9.5 %collective-permute-start.2 = (bf16[8,128,128]{2,1,0:T(8,128)(2,1)S(1)}, bf16[8,128,128]{2,1,0:T(8,128)(2,1)S(1)}, u32[]{:S(2)}, u32[]{:S(2)}) collective-permute-start(bf16[8,128,128]{2,1,0:T(8,128)(2,1)S(1)} %get-tuple-element.59), channel_id=1, source_target_pairs={{56,0},{57,1},{58,2},{59,3},{60,4},{61,5},{62,6},{63,7},{0,8},{1,9... | collective-permute-start | bytes 786440 | tf_op jit(solution)/shard_map/ppermute | solution.py:209
  40.2 7.1 %collective-permute-start.3 = (bf16[8,128,128]{2,1,0:T(8,128)(2,1)S(1)}, bf16[8,128,128]{2,1,0:T(8,128)(2,1)S(1)}, u32[]{:S(2)}, u32[]{:S(2)}) collective-permute-start(bf16[8,128,128]{2,1,0:T(8,128)(2,1)S(1)} %get-tuple-element.60), channel_id=1, source_target_pairs={{1,0},{2,1},{3,2},{4,3},{5,4},{6,5},{7,6},{0,7},{9,8},{10,9},{11,1... | collective-permute-start | bytes 786440 | tf_op jit(solution)/shard_map/ppermute | solution.py:209
  42.0 6.9 %collective-permute-start.1 = (bf16[8,128,128]{2,1,0:T(8,128)(2,1)S(1)}, bf16[8,128,128]{2,1,0:T(8,128)(2,1)S(1)}, u32[]{:S(2)}, u32[]{:S(2)}) collective-permute-start(bf16[8,128,128]{2,1,0:T(8,128)(2,1)S(1)} %get-tuple-element.60), channel_id=1, source_target_pairs={{8,0},{9,1},{10,2},{11,3},{12,4},{13,5},{14,6},{15,7},{16,8},{17,9... | collective-permute-start | bytes 786440 | tf_op jit(solution)/shard_map/ppermute | solution.py:209
  43.0 7.4 %collective-permute-start.7 = (bf16[32,8192]{1,0:T(8,128)(2,1)}, bf16[32,8192]{1,0:T(8,128)(2,1)S(1)}, u32[]{:S(2)}, u32[]{:S(2)}) collective-permute-start(bf16[32,8192]{1,0:T(8,128)(2,1)} %bitcast.20), channel_id=1, source_target_pairs={{0,64},{64,0},{1,65},{65,1},{2,66},{66,2},{3,67},{67,3},{4,68},{68... | collective-permute-start | bytes 1572872 | tf_op jit(solution)/shard_map/ppermute | solution.py:233
  45.3 57.4 %collective-permute-start = (bf16[8192,128]{1,0:T(8,128)(2,1)S(1)}, bf16[8192,128]{1,0:T(8,128)(2,1)S(1)}, u32[]{:S(2)}, u32[]{:S(2)}) collective-permute-start(bf16[8192,128]{1,0:T(8,128)(2,1)S(1)} %bitcast.10), channel_id=1, source_target_pairs={{0,64},{64,0},{1,65},{65,1},{2,66},{66,2},{3,67},{67,3},{4,68},{68... | collective-permute-start | bytes 6291464 | tf_op jit(solution)/shard_map/ppermute | solution.py:233
  47.3 6.4 %collective-permute-start.9 = (bf16[8,128,128]{2,1,0:T(8,128)(2,1)S(1)}, bf16[8,128,128]{2,1,0:T(8,128)(2,1)S(1)}, u32[]{:S(2)}, u32[]{:S(2)}) collective-permute-start(bf16[8,128,128]{2,1,0:T(8,128)(2,1)S(1)} %collective-permute-done.2.refs_2_.rest_10_), channel_id=1, source_target_pairs={{7,0},{0,1},{1,2},{2,3},{3,4},{4,5},{5,6},{6,7},{15,8},{8,9},{9,10... | collective-permute-start | bytes 786440 | tf_op jit(solution)/shard_map/ppermute | solution.py:209
  48.9 5.5 %collective-permute-start.8 = (bf16[8,128,128]{2,1,0:T(8,128)(2,1)S(1)}, bf16[8,128,128]{2,1,0:T(8,128)(2,1)S(1)}, u32[]{:S(2)}, u32[]{:S(2)}) collective-permute-start(bf16[8,128,128]{2,1,0:T(8,128)(2,1)S(1)} %collective-permute-done.1.refs_1_.rest_9_), channel_id=1, source_target_pairs={{1,0},{2,1},{3,2},{4,3},{5,4},{6,5},{7,6},{0,7},{9,8},{10,9},{11,1... | collective-permute-start | bytes 786440 | tf_op jit(solution)/shard_map/ppermute | solution.py:209
  54.4 1.0 copy-start.2
  87.8 11.2 %collective-permute-start.11 = (bf16[8,128,128]{2,1,0:T(8,128)(2,1)S(1)}, bf16[8,128,128]{2,1,0:T(8,128)(2,1)S(1)}, u32[]{:S(2)}, u32[]{:S(2)}) collective-permute-start(bf16[8,128,128]{2,1,0:T(8,128)(2,1)S(1)} %get-tuple-element.57), channel_id=1, source_target_pairs={{56,0},{57,1},{58,2},{59,3},{60,4},{61,5},{62,6},{63,7},{0,8},{1,9... | collective-permute-start | bytes 786440 | tf_op jit(solution)/shard_map/ppermute | solution.py:209
  95.6 6.4 %collective-permute-start.10 = (bf16[8,128,128]{2,1,0:T(8,128)(2,1)S(1)}, bf16[8,128,128]{2,1,0:T(8,128)(2,1)S(1)}, u32[]{:S(2)}, u32[]{:S(2)}) collective-permute-start(bf16[8,128,128]{2,1,0:T(8,128)(2,1)S(1)} %get-tuple-element.58), channel_id=1, source_target_pairs={{8,0},{9,1},{10,2},{11,3},{12,4},{13,5},{14,6},{15,7},{16,8},{17,9... | collective-permute-start | bytes 786440 | tf_op jit(solution)/shard_map/ppermute | solution.py:209
  95.6 7.9 %collective-permute-start.13 = (bf16[8,128,128]{2,1,0:T(8,128)(2,1)S(1)}, bf16[8,128,128]{2,1,0:T(8,128)(2,1)S(1)}, u32[]{:S(2)}, u32[]{:S(2)}) collective-permute-start(bf16[8,128,128]{2,1,0:T(8,128)(2,1)S(1)} %get-tuple-element.57), channel_id=1, source_target_pairs={{7,0},{0,1},{1,2},{2,3},{3,4},{4,5},{5,6},{6,7},{15,8},{8,9},{9,10... | collective-permute-start | bytes 786440 | tf_op jit(solution)/shard_map/ppermute | solution.py:209
  96.9 6.6 %collective-permute-start.12 = (bf16[8,128,128]{2,1,0:T(8,128)(2,1)S(1)}, bf16[8,128,128]{2,1,0:T(8,128)(2,1)S(1)}, u32[]{:S(2)}, u32[]{:S(2)}) collective-permute-start(bf16[8,128,128]{2,1,0:T(8,128)(2,1)S(1)} %get-tuple-element.58), channel_id=1, source_target_pairs={{1,0},{2,1},{3,2},{4,3},{5,4},{6,5},{7,6},{0,7},{9,8},{10,9},{11,1... | collective-permute-start | bytes 786440 | tf_op jit(solution)/shard_map/ppermute | solution.py:209
  98.9 8.0 %collective-permute-start.15 = (bf16[8,128,128]{2,1,0:T(8,128)(2,1)S(1)}, bf16[8,128,128]{2,1,0:T(8,128)(2,1)S(1)}, u32[]{:S(2)}, u32[]{:S(2)}) collective-permute-start(bf16[8,128,128]{2,1,0:T(8,128)(2,1)S(1)} %collective-permute-done.11.rest_1_), channel_id=1, source_target_pairs={{7,0},{0,1},{1,2},{2,3},{3,4},{4,5},{5,6},{6,7},{15,8},{8,9},{9,10... | collective-permute-start | bytes 786440 | tf_op jit(solution)/shard_map/ppermute | solution.py:209
  102.1 7.2 %collective-permute-start.14 = (bf16[8,128,128]{2,1,0:T(8,128)(2,1)S(1)}, bf16[8,128,128]{2,1,0:T(8,128)(2,1)S(1)}, u32[]{:S(2)}, u32[]{:S(2)}) collective-permute-start(bf16[8,128,128]{2,1,0:T(8,128)(2,1)S(1)} %collective-permute-done.10.rest_0_), channel_id=1, source_target_pairs={{1,0},{2,1},{3,2},{4,3},{5,4},{6,5},{7,6},{0,7},{9,8},{10,9},{11,1... | collective-permute-start | bytes 786440 | tf_op jit(solution)/shard_map/ppermute | solution.py:209
  110.1 42.5 %copy-start.3 = (bf16[1,1,8192,32]{2,3,1,0:T(8,128)(2,1)S(1)}, bf16[1,1,8192,32]{2,3,1,0:T(8,128)(2,1)}, u32[]{:S(2)}) copy-start(bf16[1,1,8192,32]{2,3,1,0:T(8,128)(2,1)} %param.10) | copy-start | bytes 1572868
  131.5 13.5 %collective-permute-start.17 = (bf16[8,128,128]{2,1,0:T(8,128)(2,1)S(1)}, bf16[8,128,128]{2,1,0:T(8,128)(2,1)S(1)}, u32[]{:S(2)}, u32[]{:S(2)}) collective-permute-start(bf16[8,128,128]{2,1,0:T(8,128)(2,1)S(1)} %get-tuple-element.55), channel_id=1, source_target_pairs={{56,0},{57,1},{58,2},{59,3},{60,4},{61,5},{62,6},{63,7},{0,8},{1,9... | collective-permute-start | bytes 786440 | tf_op jit(solution)/shard_map/ppermute | solution.py:209
  138.5 6.7 %collective-permute-start.16 = (bf16[8,128,128]{2,1,0:T(8,128)(2,1)S(1)}, bf16[8,128,128]{2,1,0:T(8,128)(2,1)S(1)}, u32[]{:S(2)}, u32[]{:S(2)}) collective-permute-start(bf16[8,128,128]{2,1,0:T(8,128)(2,1)S(1)} %get-tuple-element.56), channel_id=1, source_target_pairs={{8,0},{9,1},{10,2},{11,3},{12,4},{13,5},{14,6},{15,7},{16,8},{17,9... | collective-permute-start | bytes 786440 | tf_op jit(solution)/shard_map/ppermute | solution.py:209
  139.2 8.4 %collective-permute-start.19 = (bf16[8,128,128]{2,1,0:T(8,128)(2,1)S(1)}, bf16[8,128,128]{2,1,0:T(8,128)(2,1)S(1)}, u32[]{:S(2)}, u32[]{:S(2)}) collective-permute-start(bf16[8,128,128]{2,1,0:T(8,128)(2,1)S(1)} %get-tuple-element.55), channel_id=1, source_target_pairs={{7,0},{0,1},{1,2},{2,3},{3,4},{4,5},{5,6},{6,7},{15,8},{8,9},{9,10... | collective-permute-start | bytes 786440 | tf_op jit(solution)/shard_map/ppermute | solution.py:209
  139.5 8.1 %collective-permute-start.18 = (bf16[8,128,128]{2,1,0:T(8,128)(2,1)S(1)}, bf16[8,128,128]{2,1,0:T(8,128)(2,1)S(1)}, u32[]{:S(2)}, u32[]{:S(2)}) collective-permute-start(bf16[8,128,128]{2,1,0:T(8,128)(2,1)S(1)} %get-tuple-element.56), channel_id=1, source_target_pairs={{1,0},{2,1},{3,2},{4,3},{5,4},{6,5},{7,6},{0,7},{9,8},{10,9},{11,1... | collective-permute-start | bytes 786440 | tf_op jit(solution)/shard_map/ppermute | solution.py:209
  144.9 7.7 %collective-permute-start.21 = (bf16[8,128,128]{2,1,0:T(8,128)(2,1)S(1)}, bf16[8,128,128]{2,1,0:T(8,128)(2,1)S(1)}, u32[]{:S(2)}, u32[]{:S(2)}) collective-permute-start(bf16[8,128,128]{2,1,0:T(8,128)(2,1)S(1)} %collective-permute-done.17.refs_2_.rest_10_), channel_id=1, source_target_pairs={{7,0},{0,1},{1,2},{2,3},{3,4},{4,5},{5,6},{6,7},{15,8},{8,9},{9,10... | collective-permute-start | bytes 786440 | tf_op jit(solution)/shard_map/ppermute | solution.py:209
  145.2 7.4 %collective-permute-start.20 = (bf16[8,128,128]{2,1,0:T(8,128)(2,1)S(1)}, bf16[8,128,128]{2,1,0:T(8,128)(2,1)S(1)}, u32[]{:S(2)}, u32[]{:S(2)}) collective-permute-start(bf16[8,128,128]{2,1,0:T(8,128)(2,1)S(1)} %collective-permute-done.16.refs_1_.rest_9_), channel_id=1, source_target_pairs={{1,0},{2,1},{3,2},{4,3},{5,4},{6,5},{7,6},{0,7},{9,8},{10,9},{11,1... | collective-permute-start | bytes 786440 | tf_op jit(solution)/shard_map/ppermute | solution.py:209
  187.6 6.8 %collective-permute-start.23 = (bf16[8,128,128]{2,1,0:T(8,128)(2,1)S(1)}, bf16[8,128,128]{2,1,0:T(8,128)(2,1)S(1)}, u32[]{:S(2)}, u32[]{:S(2)}) collective-permute-start(bf16[8,128,128]{2,1,0:T(8,128)(2,1)S(1)} %get-tuple-element.53), channel_id=1, source_target_pairs={{56,0},{57,1},{58,2},{59,3},{60,4},{61,5},{62,6},{63,7},{0,8},{1,9... | collective-permute-start | bytes 786440 | tf_op jit(solution)/shard_map/ppermute | solution.py:209
  191.1 6.4 %collective-permute-start.22 = (bf16[8,128,128]{2,1,0:T(8,128)(2,1)S(1)}, bf16[8,128,128]{2,1,0:T(8,128)(2,1)S(1)}, u32[]{:S(2)}, u32[]{:S(2)}) collective-permute-start(bf16[8,128,128]{2,1,0:T(8,128)(2,1)S(1)} %get-tuple-element.54), channel_id=1, source_target_pairs={{8,0},{9,1},{10,2},{11,3},{12,4},{13,5},{14,6},{15,7},{16,8},{17,9... | collective-permute-start | bytes 786440 | tf_op jit(solution)/shard_map/ppermute | solution.py:209
  191.1 7.2 %collective-permute-start.25 = (bf16[8,128,128]{2,1,0:T(8,128)(2,1)S(1)}, bf16[8,128,128]{2,1,0:T(8,128)(2,1)S(1)}, u32[]{:S(2)}, u32[]{:S(2)}) collective-permute-start(bf16[8,128,128]{2,1,0:T(8,128)(2,1)S(1)} %get-tuple-element.53), channel_id=1, source_target_pairs={{7,0},{0,1},{1,2},{2,3},{3,4},{4,5},{5,6},{6,7},{15,8},{8,9},{9,10... | collective-permute-start | bytes 786440 | tf_op jit(solution)/shard_map/ppermute | solution.py:209
  191.4 6.9 %collective-permute-start.24 = (bf16[8,128,128]{2,1,0:T(8,128)(2,1)S(1)}, bf16[8,128,128]{2,1,0:T(8,128)(2,1)S(1)}, u32[]{:S(2)}, u32[]{:S(2)}) collective-permute-start(bf16[8,128,128]{2,1,0:T(8,128)(2,1)S(1)} %get-tuple-element.54), channel_id=1, source_target_pairs={{1,0},{2,1},{3,2},{4,3},{5,4},{6,5},{7,6},{0,7},{9,8},{10,9},{11,1... | collective-permute-start | bytes 786440 | tf_op jit(solution)/shard_map/ppermute | solution.py:209
  194.4 8.3 %collective-permute-start.27 = (bf16[8,128,128]{2,1,0:T(8,128)(2,1)S(1)}, bf16[8,128,128]{2,1,0:T(8,128)(2,1)S(1)}, u32[]{:S(2)}, u32[]{:S(2)}) collective-permute-start(bf16[8,128,128]{2,1,0:T(8,128)(2,1)S(1)} %collective-permute-done.23.rest_1_), channel_id=1, source_target_pairs={{7,0},{0,1},{1,2},{2,3},{3,4},{4,5},{5,6},{6,7},{15,8},{8,9},{9,10... | collective-permute-start | bytes 786440 | tf_op jit(solution)/shard_map/ppermute | solution.py:209
  197.5 7.6 %collective-permute-start.26 = (bf16[8,128,128]{2,1,0:T(8,128)(2,1)S(1)}, bf16[8,128,128]{2,1,0:T(8,128)(2,1)S(1)}, u32[]{:S(2)}, u32[]{:S(2)}) collective-permute-start(bf16[8,128,128]{2,1,0:T(8,128)(2,1)S(1)} %collective-permute-done.22.rest_0_), channel_id=1, source_target_pairs={{1,0},{2,1},{3,2},{4,3},{5,4},{6,5},{7,6},{0,7},{9,8},{10,9},{11,1... | collective-permute-start | bytes 786440 | tf_op jit(solution)/shard_map/ppermute | solution.py:209
  206.0 5.0 %collective-permute-start.28 = (bf16[128,128]{1,0:T(8,128)(2,1)S(1)}, bf16[128,128]{1,0:T(8,128)(2,1)S(1)}, u32[]{:S(2)}, u32[]{:S(2)}) collective-permute-start(bf16[128,128]{1,0:T(8,128)(2,1)S(1)} %get-tuple-element.52), channel_id=1, source_target_pairs={{0,64},{64,0},{1,65},{65,1},{2,66},{66,2},{3,67},{67,3},{4,68},{68... | collective-permute-start | bytes 98312 | tf_op jit(solution)/shard_map/ppermute | solution.py:283

commit v5 on v4

--- a/solution.py
+++ b/solution.py
@@ -42,18 +42,16 @@
 
 
 STAGES = (
-    ((0, 0, 0),),
-    ((1, 0, 0), (1, 0, 8), (0, 1, 0), (0, 1, 8)),
-    ((1, 1, 0), (1, 1, 8)),
+    ((0, 0),),
+    ((1, 1), (1, 0), (0, 1)),
 )
 STEP = 4
 
 
 def for_chunks(buffers, layout, body, carry, unrolled=False):
     px, py = lax.axis_index("x0"), lax.axis_index("y0")
-    for ref, (turn_x, turn_y, first) in zip(buffers, layout, strict=True):
+    for ref, (turn_x, turn_y) in zip(buffers, layout, strict=True):
         base = SIDE * jnp.where(turn_x == 1, 1 - px, px) + jnp.where(turn_y == 1, 1 - py, py)
-        base += 2 * SIDE * (first // STEP)
 
         def chunk(i, carry, ref=ref, base=base):
             place = base + 2 * SIDE * i
@@ -91,9 +89,8 @@
     return total
 
 
-def squares_kernel(*refs):
-    buffers, total = refs[:-1], refs[-1]
-    total[...] = squares_of(buffers, jnp.zeros(total.shape, jnp.float32))
+def squares_kernel(own_set, total):
+    total[...] = squares_of((own_set,), jnp.zeros(total.shape, jnp.float32))
 
 
 def project_kernel(section, layout, late, squares, *rest):
@@ -159,7 +156,8 @@
         joined = jnp.concatenate([part for part, _ in chunk], axis=1)
         return mixed + jnp.dot(joined, weight, preferred_element_type=jnp.float32)
 
-    mixed = for_chunks(buffers, layout, body, before[...].astype(jnp.float32))
+    mixed = before[...].astype(jnp.float32)
+    mixed = for_chunks(buffers, layout, body, mixed, unrolled=len(layout) > 1)
     out = mixed.astype(outs[0].dtype)
     if past:
         lower = lax.axis_index("section") == 0
@@ -171,16 +169,20 @@
         outs[1][...] = jnp.broadcast_to(out[None], outs[1].shape)
 
 
-def start_kernel(inputs, segments, current, copies, segment_row, both, sems):
+def start_kernel(
+    inputs, segments, kv, gains, current, copies, segment_row, kv_out, gains_out, both, sems
+):
     me = lax.axis_index("section")
-    fetch = pltpu.make_async_copy(inputs.at[me], current, sems.at[0])
-    fetch_rows = pltpu.make_async_copy(segments, both, sems.at[1])
-    fetch.start()
-    fetch_rows.start()
-    fetch_rows.wait()
+    moves = ((inputs.at[me], current), (segments, both), (kv, kv_out), (gains, gains_out))
+    fetches = [pltpu.make_async_copy(a, b, sems.at[k]) for k, (a, b) in enumerate(moves)]
+    for fetch in fetches:
+        fetch.start()
+    fetches[0].wait()
+    copies[...] = jnp.broadcast_to(current[...][None], copies.shape)
+    fetches[1].wait()
     segment_row[...] = jnp.where(me == 0, both[0:1, :], both[1:2, :])
-    fetch.wait()
-    copies[...] = jnp.broadcast_to(current[...][None], copies.shape)
+    fetches[2].wait()
+    fetches[3].wait()
 
 
 def place_kernel(mine, theirs, result):
@@ -214,12 +216,10 @@
 
 
 def near_stage(own):
-    low, high = own[:8], own[8:]
-
-    xa, xb = from_neighbour(low, 1, 0), from_neighbour(high, -1, 0)
-    ya, yb = from_neighbour(low, 0, 1), from_neighbour(high, 0, -1)
-    da, db = from_neighbour(xa, 0, 1), from_neighbour(xb, 0, -1)
-    return (own,), (xa, xb, ya, yb), (da, db)
+    def hop(dx, dy):
+        return from_neighbour(own, dx, dy)
+
+    return (own,), (hop(-1, -1), hop(1, 0), hop(0, 1))
 
 
 def shards(inputs, segments, gains, w_query, w_keyval, w_output):
@@ -237,18 +237,20 @@
     f32 = functools.partial(shape, dtype=jnp.float32)
     columns = own[1].shape[0]
     outs = (bf16((rows, width)), bf16((FAR_COUNT, rows, width)), shape((1, rows), jnp.int32))
+    outs += (bf16(own[1].shape), bf16(gains[0].shape))
+    sources = (inputs, segments, own[1], gains[0])
     anywhere, vmem = pl.BlockSpec(memory_space=pltpu.HBM), pl.BlockSpec(memory_space=pltpu.VMEM)
-    current, copies, segment_row = pl.pallas_call(
+    current, copies, segment_row, own[1], gain = pl.pallas_call(
         start_kernel,
         out_shape=outs,
-        in_specs=[anywhere, anywhere],
+        in_specs=[anywhere] * len(sources),
         out_specs=(vmem,) * len(outs),
         scratch_shapes=[
             pltpu.VMEM(segments.shape, segments.dtype),
-            pltpu.SemaphoreType.DMA((2,)),
+            pltpu.SemaphoreType.DMA((len(sources),)),
         ],
-        compiler_params=pltpu.CompilerParams(vmem_limit_bytes=2 * MIB),
-    )(*(pltpu.with_memory_space_constraint(a, pltpu.HBM) for a in (inputs, segments)))
+        compiler_params=pltpu.CompilerParams(vmem_limit_bytes=4 * MIB),
+    )(*(pltpu.with_memory_space_constraint(a, pltpu.HBM) for a in sources))
     copies, segment_row, freqs = lax.optimization_barrier((copies, segment_row, frequencies()))
     stages = len(STAGES)
     for s in range(sections):
@@ -257,11 +259,11 @@
             far, segment_row = lax.optimization_barrier((far, segment_row))
             cosine, sine, allowed = position_tables(segment_row[0], freqs)
         near = near_stage(far)
-        squares = call(squares_kernel, f32((rows, width)), 4, *near[0], *near[1])
+        squares = call(squares_kernel, f32((rows, width)), 4, *near[0])
         squares, cosine, sine, allowed = lax.optimization_barrier(
             (squares, cosine, sine, allowed)
         )
-        weights = (gains[0], other_gain, own[0], other[0], own[1], other[1])
+        weights = (gain, other_gain, own[0], other[0], own[1], other[1])
         kernel = functools.partial(project_kernel, s, sum(STAGES, ()), len(STAGES[-1]))
         outs = (bf16((rows, width)), bf16((ring, columns, rows)))
         query, keyval = call(kernel, outs, 10, squares, *weights, cosine, sine, *sum(near, ()))

time: 215 us -> 216 us (level)
  the two profiles are of different devices: /device:TPU:647 before, /device:TPU:513 now
where the time goes in v5:
time: 216 us; the launch traced here: 215 us
  blocking collectives  85.7 us (40%)
  waiting for transfers between devices  62.7 us (29%)
  starting transfers between devices  50.7 us (23%)
  Pallas kernels  13.5 us (6%)
    all_to_all x3, blocking collectives, far_stage(): return lax.all_to_all(copies, FAR, 0, 0, tiled=True)  65.4 us
    ppermute x12, waiting for transfers between devices, from_neighbour(): return lax.ppermute(block, MESH, pairs)  45.4 us
    ppermute x3, starting transfers between devices, shards(): other.append(lax.ppermute(w, 'section', swap))  20.7 us
    all_to_all x2, blocking collectives, shards(): keyval = lax.all_to_all(keyval, Y, 0, 0, tiled=True).reshape(-1, rows)  20.3 us
    ppermute x12, starting transfers between devices, from_neighbour(): return lax.ppermute(block, MESH, pairs)  16.4 us
    all_to_all x1, waiting for transfers between devices, far_stage(): return lax.all_to_all(copies, FAR, 0, 0, tiled=True)  16.4 us
    pallas_call x11, Pallas kernels, call(): pl.pallas_call(kernel, out_shape=outs, in_specs=[vmem] * len(args), out_s...  11.6 us
    ppermute x1, starting transfers between devices, shards(): theirs = lax.ppermute(copies, 'section', swap)  9.04 us
  transfers between devices with their start and end apart: 18, of which 12 were waited for; matrix products, arithmetic and copies ran while one was open for 0% of the time, Pallas kernels for 4%

profile of v5, /device:TPU:513, one launch (start us, length us, event | category | flops | bytes accessed | tf_op | source)
XLA Modules:
  0.0 215.1 jit_solution(7639800726067442964)
XLA Ops:
  0.0 20.4 %collective-permute-start.2 = (bf16[8192,128]{1,0:T(8,128)(2,1)}, bf16[8192,128]{1,0:T(8,128)(2,1)}, u32[]{:S(2)}, u32[]{:S(2)}) collective-permute-start(bf16[8192,128]{1,0:T(8,128)(2,1)} %bitcast.15), channel_id=1, source_target_pairs={{0,64},{64,0},{1,65},{65,1},{2,66},{66,2},{3,67},{67,3},{4,68},{68... | collective-permute-start | bytes 6291464 | tf_op jit(solution)/shard_map/ppermute | solution.py:233
  20.4 1.9 shard_map.64
  22.3 4.0 %all-to-all-start = ((bf16[16,128,128]{2,1,0:T(8,128)(2,1)}), bf16[16,128,128]{2,1,0:T(8,128)(2,1)S(1)}, u32[]{:S(2)}, u32[]{:S(2)}) async-start(bf16[16,128,128]{2,1,0:T(8,128)(2,1)} %get-tuple-element.34), calls=%async_computation | async-start | bytes 1048576 | tf_op jit(solution)/shard_map/all_to_all | solution.py:215
  26.4 0.1 collective-permute-start.3
  26.5 0.5 collective-permute-start.1
  27.0 0.2 collective-permute-start
  27.2 16.4 %all-to-all-done.own_set.rest_8_ = bf16[16,128,128]{2,1,0:T(8,128)(2,1)S(1)} async-done(((bf16[16,128,128]{2,1,0:T(8,128)(2,1)}), bf16[16,128,128]{2,1,0:T(8,128)(2,1)S(1)}, u32[]{:S(2)}, u32[]{:S(2)}) %all-to-all-start) | async-done | bytes 524320 | tf_op jit(solution)/shard_map/all_to_all | solution.py:215
  43.6 0.1 shard_map.65.squares
  43.6 0.1 collective-permute-start.6
  43.8 0.2 fusion
  44.0 0.0 collective-permute-done.1.rest_1_
  44.0 0.1 collective-permute-start.5
  44.1 0.0 collective-permute-done.3.rest_5_
  44.1 2.6 %collective-permute-start.4 = (bf16[16,128,128]{2,1,0:T(8,128)(2,1)S(1)}, bf16[16,128,128]{2,1,0:T(8,128)(2,1)S(1)}, u32[]{:S(2)}, u32[]{:S(2)}) collective-permute-start(bf16[16,128,128]{2,1,0:T(8,128)(2,1)S(1)} %all-to-all-done.own_set.rest_8_), channel_id=1, source_target_pairs={{63,0},{56,1},{57,2},{58,3},{59,4},{60,5},{61,6},{62,7},{7,8},{0,9... | collective-permute-start | bytes 1572872 | tf_op jit(solution)/shard_map/ppermute | solution.py:211
  46.7 0.3 fusion.2
  47.0 0.1 pad_maximum_fusion
  47.1 0.1 fusion.1.allowed
  47.2 8.5 %collective-permute-done.6.rest_11_ = bf16[16,128,128]{2,1,0:T(8,128)(2,1)S(1)} collective-permute-done((bf16[16,128,128]{2,1,0:T(8,128)(2,1)S(1)}, bf16[16,128,128]{2,1,0:T(8,128)(2,1)S(1)}, u32[]{:S(2)}, u32[]{:S(2)}) %collective-permute-start.6) | collective-permute-done | bytes 524320 | tf_op jit(solution)/shard_map/ppermute | solution.py:211
  55.7 0.0 collective-permute-done.5.rest_10_
  55.7 3.3 %collective-permute-done.4.rest_9_ = bf16[16,128,128]{2,1,0:T(8,128)(2,1)S(1)} collective-permute-done((bf16[16,128,128]{2,1,0:T(8,128)(2,1)S(1)}, bf16[16,128,128]{2,1,0:T(8,128)(2,1)S(1)}, u32[]{:S(2)}, u32[]{:S(2)}) %collective-permute-start.4) | collective-permute-done | bytes 524320 | tf_op jit(solution)/shard_map/ppermute | solution.py:211
  59.1 0.0 collective-permute-done.2.rest_3_
  59.1 0.0 copy-start.1
  59.1 1.6 copy-done.1
  60.7 0.0 copy-start
  60.7 3.6 %shard_map.66 = (bf16[128,128]{1,0:T(8,128)(2,1)S(1)}, bf16[8,32,128]{2,1,0:T(8,128)(2,1)S(1)}) custom-call(f32[128,128]{1,0:T(8,128)S(1)} %shard_map.65.squares, bf16[1,8192]{1,0:T(2,128)(2,1)S(1)} %get-tuple-element.40.rest_0_, bf16[1,8192]{1,0:T(2,128)(2,1)S(1)} %collective-permute-done.1.rest_1_, bf16[8192,128]{1,0:T(8,128)(2,1)S(1)} %bitcast.16, ...), custom_call_target="tpu_custom_call" | custom-call | tf_op jit(solution)/shard_map/pallas_call | solution.py:196
  64.2 10.7 %all_to_all.30 = bf16[8,32,128]{2,1,0:T(8,128)(2,1)S(1)} all-to-all(bf16[8,32,128]{2,1,0:T(8,128)(2,1)S(1)} %get-tuple-element.45), channel_id=1, replica_groups=mesh['groups'=2,'section'=2,'x2'=2,'x1'=2,'x0'=2,'y2'=2,'y1'=2,'y0'=2] {..., dimensions={0} | all-to-all | bytes 131072 | tf_op jit(solution)/shard_map/all_to_all | solution.py:270
  74.9 0.5 shard_map.67
  75.5 21.4 %all_to_all.31.rest_0_ = bf16[16,128,128]{2,1,0:T(8,128)(2,1)S(1)} all-to-all(bf16[16,128,128]{2,1,0:T(8,128)(2,1)S(1)} %shard_map.67), channel_id=1, replica_groups=mesh['groups'=2,'section'=2,'x2'=2,'x1'=2,'x0'=2,'y2'=2,'y1'=2,'y0'=2] {..., dimensions={0} | all-to-all | bytes 1048576 | tf_op jit(solution)/shard_map/all_to_all | solution.py:215
  96.8 2.2 %collective-permute-start.9 = (bf16[16,128,128]{2,1,0:T(8,128)(2,1)S(1)}, bf16[16,128,128]{2,1,0:T(8,128)(2,1)S(1)}, u32[]{:S(2)}, u32[]{:S(2)}) collective-permute-start(bf16[16,128,128]{2,1,0:T(8,128)(2,1)S(1)} %all_to_all.31.rest_0_), channel_id=1, source_target_pairs={{1,0},{2,1},{3,2},{4,3},{5,4},{6,5},{7,6},{0,7},{9,8},{10,9},{11,1... | collective-permute-start | bytes 1572872 | tf_op jit(solution)/shard_map/ppermute | solution.py:211
  99.0 0.0 collective-permute-start.8
  99.0 1.0 collective-permute-start.7
  100.0 0.0 collective-permute-done.other
  100.0 0.0 copy-done
  100.0 0.8 shard_map.68.before
  100.8 6.5 %collective-permute-done.9.rest_2_ = bf16[16,128,128]{2,1,0:T(8,128)(2,1)S(1)} collective-permute-done((bf16[16,128,128]{2,1,0:T(8,128)(2,1)S(1)}, bf16[16,128,128]{2,1,0:T(8,128)(2,1)S(1)}, u32[]{:S(2)}, u32[]{:S(2)}) %collective-permute-start.9) | collective-permute-done | bytes 524320 | tf_op jit(solution)/shard_map/ppermute | solution.py:211
  107.3 1.9 collective-permute-done.8.rest_1_
  109.2 2.0 collective-permute-done.7.rest_0_
  111.2 0.0 copy-start.2
  111.2 0.6 shard_map.69
  111.8 24.4 %all_to_all.32.own_set.rest_8_ = bf16[16,128,128]{2,1,0:T(8,128)(2,1)S(1)} all-to-all(bf16[16,128,128]{2,1,0:T(8,128)(2,1)S(1)} %get-tuple-element.48), channel_id=1, replica_groups=mesh['groups'=2,'section'=2,'x2'=2,'x1'=2,'x0'=2,'y2'=2,'y1'=2,'y0'=2] {..., dimensions={0} | all-to-all | bytes 1048576 | tf_op jit(solution)/shard_map/all_to_all | solution.py:215
  136.2 3.9 %collective-permute-start.12 = (bf16[16,128,128]{2,1,0:T(8,128)(2,1)S(1)}, bf16[16,128,128]{2,1,0:T(8,128)(2,1)S(1)}, u32[]{:S(2)}, u32[]{:S(2)}) collective-permute-start(bf16[16,128,128]{2,1,0:T(8,128)(2,1)S(1)} %all_to_all.32.own_set.rest_8_), channel_id=1, source_target_pairs={{1,0},{2,1},{3,2},{4,3},{5,4},{6,5},{7,6},{0,7},{9,8},{10,9},{11,1... | collective-permute-start | bytes 1572872 | tf_op jit(solution)/shard_map/ppermute | solution.py:211
  140.1 3.8 %collective-permute-start.11 = (bf16[16,128,128]{2,1,0:T(8,128)(2,1)S(1)}, bf16[16,128,128]{2,1,0:T(8,128)(2,1)S(1)}, u32[]{:S(2)}, u32[]{:S(2)}) collective-permute-start(bf16[16,128,128]{2,1,0:T(8,128)(2,1)S(1)} %all_to_all.32.own_set.rest_8_), channel_id=1, source_target_pairs={{8,0},{9,1},{10,2},{11,3},{12,4},{13,5},{14,6},{15,7},{16,8},{17,9... | collective-permute-start | bytes 1572872 | tf_op jit(solution)/shard_map/ppermute | solution.py:211
  143.9 0.0 collective-permute-start.10
  144.0 0.1 shard_map.70.squares
  144.0 4.3 %collective-permute-done.12.rest_11_ = bf16[16,128,128]{2,1,0:T(8,128)(2,1)S(1)} collective-permute-done((bf16[16,128,128]{2,1,0:T(8,128)(2,1)S(1)}, bf16[16,128,128]{2,1,0:T(8,128)(2,1)S(1)}, u32[]{:S(2)}, u32[]{:S(2)}) %collective-permute-start.12) | collective-permute-done | bytes 524320 | tf_op jit(solution)/shard_map/ppermute | solution.py:211
  148.4 5.7 %collective-permute-done.11.rest_10_ = bf16[16,128,128]{2,1,0:T(8,128)(2,1)S(1)} collective-permute-done((bf16[16,128,128]{2,1,0:T(8,128)(2,1)S(1)}, bf16[16,128,128]{2,1,0:T(8,128)(2,1)S(1)}, u32[]{:S(2)}, u32[]{:S(2)}) %collective-permute-start.11) | collective-permute-done | bytes 524320 | tf_op jit(solution)/shard_map/ppermute | solution.py:211
  154.1 5.2 %collective-permute-done.10.rest_9_ = bf16[16,128,128]{2,1,0:T(8,128)(2,1)S(1)} collective-permute-done((bf16[16,128,128]{2,1,0:T(8,128)(2,1)S(1)}, bf16[16,128,128]{2,1,0:T(8,128)(2,1)S(1)}, u32[]{:S(2)}, u32[]{:S(2)}) %collective-permute-start.10) | collective-permute-done | bytes 524320 | tf_op jit(solution)/shard_map/ppermute | solution.py:211
  159.3 0.0 copy-done.2
  159.3 3.4 %shard_map.71 = (bf16[128,128]{1,0:T(8,128)(2,1)S(1)}, bf16[8,32,128]{2,1,0:T(8,128)(2,1)S(1)}) custom-call(f32[128,128]{1,0:T(8,128)S(1)} %shard_map.70.squares, bf16[1,8192]{1,0:T(2,128)(2,1)S(1)} %get-tuple-element.40.rest_0_, bf16[1,8192]{1,0:T(2,128)(2,1)S(1)} %collective-permute-done.1.rest_1_, bf16[8192,128]{1,0:T(8,128)(2,1)S(1)} %bitcast.17, ...), custom_call_target="tpu_custom_call" | custom-call | tf_op jit(solution)/shard_map/pallas_call | solution.py:196
  162.8 9.6 %all_to_all.33 = bf16[8,32,128]{2,1,0:T(8,128)(2,1)S(1)} all-to-all(bf16[8,32,128]{2,1,0:T(8,128)(2,1)S(1)} %get-tuple-element.53), channel_id=1, replica_groups=mesh['groups'=2,'section'=2,'x2'=2,'x1'=2,'x0'=2,'y2'=2,'y1'=2,'y0'=2] {..., dimensions={0} | all-to-all | bytes 131072 | tf_op jit(solution)/shard_map/all_to_all | solution.py:270
  172.4 0.5 shard_map.72
  172.9 19.6 %all_to_all.34.rest_0_ = bf16[16,128,128]{2,1,0:T(8,128)(2,1)S(1)} all-to-all(bf16[16,128,128]{2,1,0:T(8,128)(2,1)S(1)} %shard_map.72), channel_id=1, replica_groups=mesh['groups'=2,'section'=2,'x2'=2,'x1'=2,'x0'=2,'y2'=2,'y1'=2,'y0'=2] {..., dimensions={0} | all-to-all | bytes 1048576 | tf_op jit(solution)/shard_map/all_to_all | solution.py:215
  192.5 0.0 collective-permute-start.15
  192.5 0.0 collective-permute-start.14
  192.5 2.6 %collective-permute-start.13 = (bf16[16,128,128]{2,1,0:T(8,128)(2,1)S(1)}, bf16[16,128,128]{2,1,0:T(8,128)(2,1)S(1)}, u32[]{:S(2)}, u32[]{:S(2)}) collective-permute-start(bf16[16,128,128]{2,1,0:T(8,128)(2,1)S(1)} %all_to_all.34.rest_0_), channel_id=1, source_target_pairs={{63,0},{56,1},{57,2},{58,3},{59,4},{60,5},{61,6},{62,7},{7,8},{0,9... | collective-permute-start | bytes 1572872 | tf_op jit(solution)/shard_map/ppermute | solution.py:211
  195.2 0.8 shard_map.73.before
  196.0 6.5 %collective-permute-done.15.rest_3_ = bf16[16,128,128]{2,1,0:T(8,128)(2,1)S(1)} collective-permute-done((bf16[16,128,128]{2,1,0:T(8,128)(2,1)S(1)}, bf16[16,128,128]{2,1,0:T(8,128)(2,1)S(1)}, u32[]{:S(2)}, u32[]{:S(2)}) %collective-permute-start.15) | collective-permute-done | bytes 524320 | tf_op jit(solution)/shard_map/ppermute | solution.py:211
  202.5 0.0 collective-permute-done.14.rest_2_
  202.5 1.4 collective-permute-done.13.rest_1_
  203.9 0.6 shard_map.74
  204.5 9.0 %collective-permute-start.16 = (bf16[128,128]{1,0:T(8,128)(2,1)S(1)}, bf16[128,128]{1,0:T(8,128)(2,1)S(1)}, u32[]{:S(2)}, u32[]{:S(2)}) collective-permute-start(bf16[128,128]{1,0:T(8,128)(2,1)S(1)} %get-tuple-element.56), channel_id=1, source_target_pairs={{0,64},{64,0},{1,65},{65,1},{2,66},{66,2},{3,67},{67,3},{4,68},{68... | collective-permute-start | bytes 98312 | tf_op jit(solution)/shard_map/ppermute | solution.py:285
  213.6 0.9 collective-permute-done.16.theirs
  214.4 0.6 shard_map.75
  (2 shorter events, 0.0 us)
Async XLA Ops:
  0.0 59.1 %collective-permute-start.2 = (bf16[8192,128]{1,0:T(8,128)(2,1)}, bf16[8192,128]{1,0:T(8,128)(2,1)}, u32[]{:S(2)}, u32[]{:S(2)}) collective-permute-start(bf16[8192,128]{1,0:T(8,128)(2,1)} %bitcast.15), channel_id=1, source_target_pairs={{0,64},{64,0},{1,65},{65,1},{2,66},{66,2},{3,67},{67,3},{4,68},{68... | collective-permute-start | bytes 6291464 | tf_op jit(solution)/shard_map/ppermute | solution.py:233
  22.3 21.2 %all-to-all-start = ((bf16[16,128,128]{2,1,0:T(8,128)(2,1)}), bf16[16,128,128]{2,1,0:T(8,128)(2,1)S(1)}, u32[]{:S(2)}, u32[]{:S(2)}) async-start(bf16[16,128,128]{2,1,0:T(8,128)(2,1)} %get-tuple-element.34), calls=%async_computation | async-start | bytes 1048576 | tf_op jit(solution)/shard_map/all_to_all | solution.py:215
  26.4 17.7 %collective-permute-start.3 = (bf16[32,8192]{1,0:T(8,128)(2,1)}, bf16[32,8192]{1,0:T(8,128)(2,1)}, u32[]{:S(2)}, u32[]{:S(2)}) collective-permute-start(bf16[32,8192]{1,0:T(8,128)(2,1)} %bitcast.23), channel_id=1, source_target_pairs={{0,64},{64,0},{1,65},{65,1},{2,66},{66,2},{3,67},{67,3},{4,68},{68... | collective-permute-start | bytes 1572872 | tf_op jit(solution)/shard_map/ppermute | solution.py:233
  26.5 17.4 %collective-permute-start.1 = (bf16[1,8192]{1,0:T(2,128)(2,1)}, bf16[1,8192]{1,0:T(2,128)(2,1)S(1)}, u32[]{:S(2)}, u32[]{:S(2)}) collective-permute-start(bf16[1,8192]{1,0:T(2,128)(2,1)} %bitcast.25), channel_id=1, source_target_pairs={{0,64},{64,0},{1,65},{65,1},{2,66},{66,2},{3,67},{67,3},{4,68},{68... | collective-permute-start | bytes 49160 | tf_op jit(solution)/shard_map/ppermute | solution.py:234
  27.0 73.0 %collective-permute-start = (bf16[8192,128]{1,0:T(8,128)(2,1)}, bf16[8192,128]{1,0:T(8,128)(2,1)S(1)}, u32[]{:S(2)}, u32[]{:S(2)}) collective-permute-start(bf16[8192,128]{1,0:T(8,128)(2,1)} %bitcast.10), channel_id=1, source_target_pairs={{0,64},{64,0},{1,65},{65,1},{2,66},{66,2},{3,67},{67,3},{4,68},{68... | collective-permute-start | bytes 6291464 | tf_op jit(solution)/shard_map/ppermute | solution.py:233
  43.6 12.1 %collective-permute-start.6 = (bf16[16,128,128]{2,1,0:T(8,128)(2,1)S(1)}, bf16[16,128,128]{2,1,0:T(8,128)(2,1)S(1)}, u32[]{:S(2)}, u32[]{:S(2)}) collective-permute-start(bf16[16,128,128]{2,1,0:T(8,128)(2,1)S(1)} %all-to-all-done.own_set.rest_8_), channel_id=1, source_target_pairs={{1,0},{2,1},{3,2},{4,3},{5,4},{6,5},{7,6},{0,7},{9,8},{10,9},{11,1... | collective-permute-start | bytes 1572872 | tf_op jit(solution)/shard_map/ppermute | solution.py:211
  44.0 11.8 %collective-permute-start.5 = (bf16[16,128,128]{2,1,0:T(8,128)(2,1)S(1)}, bf16[16,128,128]{2,1,0:T(8,128)(2,1)S(1)}, u32[]{:S(2)}, u32[]{:S(2)}) collective-permute-start(bf16[16,128,128]{2,1,0:T(8,128)(2,1)S(1)} %all-to-all-done.own_set.rest_8_), channel_id=1, source_target_pairs={{8,0},{9,1},{10,2},{11,3},{12,4},{13,5},{14,6},{15,7},{16,8},{17,9... | collective-permute-start | bytes 1572872 | tf_op jit(solution)/shard_map/ppermute | solution.py:211
  44.1 14.9 %collective-permute-start.4 = (bf16[16,128,128]{2,1,0:T(8,128)(2,1)S(1)}, bf16[16,128,128]{2,1,0:T(8,128)(2,1)S(1)}, u32[]{:S(2)}, u32[]{:S(2)}) collective-permute-start(bf16[16,128,128]{2,1,0:T(8,128)(2,1)S(1)} %all-to-all-done.own_set.rest_8_), channel_id=1, source_target_pairs={{63,0},{56,1},{57,2},{58,3},{59,4},{60,5},{61,6},{62,7},{7,8},{0,9... | collective-permute-start | bytes 1572872 | tf_op jit(solution)/shard_map/ppermute | solution.py:211
  59.1 1.6 copy-start.1
  60.7 39.3 %copy-start = (bf16[1,1,8192,128]{3,2,1,0:T(8,128)(2,1)S(1)}, bf16[1,1,8192,128]{3,2,1,0:T(8,128)(2,1)}, u32[]{:S(2)}) copy-start(bf16[1,1,8192,128]{3,2,1,0:T(8,128)(2,1)} %param.11) | copy-start | bytes 6291460
  96.8 10.4 %collective-permute-start.9 = (bf16[16,128,128]{2,1,0:T(8,128)(2,1)S(1)}, bf16[16,128,128]{2,1,0:T(8,128)(2,1)S(1)}, u32[]{:S(2)}, u32[]{:S(2)}) collective-permute-start(bf16[16,128,128]{2,1,0:T(8,128)(2,1)S(1)} %all_to_all.31.rest_0_), channel_id=1, source_target_pairs={{1,0},{2,1},{3,2},{4,3},{5,4},{6,5},{7,6},{0,7},{9,8},{10,9},{11,1... | collective-permute-start | bytes 1572872 | tf_op jit(solution)/shard_map/ppermute | solution.py:211
  99.0 10.2 %collective-permute-start.8 = (bf16[16,128,128]{2,1,0:T(8,128)(2,1)S(1)}, bf16[16,128,128]{2,1,0:T(8,128)(2,1)S(1)}, u32[]{:S(2)}, u32[]{:S(2)}) collective-permute-start(bf16[16,128,128]{2,1,0:T(8,128)(2,1)S(1)} %all_to_all.31.rest_0_), channel_id=1, source_target_pairs={{8,0},{9,1},{10,2},{11,3},{12,4},{13,5},{14,6},{15,7},{16,8},{17,9... | collective-permute-start | bytes 1572872 | tf_op jit(solution)/shard_map/ppermute | solution.py:211
  99.0 12.2 %collective-permute-start.7 = (bf16[16,128,128]{2,1,0:T(8,128)(2,1)S(1)}, bf16[16,128,128]{2,1,0:T(8,128)(2,1)S(1)}, u32[]{:S(2)}, u32[]{:S(2)}) collective-permute-start(bf16[16,128,128]{2,1,0:T(8,128)(2,1)S(1)} %all_to_all.31.rest_0_), channel_id=1, source_target_pairs={{63,0},{56,1},{57,2},{58,3},{59,4},{60,5},{61,6},{62,7},{7,8},{0,9... | collective-permute-start | bytes 1572872 | tf_op jit(solution)/shard_map/ppermute | solution.py:211
  111.2 48.2 %copy-start.2 = (bf16[1,1,8192,128]{3,2,1,0:T(8,128)(2,1)S(1)}, bf16[1,1,8192,128]{3,2,1,0:T(8,128)(2,1)}, u32[]{:S(2)}) copy-start(bf16[1,1,8192,128]{3,2,1,0:T(8,128)(2,1)} %param.9) | copy-start | bytes 6291460
  136.2 12.1 %collective-permute-start.12 = (bf16[16,128,128]{2,1,0:T(8,128)(2,1)S(1)}, bf16[16,128,128]{2,1,0:T(8,128)(2,1)S(1)}, u32[]{:S(2)}, u32[]{:S(2)}) collective-permute-start(bf16[16,128,128]{2,1,0:T(8,128)(2,1)S(1)} %all_to_all.32.own_set.rest_8_), channel_id=1, source_target_pairs={{1,0},{2,1},{3,2},{4,3},{5,4},{6,5},{7,6},{0,7},{9,8},{10,9},{11,1... | collective-permute-start | bytes 1572872 | tf_op jit(solution)/shard_map/ppermute | solution.py:211
  140.1 14.0 %collective-permute-start.11 = (bf16[16,128,128]{2,1,0:T(8,128)(2,1)S(1)}, bf16[16,128,128]{2,1,0:T(8,128)(2,1)S(1)}, u32[]{:S(2)}, u32[]{:S(2)}) collective-permute-start(bf16[16,128,128]{2,1,0:T(8,128)(2,1)S(1)} %all_to_all.32.own_set.rest_8_), channel_id=1, source_target_pairs={{8,0},{9,1},{10,2},{11,3},{12,4},{13,5},{14,6},{15,7},{16,8},{17,9... | collective-permute-start | bytes 1572872 | tf_op jit(solution)/shard_map/ppermute | solution.py:211
  143.9 15.4 %collective-permute-start.10 = (bf16[16,128,128]{2,1,0:T(8,128)(2,1)S(1)}, bf16[16,128,128]{2,1,0:T(8,128)(2,1)S(1)}, u32[]{:S(2)}, u32[]{:S(2)}) collective-permute-start(bf16[16,128,128]{2,1,0:T(8,128)(2,1)S(1)} %all_to_all.32.own_set.rest_8_), channel_id=1, source_target_pairs={{63,0},{56,1},{57,2},{58,3},{59,4},{60,5},{61,6},{62,7},{7,8},{0,9... | collective-permute-start | bytes 1572872 | tf_op jit(solution)/shard_map/ppermute | solution.py:211
  192.5 9.9 %collective-permute-start.15 = (bf16[16,128,128]{2,1,0:T(8,128)(2,1)S(1)}, bf16[16,128,128]{2,1,0:T(8,128)(2,1)S(1)}, u32[]{:S(2)}, u32[]{:S(2)}) collective-permute-start(bf16[16,128,128]{2,1,0:T(8,128)(2,1)S(1)} %all_to_all.34.rest_0_), channel_id=1, source_target_pairs={{1,0},{2,1},{3,2},{4,3},{5,4},{6,5},{7,6},{0,7},{9,8},{10,9},{11,1... | collective-permute-start | bytes 1572872 | tf_op jit(solution)/shard_map/ppermute | solution.py:211
  192.5 9.9 %collective-permute-start.14 = (bf16[16,128,128]{2,1,0:T(8,128)(2,1)S(1)}, bf16[16,128,128]{2,1,0:T(8,128)(2,1)S(1)}, u32[]{:S(2)}, u32[]{:S(2)}) collective-permute-start(bf16[16,128,128]{2,1,0:T(8,128)(2,1)S(1)} %all_to_all.34.rest_0_), channel_id=1, source_target_pairs={{8,0},{9,1},{10,2},{11,3},{12,4},{13,5},{14,6},{15,7},{16,8},{17,9... | collective-permute-start | bytes 1572872 | tf_op jit(solution)/shard_map/ppermute | solution.py:211
  192.5 11.4 %collective-permute-start.13 = (bf16[16,128,128]{2,1,0:T(8,128)(2,1)S(1)}, bf16[16,128,128]{2,1,0:T(8,128)(2,1)S(1)}, u32[]{:S(2)}, u32[]{:S(2)}) collective-permute-start(bf16[16,128,128]{2,1,0:T(8,128)(2,1)S(1)} %all_to_all.34.rest_0_), channel_id=1, source_target_pairs={{63,0},{56,1},{57,2},{58,3},{59,4},{60,5},{61,6},{62,7},{7,8},{0,9... | collective-permute-start | bytes 1572872 | tf_op jit(solution)/shard_map/ppermute | solution.py:211
  204.5 9.9 %collective-permute-start.16 = (bf16[128,128]{1,0:T(8,128)(2,1)S(1)}, bf16[128,128]{1,0:T(8,128)(2,1)S(1)}, u32[]{:S(2)}, u32[]{:S(2)}) collective-permute-start(bf16[128,128]{1,0:T(8,128)(2,1)S(1)} %get-tuple-element.56), channel_id=1, source_target_pairs={{0,64},{64,0},{1,65},{65,1},{2,66},{66,2},{3,67},{67,3},{4,68},{68... | collective-permute-start | bytes 98312 | tf_op jit(solution)/shard_map/ppermute | solution.py:285

commit v6 on v5

--- a/solution.py
+++ b/solution.py
@@ -13,7 +13,6 @@
 X = ("x2", "x1", "x0")
 Y = ("y2", "y1", "y0")
 MESH = X + Y
-FAR = ("x2", "x1", "y2", "y1")
 SIDE = 8
 FAR_COUNT = 16
 norm_epsilon = 1e-05
@@ -41,20 +40,25 @@
     )
 
 
-STAGES = (
-    ((0, 0),),
-    ((1, 1), (1, 0), (0, 1)),
-)
+STAGES = ((0,), (1, 3, 2))
 STEP = 4
 
 
+def colour_groups(devices):
+    groups = [[] for _ in range(STEP)]
+    for place in range(devices):
+        groups[(place // SIDE + 2 * (place % SIDE)) % STEP].append(place)
+    return groups
+
+
 def for_chunks(buffers, layout, body, carry, unrolled=False):
-    px, py = lax.axis_index("x0"), lax.axis_index("y0")
-    for ref, (turn_x, turn_y) in zip(buffers, layout, strict=True):
-        base = SIDE * jnp.where(turn_x == 1, 1 - px, px) + jnp.where(turn_y == 1, 1 - py, py)
-
-        def chunk(i, carry, ref=ref, base=base):
-            place = base + 2 * SIDE * i
+    for ref, turn in zip(buffers, layout, strict=True):
+        odd, half = lax.axis_index("x0"), lax.axis_index("x1") + lax.axis_index("y0")
+        colour = odd + 2 * half + turn
+        odd, half = colour % 2, colour // 2
+
+        def chunk(i, carry, ref=ref, odd=odd, half=half):
+            place = SIDE * odd + 2 * SIDE * i + (half + i) % 2
             return body([(ref[i * STEP + k], place + 2 * k) for k in range(STEP)], carry)
 
         count = ref.shape[0] // STEP
@@ -212,14 +216,15 @@
 
 
 def far_stage(copies):
-    return lax.all_to_all(copies, FAR, 0, 0, tiled=True)
+    groups = colour_groups(lax.axis_size(MESH))
+    return lax.all_to_all(copies, MESH, 0, 0, axis_index_groups=groups, tiled=True)
 
 
 def near_stage(own):
     def hop(dx, dy):
         return from_neighbour(own, dx, dy)
 
-    return (own,), (hop(-1, -1), hop(1, 0), hop(0, 1))
+    return (own,), (hop(1, 0), hop(-1, 0), hop(0, 1))
 
 
 def shards(inputs, segments, gains, w_query, w_keyval, w_output):

time: 216 us -> 207 us (0.958)
  blocking collectives: 85.7 us -> 78.4 us
  waiting for transfers between devices: 62.7 us -> 60.2 us
    ppermute x12, starting transfers between devices: 16.4 us -> 23.9 us  [from_neighbour(): return lax.ppermute(block, MESH, pairs)]
    all_to_all x3, blocking collectives: 65.4 us -> 58.3 us  [far_stage(): lax.all_to_all(copies, MESH, 0, 0, axis_index_groups=groups, tiled=True)]
    ppermute x1, starting transfers between devices: 9.04 us -> 3.08 us  [shards(): theirs = lax.ppermute(copies, 'section', swap)]
    ppermute x12, waiting for transfers between devices: 45.4 us -> 41.8 us  [from_neighbour(): return lax.ppermute(block, MESH, pairs)]
  transfers between devices with their start and end apart: 18 -> 18, of which waited for: 12 -> 11; matrix products, arithmetic and copies ran while one was open for 0% -> 0% of each run, Pallas kernels for 4% -> 4%
where the time goes in v6:
time: 207 us
  blocking collectives  78.4 us (38%)
  waiting for transfers between devices  60.2 us (29%)
  starting transfers between devices  52.2 us (25%)
  Pallas kernels  13.6 us (7%)
    all_to_all x3, blocking collectives, far_stage(): lax.all_to_all(copies, MESH, 0, 0, axis_index_groups=groups, tiled=True)  58.3 us
    ppermute x12, waiting for transfers between devices, from_neighbour(): return lax.ppermute(block, MESH, pairs)  41.8 us
    ppermute x12, starting transfers between devices, from_neighbour(): return lax.ppermute(block, MESH, pairs)  23.9 us
    ppermute x3, starting transfers between devices, shards(): other.append(lax.ppermute(w, 'section', swap))  20.7 us
    all_to_all x2, blocking collectives, shards(): keyval = lax.all_to_all(keyval, Y, 0, 0, tiled=True).reshape(-1, rows)  20.1 us
    all_to_all x1, waiting for transfers between devices, far_stage(): lax.all_to_all(copies, MESH, 0, 0, axis_index_groups=groups, tiled=True)  17.6 us
    pallas_call x11, Pallas kernels, call(): pl.pallas_call(kernel, out_shape=outs, in_specs=[vmem] * len(args), out_s...  11.7 us
  transfers between devices with their start and end apart: 18, of which 11 were waited for; matrix products, arithmetic and copies ran while one was open for 0% of the time, Pallas kernels for 4%

profile of v6, /device:TPU:513, one launch (start us, length us, event | category | flops | bytes accessed | tf_op | source)
XLA Modules:
  0.0 206.8 jit_solution(9757249363002598958)
XLA Ops:
  0.0 20.4 %collective-permute-start.2 = (bf16[8192,128]{1,0:T(8,128)(2,1)}, bf16[8192,128]{1,0:T(8,128)(2,1)}, u32[]{:S(2)}, u32[]{:S(2)}) collective-permute-start(bf16[8192,128]{1,0:T(8,128)(2,1)} %bitcast.15), channel_id=1, source_target_pairs={{0,64},{64,0},{1,65},{65,1},{2,66},{66,2},{3,67},{67,3},{4,68},{68... | collective-permute-start | bytes 6291464 | tf_op jit(solution)/shard_map/ppermute | solution.py:238
  20.4 1.9 shard_map.64
  22.3 4.0 %all-to-all-start = ((bf16[16,128,128]{2,1,0:T(8,128)(2,1)}), bf16[16,128,128]{2,1,0:T(8,128)(2,1)S(1)}, u32[]{:S(2)}, u32[]{:S(2)}) async-start(bf16[16,128,128]{2,1,0:T(8,128)(2,1)} %get-tuple-element.34), calls=%async_computation | async-start | bytes 1048576 | tf_op jit(solution)/shard_map/all_to_all | solution.py:220
  26.4 0.1 collective-permute-start.3
  26.5 0.5 collective-permute-start.1
  27.0 0.2 collective-permute-start
  27.2 17.6 %all-to-all-done.own_set.rest_8_ = bf16[16,128,128]{2,1,0:T(8,128)(2,1)S(1)} async-done(((bf16[16,128,128]{2,1,0:T(8,128)(2,1)}), bf16[16,128,128]{2,1,0:T(8,128)(2,1)S(1)}, u32[]{:S(2)}, u32[]{:S(2)}) %all-to-all-start) | async-done | bytes 524320 | tf_op jit(solution)/shard_map/all_to_all | solution.py:220
  44.7 0.1 shard_map.65.squares
  44.8 0.1 collective-permute-start.6
  44.9 0.2 fusion
  45.1 0.0 collective-permute-done.1.rest_1_
  45.1 0.1 collective-permute-start.5
  45.3 0.0 collective-permute-done.3.rest_5_
  45.3 2.6 %collective-permute-start.4 = (bf16[16,128,128]{2,1,0:T(8,128)(2,1)S(1)}, bf16[16,128,128]{2,1,0:T(8,128)(2,1)S(1)}, u32[]{:S(2)}, u32[]{:S(2)}) collective-permute-start(bf16[16,128,128]{2,1,0:T(8,128)(2,1)S(1)} %all-to-all-done.own_set.rest_8_), channel_id=1, source_target_pairs={{8,0},{9,1},{10,2},{11,3},{12,4},{13,5},{14,6},{15,7},{16,8},{17,9... | collective-permute-start | bytes 1572872 | tf_op jit(solution)/shard_map/ppermute | solution.py:215
  47.9 0.3 fusion.2
  48.2 0.1 pad_maximum_fusion
  48.4 0.1 fusion.1.allowed
  48.4 9.0 %collective-permute-done.6.rest_11_ = bf16[16,128,128]{2,1,0:T(8,128)(2,1)S(1)} collective-permute-done((bf16[16,128,128]{2,1,0:T(8,128)(2,1)S(1)}, bf16[16,128,128]{2,1,0:T(8,128)(2,1)S(1)}, u32[]{:S(2)}, u32[]{:S(2)}) %collective-permute-start.6) | collective-permute-done | bytes 524320 | tf_op jit(solution)/shard_map/ppermute | solution.py:215
  57.4 1.6 collective-permute-done.5.rest_10_
  59.0 0.0 collective-permute-done.4.rest_9_
  59.0 0.0 collective-permute-done.2.rest_3_
  59.0 0.0 copy-start.1
  59.0 1.6 copy-done.1
  60.6 0.0 copy-start
  60.6 3.6 %shard_map.66 = (bf16[128,128]{1,0:T(8,128)(2,1)S(1)}, bf16[8,32,128]{2,1,0:T(8,128)(2,1)S(1)}) custom-call(f32[128,128]{1,0:T(8,128)S(1)} %shard_map.65.squares, bf16[1,8192]{1,0:T(2,128)(2,1)S(1)} %get-tuple-element.40.rest_0_, bf16[1,8192]{1,0:T(2,128)(2,1)S(1)} %collective-permute-done.1.rest_1_, bf16[8192,128]{1,0:T(8,128)(2,1)S(1)} %bitcast.16, ...), custom_call_target="tpu_custom_call" | custom-call | tf_op jit(solution)/shard_map/pallas_call | solution.py:200
  64.2 9.9 %all_to_all.30 = bf16[8,32,128]{2,1,0:T(8,128)(2,1)S(1)} all-to-all(bf16[8,32,128]{2,1,0:T(8,128)(2,1)S(1)} %get-tuple-element.45), channel_id=1, replica_groups=mesh['groups'=2,'section'=2,'x2'=2,'x1'=2,'x0'=2,'y2'=2,'y1'=2,'y0'=2] {..., dimensions={0} | all-to-all | bytes 131072 | tf_op jit(solution)/shard_map/all_to_all | solution.py:275
  74.1 0.5 shard_map.67
  74.6 20.6 %all_to_all.31.rest_0_ = bf16[16,128,128]{2,1,0:T(8,128)(2,1)S(1)} all-to-all(bf16[16,128,128]{2,1,0:T(8,128)(2,1)S(1)} %shard_map.67), channel_id=1, replica_groups={{0,2,4,6,17,19,21,23,32,34,36,38,49,51,53,55},{8,10,12,14,25,27,29,31,4..., dimensions={0} | all-to-all | bytes 1048576 | tf_op jit(solution)/shard_map/all_to_all | solution.py:220
  95.3 3.1 %collective-permute-start.9 = (bf16[16,128,128]{2,1,0:T(8,128)(2,1)S(1)}, bf16[16,128,128]{2,1,0:T(8,128)(2,1)S(1)}, u32[]{:S(2)}, u32[]{:S(2)}) collective-permute-start(bf16[16,128,128]{2,1,0:T(8,128)(2,1)S(1)} %all_to_all.31.rest_0_), channel_id=1, source_target_pairs={{1,0},{2,1},{3,2},{4,3},{5,4},{6,5},{7,6},{0,7},{9,8},{10,9},{11,1... | collective-permute-start | bytes 1572872 | tf_op jit(solution)/shard_map/ppermute | solution.py:215
  98.3 0.0 collective-permute-start.8
  98.3 2.7 %collective-permute-start.7 = (bf16[16,128,128]{2,1,0:T(8,128)(2,1)S(1)}, bf16[16,128,128]{2,1,0:T(8,128)(2,1)S(1)}, u32[]{:S(2)}, u32[]{:S(2)}) collective-permute-start(bf16[16,128,128]{2,1,0:T(8,128)(2,1)S(1)} %all_to_all.31.rest_0_), channel_id=1, source_target_pairs={{8,0},{9,1},{10,2},{11,3},{12,4},{13,5},{14,6},{15,7},{16,8},{17,9... | collective-permute-start | bytes 1572872 | tf_op jit(solution)/shard_map/ppermute | solution.py:215
  101.0 0.0 collective-permute-done.other
  101.0 0.0 copy-done
  101.0 0.8 shard_map.68.before
  101.8 5.8 %collective-permute-done.9.rest_2_ = bf16[16,128,128]{2,1,0:T(8,128)(2,1)S(1)} collective-permute-done((bf16[16,128,128]{2,1,0:T(8,128)(2,1)S(1)}, bf16[16,128,128]{2,1,0:T(8,128)(2,1)S(1)}, u32[]{:S(2)}, u32[]{:S(2)}) %collective-permute-start.9) | collective-permute-done | bytes 524320 | tf_op jit(solution)/shard_map/ppermute | solution.py:215
  107.6 3.1 %collective-permute-done.8.rest_1_ = bf16[16,128,128]{2,1,0:T(8,128)(2,1)S(1)} collective-permute-done((bf16[16,128,128]{2,1,0:T(8,128)(2,1)S(1)}, bf16[16,128,128]{2,1,0:T(8,128)(2,1)S(1)}, u32[]{:S(2)}, u32[]{:S(2)}) %collective-permute-start.8) | collective-permute-done | bytes 524320 | tf_op jit(solution)/shard_map/ppermute | solution.py:215
  110.7 2.0 collective-permute-done.7.rest_0_
  112.7 0.0 copy-start.2
  112.7 0.6 shard_map.69
  113.4 20.5 %all_to_all.32.own_set.rest_8_ = bf16[16,128,128]{2,1,0:T(8,128)(2,1)S(1)} all-to-all(bf16[16,128,128]{2,1,0:T(8,128)(2,1)S(1)} %get-tuple-element.48), channel_id=1, replica_groups={{0,2,4,6,17,19,21,23,32,34,36,38,49,51,53,55},{8,10,12,14,25,27,29,31,4..., dimensions={0} | all-to-all | bytes 1048576 | tf_op jit(solution)/shard_map/all_to_all | solution.py:220
  133.8 4.3 %collective-permute-start.12 = (bf16[16,128,128]{2,1,0:T(8,128)(2,1)S(1)}, bf16[16,128,128]{2,1,0:T(8,128)(2,1)S(1)}, u32[]{:S(2)}, u32[]{:S(2)}) collective-permute-start(bf16[16,128,128]{2,1,0:T(8,128)(2,1)S(1)} %all_to_all.32.own_set.rest_8_), channel_id=1, source_target_pairs={{1,0},{2,1},{3,2},{4,3},{5,4},{6,5},{7,6},{0,7},{9,8},{10,9},{11,1... | collective-permute-start | bytes 1572872 | tf_op jit(solution)/shard_map/ppermute | solution.py:215
  138.1 0.0 collective-permute-start.11
  138.1 2.7 %collective-permute-start.10 = (bf16[16,128,128]{2,1,0:T(8,128)(2,1)S(1)}, bf16[16,128,128]{2,1,0:T(8,128)(2,1)S(1)}, u32[]{:S(2)}, u32[]{:S(2)}) collective-permute-start(bf16[16,128,128]{2,1,0:T(8,128)(2,1)S(1)} %all_to_all.32.own_set.rest_8_), channel_id=1, source_target_pairs={{8,0},{9,1},{10,2},{11,3},{12,4},{13,5},{14,6},{15,7},{16,8},{17,9... | collective-permute-start | bytes 1572872 | tf_op jit(solution)/shard_map/ppermute | solution.py:215
  140.8 0.1 shard_map.70.squares
  140.9 7.2 %collective-permute-done.12.rest_11_ = bf16[16,128,128]{2,1,0:T(8,128)(2,1)S(1)} collective-permute-done((bf16[16,128,128]{2,1,0:T(8,128)(2,1)S(1)}, bf16[16,128,128]{2,1,0:T(8,128)(2,1)S(1)}, u32[]{:S(2)}, u32[]{:S(2)}) %collective-permute-start.12) | collective-permute-done | bytes 524320 | tf_op jit(solution)/shard_map/ppermute | solution.py:215
  148.1 3.1 %collective-permute-done.11.rest_10_ = bf16[16,128,128]{2,1,0:T(8,128)(2,1)S(1)} collective-permute-done((bf16[16,128,128]{2,1,0:T(8,128)(2,1)S(1)}, bf16[16,128,128]{2,1,0:T(8,128)(2,1)S(1)}, u32[]{:S(2)}, u32[]{:S(2)}) %collective-permute-start.11) | collective-permute-done | bytes 524320 | tf_op jit(solution)/shard_map/ppermute | solution.py:215
  151.2 0.8 collective-permute-done.10.rest_9_
  152.1 0.0 copy-done.2
  152.1 3.4 %shard_map.71 = (bf16[128,128]{1,0:T(8,128)(2,1)S(1)}, bf16[8,32,128]{2,1,0:T(8,128)(2,1)S(1)}) custom-call(f32[128,128]{1,0:T(8,128)S(1)} %shard_map.70.squares, bf16[1,8192]{1,0:T(2,128)(2,1)S(1)} %get-tuple-element.40.rest_0_, bf16[1,8192]{1,0:T(2,128)(2,1)S(1)} %collective-permute-done.1.rest_1_, bf16[8192,128]{1,0:T(8,128)(2,1)S(1)} %bitcast.17, ...), custom_call_target="tpu_custom_call" | custom-call | tf_op jit(solution)/shard_map/pallas_call | solution.py:200
  155.5 10.2 %all_to_all.33 = bf16[8,32,128]{2,1,0:T(8,128)(2,1)S(1)} all-to-all(bf16[8,32,128]{2,1,0:T(8,128)(2,1)S(1)} %get-tuple-element.53), channel_id=1, replica_groups=mesh['groups'=2,'section'=2,'x2'=2,'x1'=2,'x0'=2,'y2'=2,'y1'=2,'y0'=2] {..., dimensions={0} | all-to-all | bytes 131072 | tf_op jit(solution)/shard_map/all_to_all | solution.py:275
  165.7 0.5 shard_map.72
  166.2 17.2 %all_to_all.34.rest_0_ = bf16[16,128,128]{2,1,0:T(8,128)(2,1)S(1)} all-to-all(bf16[16,128,128]{2,1,0:T(8,128)(2,1)S(1)} %shard_map.72), channel_id=1, replica_groups={{0,2,4,6,17,19,21,23,32,34,36,38,49,51,53,55},{8,10,12,14,25,27,29,31,4..., dimensions={0} | all-to-all | bytes 1048576 | tf_op jit(solution)/shard_map/all_to_all | solution.py:220
  183.4 2.0 collective-permute-start.15
  185.4 4.7 %collective-permute-start.14 = (bf16[16,128,128]{2,1,0:T(8,128)(2,1)S(1)}, bf16[16,128,128]{2,1,0:T(8,128)(2,1)S(1)}, u32[]{:S(2)}, u32[]{:S(2)}) collective-permute-start(bf16[16,128,128]{2,1,0:T(8,128)(2,1)S(1)} %all_to_all.34.rest_0_), channel_id=1, source_target_pairs={{56,0},{57,1},{58,2},{59,3},{60,4},{61,5},{62,6},{63,7},{0,8},{1,9... | collective-permute-start | bytes 1572872 | tf_op jit(solution)/shard_map/ppermute | solution.py:215
  190.1 1.5 collective-permute-start.13
  191.7 0.8 shard_map.73.before
  192.4 0.0 collective-permute-done.15.rest_3_
  192.5 9.1 %collective-permute-done.14.rest_2_ = bf16[16,128,128]{2,1,0:T(8,128)(2,1)S(1)} collective-permute-done((bf16[16,128,128]{2,1,0:T(8,128)(2,1)S(1)}, bf16[16,128,128]{2,1,0:T(8,128)(2,1)S(1)}, u32[]{:S(2)}, u32[]{:S(2)}) %collective-permute-start.14) | collective-permute-done | bytes 524320 | tf_op jit(solution)/shard_map/ppermute | solution.py:215
  201.6 0.0 collective-permute-done.13.rest_1_
  201.6 0.6 shard_map.74
  202.2 3.1 %collective-permute-start.16 = (bf16[128,128]{1,0:T(8,128)(2,1)S(1)}, bf16[128,128]{1,0:T(8,128)(2,1)S(1)}, u32[]{:S(2)}, u32[]{:S(2)}) collective-permute-start(bf16[128,128]{1,0:T(8,128)(2,1)S(1)} %get-tuple-element.56), channel_id=1, source_target_pairs={{0,64},{64,0},{1,65},{65,1},{2,66},{66,2},{3,67},{67,3},{4,68},{68... | collective-permute-start | bytes 98312 | tf_op jit(solution)/shard_map/ppermute | solution.py:290
  205.3 0.9 collective-permute-done.16.theirs
  206.2 0.6 shard_map.75
  (2 shorter events, 0.0 us)
Async XLA Ops:
  0.0 59.0 %collective-permute-start.2 = (bf16[8192,128]{1,0:T(8,128)(2,1)}, bf16[8192,128]{1,0:T(8,128)(2,1)}, u32[]{:S(2)}, u32[]{:S(2)}) collective-permute-start(bf16[8192,128]{1,0:T(8,128)(2,1)} %bitcast.15), channel_id=1, source_target_pairs={{0,64},{64,0},{1,65},{65,1},{2,66},{66,2},{3,67},{67,3},{4,68},{68... | collective-permute-start | bytes 6291464 | tf_op jit(solution)/shard_map/ppermute | solution.py:238
  22.3 22.4 %all-to-all-start = ((bf16[16,128,128]{2,1,0:T(8,128)(2,1)}), bf16[16,128,128]{2,1,0:T(8,128)(2,1)S(1)}, u32[]{:S(2)}, u32[]{:S(2)}) async-start(bf16[16,128,128]{2,1,0:T(8,128)(2,1)} %get-tuple-element.34), calls=%async_computation | async-start | bytes 1048576 | tf_op jit(solution)/shard_map/all_to_all | solution.py:220
  26.4 18.9 %collective-permute-start.3 = (bf16[32,8192]{1,0:T(8,128)(2,1)}, bf16[32,8192]{1,0:T(8,128)(2,1)}, u32[]{:S(2)}, u32[]{:S(2)}) collective-permute-start(bf16[32,8192]{1,0:T(8,128)(2,1)} %bitcast.23), channel_id=1, source_target_pairs={{0,64},{64,0},{1,65},{65,1},{2,66},{66,2},{3,67},{67,3},{4,68},{68... | collective-permute-start | bytes 1572872 | tf_op jit(solution)/shard_map/ppermute | solution.py:238
  26.5 18.6 %collective-permute-start.1 = (bf16[1,8192]{1,0:T(2,128)(2,1)}, bf16[1,8192]{1,0:T(2,128)(2,1)S(1)}, u32[]{:S(2)}, u32[]{:S(2)}) collective-permute-start(bf16[1,8192]{1,0:T(2,128)(2,1)} %bitcast.25), channel_id=1, source_target_pairs={{0,64},{64,0},{1,65},{65,1},{2,66},{66,2},{3,67},{67,3},{4,68},{68... | collective-permute-start | bytes 49160 | tf_op jit(solution)/shard_map/ppermute | solution.py:239
  27.0 74.0 %collective-permute-start = (bf16[8192,128]{1,0:T(8,128)(2,1)}, bf16[8192,128]{1,0:T(8,128)(2,1)S(1)}, u32[]{:S(2)}, u32[]{:S(2)}) collective-permute-start(bf16[8192,128]{1,0:T(8,128)(2,1)} %bitcast.10), channel_id=1, source_target_pairs={{0,64},{64,0},{1,65},{65,1},{2,66},{66,2},{3,67},{67,3},{4,68},{68... | collective-permute-start | bytes 6291464 | tf_op jit(solution)/shard_map/ppermute | solution.py:238
  44.8 12.6 %collective-permute-start.6 = (bf16[16,128,128]{2,1,0:T(8,128)(2,1)S(1)}, bf16[16,128,128]{2,1,0:T(8,128)(2,1)S(1)}, u32[]{:S(2)}, u32[]{:S(2)}) collective-permute-start(bf16[16,128,128]{2,1,0:T(8,128)(2,1)S(1)} %all-to-all-done.own_set.rest_8_), channel_id=1, source_target_pairs={{1,0},{2,1},{3,2},{4,3},{5,4},{6,5},{7,6},{0,7},{9,8},{10,9},{11,1... | collective-permute-start | bytes 1572872 | tf_op jit(solution)/shard_map/ppermute | solution.py:215
  45.1 13.9 %collective-permute-start.5 = (bf16[16,128,128]{2,1,0:T(8,128)(2,1)S(1)}, bf16[16,128,128]{2,1,0:T(8,128)(2,1)S(1)}, u32[]{:S(2)}, u32[]{:S(2)}) collective-permute-start(bf16[16,128,128]{2,1,0:T(8,128)(2,1)S(1)} %all-to-all-done.own_set.rest_8_), channel_id=1, source_target_pairs={{56,0},{57,1},{58,2},{59,3},{60,4},{61,5},{62,6},{63,7},{0,8},{1,9... | collective-permute-start | bytes 1572872 | tf_op jit(solution)/shard_map/ppermute | solution.py:215
  45.3 13.7 %collective-permute-start.4 = (bf16[16,128,128]{2,1,0:T(8,128)(2,1)S(1)}, bf16[16,128,128]{2,1,0:T(8,128)(2,1)S(1)}, u32[]{:S(2)}, u32[]{:S(2)}) collective-permute-start(bf16[16,128,128]{2,1,0:T(8,128)(2,1)S(1)} %all-to-all-done.own_set.rest_8_), channel_id=1, source_target_pairs={{8,0},{9,1},{10,2},{11,3},{12,4},{13,5},{14,6},{15,7},{16,8},{17,9... | collective-permute-start | bytes 1572872 | tf_op jit(solution)/shard_map/ppermute | solution.py:215
  59.0 1.6 copy-start.1
  60.6 40.4 %copy-start = (bf16[1,1,8192,128]{3,2,1,0:T(8,128)(2,1)S(1)}, bf16[1,1,8192,128]{3,2,1,0:T(8,128)(2,1)}, u32[]{:S(2)}) copy-start(bf16[1,1,8192,128]{3,2,1,0:T(8,128)(2,1)} %param.11) | copy-start | bytes 6291460
  95.3 12.3 %collective-permute-start.9 = (bf16[16,128,128]{2,1,0:T(8,128)(2,1)S(1)}, bf16[16,128,128]{2,1,0:T(8,128)(2,1)S(1)}, u32[]{:S(2)}, u32[]{:S(2)}) collective-permute-start(bf16[16,128,128]{2,1,0:T(8,128)(2,1)S(1)} %all_to_all.31.rest_0_), channel_id=1, source_target_pairs={{1,0},{2,1},{3,2},{4,3},{5,4},{6,5},{7,6},{0,7},{9,8},{10,9},{11,1... | collective-permute-start | bytes 1572872 | tf_op jit(solution)/shard_map/ppermute | solution.py:215
  98.3 12.4 %collective-permute-start.8 = (bf16[16,128,128]{2,1,0:T(8,128)(2,1)S(1)}, bf16[16,128,128]{2,1,0:T(8,128)(2,1)S(1)}, u32[]{:S(2)}, u32[]{:S(2)}) collective-permute-start(bf16[16,128,128]{2,1,0:T(8,128)(2,1)S(1)} %all_to_all.31.rest_0_), channel_id=1, source_target_pairs={{56,0},{57,1},{58,2},{59,3},{60,4},{61,5},{62,6},{63,7},{0,8},{1,9... | collective-permute-start | bytes 1572872 | tf_op jit(solution)/shard_map/ppermute | solution.py:215
  98.3 14.4 %collective-permute-start.7 = (bf16[16,128,128]{2,1,0:T(8,128)(2,1)S(1)}, bf16[16,128,128]{2,1,0:T(8,128)(2,1)S(1)}, u32[]{:S(2)}, u32[]{:S(2)}) collective-permute-start(bf16[16,128,128]{2,1,0:T(8,128)(2,1)S(1)} %all_to_all.31.rest_0_), channel_id=1, source_target_pairs={{8,0},{9,1},{10,2},{11,3},{12,4},{13,5},{14,6},{15,7},{16,8},{17,9... | collective-permute-start | bytes 1572872 | tf_op jit(solution)/shard_map/ppermute | solution.py:215
  112.7 39.4 %copy-start.2 = (bf16[1,1,8192,128]{3,2,1,0:T(8,128)(2,1)S(1)}, bf16[1,1,8192,128]{3,2,1,0:T(8,128)(2,1)}, u32[]{:S(2)}) copy-start(bf16[1,1,8192,128]{3,2,1,0:T(8,128)(2,1)} %param.9) | copy-start | bytes 6291460
  133.8 14.3 %collective-permute-start.12 = (bf16[16,128,128]{2,1,0:T(8,128)(2,1)S(1)}, bf16[16,128,128]{2,1,0:T(8,128)(2,1)S(1)}, u32[]{:S(2)}, u32[]{:S(2)}) collective-permute-start(bf16[16,128,128]{2,1,0:T(8,128)(2,1)S(1)} %all_to_all.32.own_set.rest_8_), channel_id=1, source_target_pairs={{1,0},{2,1},{3,2},{4,3},{5,4},{6,5},{7,6},{0,7},{9,8},{10,9},{11,1... | collective-permute-start | bytes 1572872 | tf_op jit(solution)/shard_map/ppermute | solution.py:215
  138.1 13.1 %collective-permute-start.11 = (bf16[16,128,128]{2,1,0:T(8,128)(2,1)S(1)}, bf16[16,128,128]{2,1,0:T(8,128)(2,1)S(1)}, u32[]{:S(2)}, u32[]{:S(2)}) collective-permute-start(bf16[16,128,128]{2,1,0:T(8,128)(2,1)S(1)} %all_to_all.32.own_set.rest_8_), channel_id=1, source_target_pairs={{56,0},{57,1},{58,2},{59,3},{60,4},{61,5},{62,6},{63,7},{0,8},{1,9... | collective-permute-start | bytes 1572872 | tf_op jit(solution)/shard_map/ppermute | solution.py:215
  138.1 13.9 %collective-permute-start.10 = (bf16[16,128,128]{2,1,0:T(8,128)(2,1)S(1)}, bf16[16,128,128]{2,1,0:T(8,128)(2,1)S(1)}, u32[]{:S(2)}, u32[]{:S(2)}) collective-permute-start(bf16[16,128,128]{2,1,0:T(8,128)(2,1)S(1)} %all_to_all.32.own_set.rest_8_), channel_id=1, source_target_pairs={{8,0},{9,1},{10,2},{11,3},{12,4},{13,5},{14,6},{15,7},{16,8},{17,9... | collective-permute-start | bytes 1572872 | tf_op jit(solution)/shard_map/ppermute | solution.py:215
  183.4 9.0 %collective-permute-start.15 = (bf16[16,128,128]{2,1,0:T(8,128)(2,1)S(1)}, bf16[16,128,128]{2,1,0:T(8,128)(2,1)S(1)}, u32[]{:S(2)}, u32[]{:S(2)}) collective-permute-start(bf16[16,128,128]{2,1,0:T(8,128)(2,1)S(1)} %all_to_all.34.rest_0_), channel_id=1, source_target_pairs={{1,0},{2,1},{3,2},{4,3},{5,4},{6,5},{7,6},{0,7},{9,8},{10,9},{11,1... | collective-permute-start | bytes 1572872 | tf_op jit(solution)/shard_map/ppermute | solution.py:215
  185.4 16.2 %collective-permute-start.14 = (bf16[16,128,128]{2,1,0:T(8,128)(2,1)S(1)}, bf16[16,128,128]{2,1,0:T(8,128)(2,1)S(1)}, u32[]{:S(2)}, u32[]{:S(2)}) collective-permute-start(bf16[16,128,128]{2,1,0:T(8,128)(2,1)S(1)} %all_to_all.34.rest_0_), channel_id=1, source_target_pairs={{56,0},{57,1},{58,2},{59,3},{60,4},{61,5},{62,6},{63,7},{0,8},{1,9... | collective-permute-start | bytes 1572872 | tf_op jit(solution)/shard_map/ppermute | solution.py:215
  190.1 11.5 %collective-permute-start.13 = (bf16[16,128,128]{2,1,0:T(8,128)(2,1)S(1)}, bf16[16,128,128]{2,1,0:T(8,128)(2,1)S(1)}, u32[]{:S(2)}, u32[]{:S(2)}) collective-permute-start(bf16[16,128,128]{2,1,0:T(8,128)(2,1)S(1)} %all_to_all.34.rest_0_), channel_id=1, source_target_pairs={{8,0},{9,1},{10,2},{11,3},{12,4},{13,5},{14,6},{15,7},{16,8},{17,9... | collective-permute-start | bytes 1572872 | tf_op jit(solution)/shard_map/ppermute | solution.py:215
  202.2 3.9 %collective-permute-start.16 = (bf16[128,128]{1,0:T(8,128)(2,1)S(1)}, bf16[128,128]{1,0:T(8,128)(2,1)S(1)}, u32[]{:S(2)}, u32[]{:S(2)}) collective-permute-start(bf16[128,128]{1,0:T(8,128)(2,1)S(1)} %get-tuple-element.56), channel_id=1, source_target_pairs={{0,64},{64,0},{1,65},{65,1},{2,66},{66,2},{3,67},{67,3},{4,68},{68... | collective-permute-start | bytes 98312 | tf_op jit(solution)/shard_map/ppermute | solution.py:290

commit v7 on v6

--- a/solution.py
+++ b/solution.py
@@ -40,26 +40,36 @@
     )
 
 
-STAGES = ((0,), (1, 3, 2))
+STAGES = (((0, 0),), ((1, 0), (3, 0), (2, 0), (2, 2)))
 STEP = 4
 
 
-def colour_groups(devices):
-    groups = [[] for _ in range(STEP)]
-    for place in range(devices):
-        groups[(place // SIDE + 2 * (place % SIDE)) % STEP].append(place)
+def colour_groups(sections):
+    groups = []
+    for section in range(sections):
+        one = [[] for _ in range(STEP)]
+        for first in range(SIDE):
+            for second in range(SIDE):
+                x, y = (first, second) if section == 0 else (second, first)
+                one[(first + 2 * second) % STEP].append((section * SIDE + x) * SIDE + y)
+        groups += one
     return groups
 
 
 def for_chunks(buffers, layout, body, carry, unrolled=False):
-    for ref, turn in zip(buffers, layout, strict=True):
-        odd, half = lax.axis_index("x0"), lax.axis_index("x1") + lax.axis_index("y0")
-        colour = odd + 2 * half + turn
+    swapped = lax.axis_index("section") != 0
+    x0, x1, y0, y1 = (lax.axis_index(name) for name in ("x0", "x1", "y0", "y1"))
+    own_odd = jnp.where(swapped, y0, x0)
+    own_half = jnp.where(swapped, y1 + x0, x1 + y0)
+    stride, side = jnp.where(swapped, 1, SIDE), jnp.where(swapped, SIDE, 1)
+    for ref, (turn, skip) in zip(buffers, layout, strict=True):
+        colour = own_odd + 2 * own_half + turn
         odd, half = colour % 2, colour // 2
 
-        def chunk(i, carry, ref=ref, odd=odd, half=half):
-            place = SIDE * odd + 2 * SIDE * i + (half + i) % 2
-            return body([(ref[i * STEP + k], place + 2 * k) for k in range(STEP)], carry)
+        def chunk(i, carry, ref=ref, odd=odd, half=half, skip=skip):
+            line = i + skip
+            place = stride * (odd + 2 * line) + side * ((half + line) % 2)
+            return body([(ref[i * STEP + k], place + side * 2 * k) for k in range(STEP)], carry)
 
         count = ref.shape[0] // STEP
         if unrolled:
@@ -206,25 +216,28 @@
     )(*args)
 
 
-def from_neighbour(block, dx, dy):
+def from_neighbour(block, first, second):
     pairs = []
-    for x in range(SIDE):
-        for y in range(SIDE):
-            there = (x + dx) % SIDE * SIDE + (y + dy) % SIDE
-            pairs.append((there, x * SIDE + y))
-    return lax.ppermute(block, MESH, pairs)
+    for section in range(lax.axis_size("section")):
+        dx, dy = (first, second) if section == 0 else (second, first)
+        for x in range(SIDE):
+            for y in range(SIDE):
+                there = (x + dx) % SIDE * SIDE + (y + dy) % SIDE
+                base = section * SIDE * SIDE
+                pairs.append((base + there, base + x * SIDE + y))
+    return lax.ppermute(block, ("section",) + MESH, pairs)
 
 
 def far_stage(copies):
-    groups = colour_groups(lax.axis_size(MESH))
-    return lax.all_to_all(copies, MESH, 0, 0, axis_index_groups=groups, tiled=True)
+    groups = colour_groups(lax.axis_size("section"))
+    axes = ("section",) + MESH
+    return lax.all_to_all(copies, axes, 0, 0, axis_index_groups=groups, tiled=True)
 
 
 def near_stage(own):
-    def hop(dx, dy):
-        return from_neighbour(own, dx, dy)
-
-    return (own,), (hop(1, 0), hop(-1, 0), hop(0, 1))
+    half = own.shape[0] // 2
+    sets = from_neighbour(own, 1, 0), from_neighbour(own, -1, 0)
+    return (own,), sets + (from_neighbour(own[:half], 0, 1), from_neighbour(own[half:], 0, -1))
 
 
 def shards(inputs, segments, gains, w_query, w_keyval, w_output):

time: 207 us -> 189 us (0.913)
  waiting for transfers between devices: 60.2 us -> 31.3 us
  starting transfers between devices: 52.2 us -> 61.7 us
  blocking collectives: 78.4 us -> 80.6 us
    ppermute x12 -> x16, waiting for transfers between devices: 41.8 us -> 23.1 us  [from_neighbour(): return lax.ppermute(block, ('section',) + MESH, pairs)]
    all_to_all x1, starting transfers between devices: 4.02 us -> 18.3 us  [far_stage(): lax.all_to_all(copies, axes, 0, 0, axis_index_groups=groups, tiled=True)]
    ppermute x3, starting transfers between devices: 20.7 us -> 6.73 us  [shards(): other.append(lax.ppermute(w, 'section', swap))]
    all_to_all x1, waiting for transfers between devices: 17.6 us -> 7.29 us  [far_stage(): lax.all_to_all(copies, axes, 0, 0, axis_index_groups=groups, tiled=True)]
    ppermute x1, starting transfers between devices: 3.08 us -> 9.95 us  [shards(): theirs = lax.ppermute(copies, 'section', swap)]
    all_to_all x2, blocking collectives: 20.1 us -> 24.5 us  [shards(): keyval = lax.all_to_all(keyval, Y, 0, 0, tiled=True).reshape(-1, rows)]
    ppermute x12 -> x16, starting transfers between devices: 23.9 us -> 26.6 us  [from_neighbour(): return lax.ppermute(block, ('section',) + MESH, pairs)]
    all_to_all x3, blocking collectives: 58.3 us -> 56 us  [far_stage(): lax.all_to_all(copies, axes, 0, 0, axis_index_groups=groups, tiled=True)]
  transfers between devices with their start and end apart: 18 -> 22, of which waited for: 11 -> 11; matrix products, arithmetic and copies ran while one was open for 0% -> 0% of each run, Pallas kernels for 4% -> 3%
where the time goes in v7:
time: 189 us; the launch traced here: 188 us
  blocking collectives  80.6 us (43%)
  starting transfers between devices  61.7 us (33%)
  waiting for transfers between devices  31.3 us (17%)
  Pallas kernels  13.5 us (7%)
    all_to_all x3, blocking collectives, far_stage(): lax.all_to_all(copies, axes, 0, 0, axis_index_groups=groups, tiled=True)  56 us
    ppermute x16, starting transfers between devices, from_neighbour(): return lax.ppermute(block, ('section',) + MESH, pairs)  26.6 us
    all_to_all x2, blocking collectives, shards(): keyval = lax.all_to_all(keyval, Y, 0, 0, tiled=True).reshape(-1, rows)  24.5 us
    ppermute x16, waiting for transfers between devices, from_neighbour(): return lax.ppermute(block, ('section',) + MESH, pairs)  23.1 us
    all_to_all x1, starting transfers between devices, far_stage(): lax.all_to_all(copies, axes, 0, 0, axis_index_groups=groups, tiled=True)  18.3 us
    pallas_call x11, Pallas kernels, call(): pl.pallas_call(kernel, out_shape=outs, in_specs=[vmem] * len(args), out_s...  11.6 us
    ppermute x1, starting transfers between devices, shards(): theirs = lax.ppermute(copies, 'section', swap)  9.95 us
    all_to_all x1, waiting for transfers between devices, far_stage(): lax.all_to_all(copies, axes, 0, 0, axis_index_groups=groups, tiled=True)  7.29 us
  transfers between devices with their start and end apart: 22, of which 11 were waited for; matrix products, arithmetic and copies ran while one was open for 0% of the time, Pallas kernels for 3%

profile of v7, /device:TPU:513, one launch (start us, length us, event | category | flops | bytes accessed | tf_op | source)
XLA Modules:
  0.0 188.1 jit_solution(10521203300037688665)
XLA Ops:
  0.0 1.9 %shard_map.64 = (bf16[128,128]{1,0:T(8,128)(2,1)S(1)}, bf16[16,128,128]{2,1,0:T(8,128)(2,1)}, s32[1,128]{1,0:T(1,128)S(1)}, bf16[32,8192]{1,0:T(8,128)(2,1)S(1)}, bf16[1,8192]{1,0:T(2,128)(2,1)S(1)}) custom-call(bf16[2,128,128]{2,1,0:T(8,128)(2,1)} %inputs.1, s32[2,128]{1,0:T(2,128)} %segments.1, bf16[32,8192]{1,0:T(8,128)(2,1)} %bitcast.22, ...), custom_call_target="tpu_custom_call" | custom-call | tf_op jit(solution)/shard_map/pallas_call | solution.py:261
  1.9 18.3 %all-to-all-start = ((bf16[16,128,128]{2,1,0:T(8,128)(2,1)}), bf16[16,128,128]{2,1,0:T(8,128)(2,1)S(1)}, u32[]{:S(2)}, u32[]{:S(2)}) async-start(bf16[16,128,128]{2,1,0:T(8,128)(2,1)} %get-tuple-element.34), calls=%async_computation | async-start | bytes 1048576 | tf_op jit(solution)/shard_map/all_to_all | solution.py:234
  20.3 6.2 %collective-permute-start.2 = (bf16[8192,128]{1,0:T(8,128)(2,1)}, bf16[8192,128]{1,0:T(8,128)(2,1)}, u32[]{:S(2)}, u32[]{:S(2)}) collective-permute-start(bf16[8192,128]{1,0:T(8,128)(2,1)} %bitcast.15), channel_id=1, source_target_pairs={{0,64},{64,0},{1,65},{65,1},{2,66},{66,2},{3,67},{67,3},{4,68},{68... | collective-permute-start | bytes 6291464 | tf_op jit(solution)/shard_map/ppermute | solution.py:251
  26.5 0.2 collective-permute-start.1
  26.7 0.4 collective-permute-start.3
  27.0 0.2 collective-permute-start
  27.2 7.3 %all-to-all-done.own_set.rest_8_ = bf16[16,128,128]{2,1,0:T(8,128)(2,1)S(1)} async-done(((bf16[16,128,128]{2,1,0:T(8,128)(2,1)}), bf16[16,128,128]{2,1,0:T(8,128)(2,1)S(1)}, u32[]{:S(2)}, u32[]{:S(2)}) %all-to-all-start) | async-done | bytes 524320 | tf_op jit(solution)/shard_map/all_to_all | solution.py:234
  34.5 2.7 %collective-permute-start.7 = (bf16[8,128,128]{2,1,0:T(8,128)(2,1)S(1)}, bf16[8,128,128]{2,1,0:T(8,128)(2,1)S(1)}, u32[]{:S(2)}, u32[]{:S(2)}) collective-permute-start(bf16[8,128,128]{2,1,0:T(8,128)(2,1)S(1)} %get-tuple-element.63), channel_id=1, source_target_pairs={{7,0},{0,1},{1,2},{2,3},{3,4},{4,5},{5,6},{6,7},{15,8},{8,9},{9,10... | collective-permute-start | bytes 786440 | tf_op jit(solution)/shard_map/ppermute | solution.py:228
  37.2 0.2 fusion
  37.4 0.0 collective-permute-done.1.rest_1_
  37.4 5.2 %collective-permute-start.5 = (bf16[16,128,128]{2,1,0:T(8,128)(2,1)S(1)}, bf16[16,128,128]{2,1,0:T(8,128)(2,1)S(1)}, u32[]{:S(2)}, u32[]{:S(2)}) collective-permute-start(bf16[16,128,128]{2,1,0:T(8,128)(2,1)S(1)} %all-to-all-done.own_set.rest_8_), channel_id=1, source_target_pairs={{56,0},{57,1},{58,2},{59,3},{60,4},{61,5},{62,6},{63,7},{0,8},{1,9... | collective-permute-start | bytes 1572872 | tf_op jit(solution)/shard_map/ppermute | solution.py:228
  42.7 0.0 collective-permute-done.3.rest_5_
  42.7 0.0 collective-permute-start.4
  42.7 0.3 fusion.2
  43.0 0.0 collective-permute-done.7.rest_12_
  43.0 0.8 collective-permute-start.6
  43.8 0.1 pad_maximum_fusion
  43.9 0.1 shard_map.65.squares
  44.0 0.1 fusion.1.allowed
  44.1 7.2 %collective-permute-done.6.rest_11_ = bf16[8,128,128]{2,1,0:T(8,128)(2,1)S(1)} collective-permute-done((bf16[8,128,128]{2,1,0:T(8,128)(2,1)S(1)}, bf16[8,128,128]{2,1,0:T(8,128)(2,1)S(1)}, u32[]{:S(2)}, u32[]{:S(2)}) %collective-permute-start.6) | collective-permute-done | bytes 262176 | tf_op jit(solution)/shard_map/ppermute | solution.py:228
  51.3 0.1 collective-permute-done.5.rest_10_
  51.4 0.0 collective-permute-done.4.rest_9_
  51.4 0.0 collective-permute-done.2.rest_3_
  51.4 3.4 %shard_map.66 = (bf16[128,128]{1,0:T(8,128)(2,1)S(1)}, bf16[8,32,128]{2,1,0:T(8,128)(2,1)S(1)}) custom-call(f32[128,128]{1,0:T(8,128)S(1)} %shard_map.65.squares, bf16[1,8192]{1,0:T(2,128)(2,1)S(1)} %get-tuple-element.40.rest_0_, bf16[1,8192]{1,0:T(2,128)(2,1)S(1)} %collective-permute-done.1.rest_1_, bf16[8192,128]{1,0:T(8,128)(2,1)S(1)} %bitcast.16, ...), custom_call_target="tpu_custom_call" | custom-call | tf_op jit(solution)/shard_map/pallas_call | solution.py:210
  54.9 0.0 copy-start
  54.9 13.3 %all_to_all.30 = bf16[8,32,128]{2,1,0:T(8,128)(2,1)S(1)} all-to-all(bf16[8,32,128]{2,1,0:T(8,128)(2,1)S(1)} %get-tuple-element.45), channel_id=1, replica_groups=mesh['groups'=2,'section'=2,'x2'=2,'x1'=2,'x0'=2,'y2'=2,'y1'=2,'y0'=2] {..., dimensions={0} | all-to-all | bytes 131072 | tf_op jit(solution)/shard_map/all_to_all | solution.py:288
  68.2 0.5 shard_map.67
  68.8 17.3 %all_to_all.31.rest_0_ = bf16[16,128,128]{2,1,0:T(8,128)(2,1)S(1)} all-to-all(bf16[16,128,128]{2,1,0:T(8,128)(2,1)S(1)} %shard_map.67), channel_id=1, replica_groups={{0,2,4,6,17,19,21,23,32,34,36,38,49,51,53,55},{8,10,12,14,25,27,29,31,4..., dimensions={0} | all-to-all | bytes 1048576 | tf_op jit(solution)/shard_map/all_to_all | solution.py:234
  86.1 0.2 collective-permute-start.9
  86.4 3.8 %collective-permute-start.8 = (bf16[16,128,128]{2,1,0:T(8,128)(2,1)S(1)}, bf16[16,128,128]{2,1,0:T(8,128)(2,1)S(1)}, u32[]{:S(2)}, u32[]{:S(2)}) collective-permute-start(bf16[16,128,128]{2,1,0:T(8,128)(2,1)S(1)} %all_to_all.31.rest_0_), channel_id=1, source_target_pairs={{8,0},{9,1},{10,2},{11,3},{12,4},{13,5},{14,6},{15,7},{16,8},{17,9... | collective-permute-start | bytes 1572872 | tf_op jit(solution)/shard_map/ppermute | solution.py:228
  90.2 0.1 collective-permute-start.11
  90.3 2.7 %collective-permute-start.10 = (bf16[8,128,128]{2,1,0:T(8,128)(2,1)S(1)}, bf16[8,128,128]{2,1,0:T(8,128)(2,1)S(1)}, u32[]{:S(2)}, u32[]{:S(2)}) collective-permute-start(bf16[8,128,128]{2,1,0:T(8,128)(2,1)S(1)} %get-tuple-element.62), channel_id=1, source_target_pairs={{1,0},{2,1},{3,2},{4,3},{5,4},{6,5},{7,6},{0,7},{9,8},{10,9},{11,1... | collective-permute-start | bytes 786440 | tf_op jit(solution)/shard_map/ppermute | solution.py:228
  93.1 0.8 shard_map.68.before
  93.9 2.9 %collective-permute-done.11.rest_3_ = bf16[8,128,128]{2,1,0:T(8,128)(2,1)S(1)} collective-permute-done((bf16[8,128,128]{2,1,0:T(8,128)(2,1)S(1)}, bf16[8,128,128]{2,1,0:T(8,128)(2,1)S(1)}, u32[]{:S(2)}, u32[]{:S(2)}) %collective-permute-start.11) | collective-permute-done | bytes 262176 | tf_op jit(solution)/shard_map/ppermute | solution.py:228
  96.7 2.2 %collective-permute-done.10.rest_2_ = bf16[8,128,128]{2,1,0:T(8,128)(2,1)S(1)} collective-permute-done((bf16[8,128,128]{2,1,0:T(8,128)(2,1)S(1)}, bf16[8,128,128]{2,1,0:T(8,128)(2,1)S(1)}, u32[]{:S(2)}, u32[]{:S(2)}) %collective-permute-start.10) | collective-permute-done | bytes 262176 | tf_op jit(solution)/shard_map/ppermute | solution.py:228
  98.9 0.0 collective-permute-done.9.rest_1_
  98.9 0.0 collective-permute-done.8.rest_0_
  98.9 0.7 shard_map.69
  99.6 19.2 %all_to_all.32.own_set.rest_8_ = bf16[16,128,128]{2,1,0:T(8,128)(2,1)S(1)} all-to-all(bf16[16,128,128]{2,1,0:T(8,128)(2,1)S(1)} %get-tuple-element.48), channel_id=1, replica_groups={{0,2,4,6,17,19,21,23,32,34,36,38,49,51,53,55},{8,10,12,14,25,27,29,31,4..., dimensions={0} | all-to-all | bytes 1048576 | tf_op jit(solution)/shard_map/all_to_all | solution.py:234
  118.8 2.5 %collective-permute-start.13 = (bf16[16,128,128]{2,1,0:T(8,128)(2,1)S(1)}, bf16[16,128,128]{2,1,0:T(8,128)(2,1)S(1)}, u32[]{:S(2)}, u32[]{:S(2)}) collective-permute-start(bf16[16,128,128]{2,1,0:T(8,128)(2,1)S(1)} %all_to_all.32.own_set.rest_8_), channel_id=1, source_target_pairs={{56,0},{57,1},{58,2},{59,3},{60,4},{61,5},{62,6},{63,7},{0,8},{1,9... | collective-permute-start | bytes 1572872 | tf_op jit(solution)/shard_map/ppermute | solution.py:228
  121.2 0.2 collective-permute-start.12
  121.5 1.9 collective-permute-start.15
  123.3 0.9 collective-permute-start.14
  124.3 0.1 shard_map.70.squares
  124.3 3.7 %collective-permute-done.15.rest_12_ = bf16[8,128,128]{2,1,0:T(8,128)(2,1)S(1)} collective-permute-done((bf16[8,128,128]{2,1,0:T(8,128)(2,1)S(1)}, bf16[8,128,128]{2,1,0:T(8,128)(2,1)S(1)}, u32[]{:S(2)}, u32[]{:S(2)}) %collective-permute-start.15) | collective-permute-done | bytes 262176 | tf_op jit(solution)/shard_map/ppermute | solution.py:228
  128.0 0.5 collective-permute-done.14.rest_11_
  128.6 1.2 collective-permute-done.13.rest_10_
  129.8 0.0 collective-permute-done.12.rest_9_
  129.8 3.4 %shard_map.71 = (bf16[128,128]{1,0:T(8,128)(2,1)S(1)}, bf16[8,32,128]{2,1,0:T(8,128)(2,1)S(1)}) custom-call(f32[128,128]{1,0:T(8,128)S(1)} %shard_map.70.squares, bf16[1,8192]{1,0:T(2,128)(2,1)S(1)} %get-tuple-element.40.rest_0_, bf16[1,8192]{1,0:T(2,128)(2,1)S(1)} %collective-permute-done.1.rest_1_, bf16[8192,128]{1,0:T(8,128)(2,1)S(1)} %bitcast.17, ...), custom_call_target="tpu_custom_call" | custom-call | tf_op jit(solution)/shard_map/pallas_call | solution.py:210
  133.2 11.2 %all_to_all.33 = bf16[8,32,128]{2,1,0:T(8,128)(2,1)S(1)} all-to-all(bf16[8,32,128]{2,1,0:T(8,128)(2,1)S(1)} %get-tuple-element.53), channel_id=1, replica_groups=mesh['groups'=2,'section'=2,'x2'=2,'x1'=2,'x0'=2,'y2'=2,'y1'=2,'y0'=2] {..., dimensions={0} | all-to-all | bytes 131072 | tf_op jit(solution)/shard_map/all_to_all | solution.py:288
  144.4 0.5 shard_map.72
  145.0 19.5 %all_to_all.34.rest_0_ = bf16[16,128,128]{2,1,0:T(8,128)(2,1)S(1)} all-to-all(bf16[16,128,128]{2,1,0:T(8,128)(2,1)S(1)} %shard_map.72), channel_id=1, replica_groups={{0,2,4,6,17,19,21,23,32,34,36,38,49,51,53,55},{8,10,12,14,25,27,29,31,4..., dimensions={0} | all-to-all | bytes 1048576 | tf_op jit(solution)/shard_map/all_to_all | solution.py:234
  164.5 1.2 collective-permute-start.17
  165.7 1.5 collective-permute-start.16
  167.2 0.5 collective-permute-start.19
  167.7 2.3 %collective-permute-start.18 = (bf16[8,128,128]{2,1,0:T(8,128)(2,1)S(1)}, bf16[8,128,128]{2,1,0:T(8,128)(2,1)S(1)}, u32[]{:S(2)}, u32[]{:S(2)}) collective-permute-start(bf16[8,128,128]{2,1,0:T(8,128)(2,1)S(1)} %get-tuple-element.58), channel_id=1, source_target_pairs={{1,0},{2,1},{3,2},{4,3},{5,4},{6,5},{7,6},{0,7},{9,8},{10,9},{11,1... | collective-permute-start | bytes 786440 | tf_op jit(solution)/shard_map/ppermute | solution.py:228
  170.0 0.8 shard_map.73.before
  170.8 3.0 %collective-permute-done.19.rest_4_ = bf16[8,128,128]{2,1,0:T(8,128)(2,1)S(1)} collective-permute-done((bf16[8,128,128]{2,1,0:T(8,128)(2,1)S(1)}, bf16[8,128,128]{2,1,0:T(8,128)(2,1)S(1)}, u32[]{:S(2)}, u32[]{:S(2)}) %collective-permute-start.19) | collective-permute-done | bytes 262176 | tf_op jit(solution)/shard_map/ppermute | solution.py:228
  173.7 0.0 collective-permute-done.18.rest_3_
  173.7 2.3 %collective-permute-done.17.rest_2_ = bf16[16,128,128]{2,1,0:T(8,128)(2,1)S(1)} collective-permute-done((bf16[16,128,128]{2,1,0:T(8,128)(2,1)S(1)}, bf16[16,128,128]{2,1,0:T(8,128)(2,1)S(1)}, u32[]{:S(2)}, u32[]{:S(2)}) %collective-permute-start.17) | collective-permute-done | bytes 524320 | tf_op jit(solution)/shard_map/ppermute | solution.py:228
  176.1 0.6 shard_map.74
  176.7 9.9 %collective-permute-start.20 = (bf16[128,128]{1,0:T(8,128)(2,1)S(1)}, bf16[128,128]{1,0:T(8,128)(2,1)S(1)}, u32[]{:S(2)}, u32[]{:S(2)}) collective-permute-start(bf16[128,128]{1,0:T(8,128)(2,1)S(1)} %get-tuple-element.56), channel_id=1, source_target_pairs={{0,64},{64,0},{1,65},{65,1},{2,66},{66,2},{3,67},{67,3},{4,68},{68... | collective-permute-start | bytes 98312 | tf_op jit(solution)/shard_map/ppermute | solution.py:303
  186.6 0.9 collective-permute-done.20.theirs
  187.5 0.6 shard_map.75
  (11 shorter events, 0.2 us)
Async XLA Ops:
  1.9 32.5 %all-to-all-start = ((bf16[16,128,128]{2,1,0:T(8,128)(2,1)}), bf16[16,128,128]{2,1,0:T(8,128)(2,1)S(1)}, u32[]{:S(2)}, u32[]{:S(2)}) async-start(bf16[16,128,128]{2,1,0:T(8,128)(2,1)} %get-tuple-element.34), calls=%async_computation | async-start | bytes 1048576 | tf_op jit(solution)/shard_map/all_to_all | solution.py:234
  20.3 31.1 %collective-permute-start.2 = (bf16[8192,128]{1,0:T(8,128)(2,1)}, bf16[8192,128]{1,0:T(8,128)(2,1)}, u32[]{:S(2)}, u32[]{:S(2)}) collective-permute-start(bf16[8192,128]{1,0:T(8,128)(2,1)} %bitcast.15), channel_id=1, source_target_pairs={{0,64},{64,0},{1,65},{65,1},{2,66},{66,2},{3,67},{67,3},{4,68},{68... | collective-permute-start | bytes 6291464 | tf_op jit(solution)/shard_map/ppermute | solution.py:251
  26.5 10.9 %collective-permute-start.1 = (bf16[1,8192]{1,0:T(2,128)(2,1)}, bf16[1,8192]{1,0:T(2,128)(2,1)S(1)}, u32[]{:S(2)}, u32[]{:S(2)}) collective-permute-start(bf16[1,8192]{1,0:T(2,128)(2,1)} %bitcast.25), channel_id=1, source_target_pairs={{0,64},{64,0},{1,65},{65,1},{2,66},{66,2},{3,67},{67,3},{4,68},{68... | collective-permute-start | bytes 49160 | tf_op jit(solution)/shard_map/ppermute | solution.py:252
  26.7 16.0 %collective-permute-start.3 = (bf16[32,8192]{1,0:T(8,128)(2,1)}, bf16[32,8192]{1,0:T(8,128)(2,1)}, u32[]{:S(2)}, u32[]{:S(2)}) collective-permute-start(bf16[32,8192]{1,0:T(8,128)(2,1)} %bitcast.23), channel_id=1, source_target_pairs={{0,64},{64,0},{1,65},{65,1},{2,66},{66,2},{3,67},{67,3},{4,68},{68... | collective-permute-start | bytes 1572872 | tf_op jit(solution)/shard_map/ppermute | solution.py:251
  27.0 66.0 %collective-permute-start = (bf16[8192,128]{1,0:T(8,128)(2,1)}, bf16[8192,128]{1,0:T(8,128)(2,1)S(1)}, u32[]{:S(2)}, u32[]{:S(2)}) collective-permute-start(bf16[8192,128]{1,0:T(8,128)(2,1)} %bitcast.10), channel_id=1, source_target_pairs={{0,64},{64,0},{1,65},{65,1},{2,66},{66,2},{3,67},{67,3},{4,68},{68... | collective-permute-start | bytes 6291464 | tf_op jit(solution)/shard_map/ppermute | solution.py:251
  34.5 17.0 %copy-start.1 = (bf16[1,1,8192,128]{3,2,1,0:T(8,128)(2,1)S(1)}, bf16[1,1,8192,128]{3,2,1,0:T(8,128)(2,1)}, u32[]{:S(2)}) copy-start(bf16[1,1,8192,128]{3,2,1,0:T(8,128)(2,1)} %param.9) | copy-start | bytes 6291460
  34.5 8.5 %collective-permute-start.7 = (bf16[8,128,128]{2,1,0:T(8,128)(2,1)S(1)}, bf16[8,128,128]{2,1,0:T(8,128)(2,1)S(1)}, u32[]{:S(2)}, u32[]{:S(2)}) collective-permute-start(bf16[8,128,128]{2,1,0:T(8,128)(2,1)S(1)} %get-tuple-element.63), channel_id=1, source_target_pairs={{7,0},{0,1},{1,2},{2,3},{3,4},{4,5},{5,6},{6,7},{15,8},{8,9},{9,10... | collective-permute-start | bytes 786440 | tf_op jit(solution)/shard_map/ppermute | solution.py:228
  37.4 14.0 %collective-permute-start.5 = (bf16[16,128,128]{2,1,0:T(8,128)(2,1)S(1)}, bf16[16,128,128]{2,1,0:T(8,128)(2,1)S(1)}, u32[]{:S(2)}, u32[]{:S(2)}) collective-permute-start(bf16[16,128,128]{2,1,0:T(8,128)(2,1)S(1)} %all-to-all-done.own_set.rest_8_), channel_id=1, source_target_pairs={{56,0},{57,1},{58,2},{59,3},{60,4},{61,5},{62,6},{63,7},{0,8},{1,9... | collective-permute-start | bytes 1572872 | tf_op jit(solution)/shard_map/ppermute | solution.py:228
  42.7 8.8 %collective-permute-start.4 = (bf16[16,128,128]{2,1,0:T(8,128)(2,1)S(1)}, bf16[16,128,128]{2,1,0:T(8,128)(2,1)S(1)}, u32[]{:S(2)}, u32[]{:S(2)}) collective-permute-start(bf16[16,128,128]{2,1,0:T(8,128)(2,1)S(1)} %all-to-all-done.own_set.rest_8_), channel_id=1, source_target_pairs={{8,0},{9,1},{10,2},{11,3},{12,4},{13,5},{14,6},{15,7},{16,8},{17,9... | collective-permute-start | bytes 1572872 | tf_op jit(solution)/shard_map/ppermute | solution.py:228
  43.0 8.3 %collective-permute-start.6 = (bf16[8,128,128]{2,1,0:T(8,128)(2,1)S(1)}, bf16[8,128,128]{2,1,0:T(8,128)(2,1)S(1)}, u32[]{:S(2)}, u32[]{:S(2)}) collective-permute-start(bf16[8,128,128]{2,1,0:T(8,128)(2,1)S(1)} %get-tuple-element.64), channel_id=1, source_target_pairs={{1,0},{2,1},{3,2},{4,3},{5,4},{6,5},{7,6},{0,7},{9,8},{10,9},{11,1... | collective-permute-start | bytes 786440 | tf_op jit(solution)/shard_map/ppermute | solution.py:228
  54.9 38.2 %copy-start = (bf16[1,1,8192,128]{3,2,1,0:T(8,128)(2,1)S(1)}, bf16[1,1,8192,128]{3,2,1,0:T(8,128)(2,1)}, u32[]{:S(2)}) copy-start(bf16[1,1,8192,128]{3,2,1,0:T(8,128)(2,1)} %param.11) | copy-start | bytes 6291460
  86.1 12.8 %collective-permute-start.9 = (bf16[16,128,128]{2,1,0:T(8,128)(2,1)S(1)}, bf16[16,128,128]{2,1,0:T(8,128)(2,1)S(1)}, u32[]{:S(2)}, u32[]{:S(2)}) collective-permute-start(bf16[16,128,128]{2,1,0:T(8,128)(2,1)S(1)} %all_to_all.31.rest_0_), channel_id=1, source_target_pairs={{56,0},{57,1},{58,2},{59,3},{60,4},{61,5},{62,6},{63,7},{0,8},{1,9... | collective-permute-start | bytes 1572872 | tf_op jit(solution)/shard_map/ppermute | solution.py:228
  86.4 12.5 %collective-permute-start.8 = (bf16[16,128,128]{2,1,0:T(8,128)(2,1)S(1)}, bf16[16,128,128]{2,1,0:T(8,128)(2,1)S(1)}, u32[]{:S(2)}, u32[]{:S(2)}) collective-permute-start(bf16[16,128,128]{2,1,0:T(8,128)(2,1)S(1)} %all_to_all.31.rest_0_), channel_id=1, source_target_pairs={{8,0},{9,1},{10,2},{11,3},{12,4},{13,5},{14,6},{15,7},{16,8},{17,9... | collective-permute-start | bytes 1572872 | tf_op jit(solution)/shard_map/ppermute | solution.py:228
  90.2 6.5 %collective-permute-start.11 = (bf16[8,128,128]{2,1,0:T(8,128)(2,1)S(1)}, bf16[8,128,128]{2,1,0:T(8,128)(2,1)S(1)}, u32[]{:S(2)}, u32[]{:S(2)}) collective-permute-start(bf16[8,128,128]{2,1,0:T(8,128)(2,1)S(1)} %get-tuple-element.61), channel_id=1, source_target_pairs={{7,0},{0,1},{1,2},{2,3},{3,4},{4,5},{5,6},{6,7},{15,8},{8,9},{9,10... | collective-permute-start | bytes 786440 | tf_op jit(solution)/shard_map/ppermute | solution.py:228
  90.3 8.6 %collective-permute-start.10 = (bf16[8,128,128]{2,1,0:T(8,128)(2,1)S(1)}, bf16[8,128,128]{2,1,0:T(8,128)(2,1)S(1)}, u32[]{:S(2)}, u32[]{:S(2)}) collective-permute-start(bf16[8,128,128]{2,1,0:T(8,128)(2,1)S(1)} %get-tuple-element.62), channel_id=1, source_target_pairs={{1,0},{2,1},{3,2},{4,3},{5,4},{6,5},{7,6},{0,7},{9,8},{10,9},{11,1... | collective-permute-start | bytes 786440 | tf_op jit(solution)/shard_map/ppermute | solution.py:228
  118.8 11.0 %collective-permute-start.13 = (bf16[16,128,128]{2,1,0:T(8,128)(2,1)S(1)}, bf16[16,128,128]{2,1,0:T(8,128)(2,1)S(1)}, u32[]{:S(2)}, u32[]{:S(2)}) collective-permute-start(bf16[16,128,128]{2,1,0:T(8,128)(2,1)S(1)} %all_to_all.32.own_set.rest_8_), channel_id=1, source_target_pairs={{56,0},{57,1},{58,2},{59,3},{60,4},{61,5},{62,6},{63,7},{0,8},{1,9... | collective-permute-start | bytes 1572872 | tf_op jit(solution)/shard_map/ppermute | solution.py:228
  121.2 8.5 %collective-permute-start.12 = (bf16[16,128,128]{2,1,0:T(8,128)(2,1)S(1)}, bf16[16,128,128]{2,1,0:T(8,128)(2,1)S(1)}, u32[]{:S(2)}, u32[]{:S(2)}) collective-permute-start(bf16[16,128,128]{2,1,0:T(8,128)(2,1)S(1)} %all_to_all.32.own_set.rest_8_), channel_id=1, source_target_pairs={{8,0},{9,1},{10,2},{11,3},{12,4},{13,5},{14,6},{15,7},{16,8},{17,9... | collective-permute-start | bytes 1572872 | tf_op jit(solution)/shard_map/ppermute | solution.py:228
  121.5 6.5 %collective-permute-start.15 = (bf16[8,128,128]{2,1,0:T(8,128)(2,1)S(1)}, bf16[8,128,128]{2,1,0:T(8,128)(2,1)S(1)}, u32[]{:S(2)}, u32[]{:S(2)}) collective-permute-start(bf16[8,128,128]{2,1,0:T(8,128)(2,1)S(1)} %get-tuple-element.59), channel_id=1, source_target_pairs={{7,0},{0,1},{1,2},{2,3},{3,4},{4,5},{5,6},{6,7},{15,8},{8,9},{9,10... | collective-permute-start | bytes 786440 | tf_op jit(solution)/shard_map/ppermute | solution.py:228
  123.3 5.2 %collective-permute-start.14 = (bf16[8,128,128]{2,1,0:T(8,128)(2,1)S(1)}, bf16[8,128,128]{2,1,0:T(8,128)(2,1)S(1)}, u32[]{:S(2)}, u32[]{:S(2)}) collective-permute-start(bf16[8,128,128]{2,1,0:T(8,128)(2,1)S(1)} %get-tuple-element.60), channel_id=1, source_target_pairs={{1,0},{2,1},{3,2},{4,3},{5,4},{6,5},{7,6},{0,7},{9,8},{10,9},{11,1... | collective-permute-start | bytes 786440 | tf_op jit(solution)/shard_map/ppermute | solution.py:228
  164.5 11.6 %collective-permute-start.17 = (bf16[16,128,128]{2,1,0:T(8,128)(2,1)S(1)}, bf16[16,128,128]{2,1,0:T(8,128)(2,1)S(1)}, u32[]{:S(2)}, u32[]{:S(2)}) collective-permute-start(bf16[16,128,128]{2,1,0:T(8,128)(2,1)S(1)} %all_to_all.34.rest_0_), channel_id=1, source_target_pairs={{56,0},{57,1},{58,2},{59,3},{60,4},{61,5},{62,6},{63,7},{0,8},{1,9... | collective-permute-start | bytes 1572872 | tf_op jit(solution)/shard_map/ppermute | solution.py:228
  165.7 10.4 %collective-permute-start.16 = (bf16[16,128,128]{2,1,0:T(8,128)(2,1)S(1)}, bf16[16,128,128]{2,1,0:T(8,128)(2,1)S(1)}, u32[]{:S(2)}, u32[]{:S(2)}) collective-permute-start(bf16[16,128,128]{2,1,0:T(8,128)(2,1)S(1)} %all_to_all.34.rest_0_), channel_id=1, source_target_pairs={{8,0},{9,1},{10,2},{11,3},{12,4},{13,5},{14,6},{15,7},{16,8},{17,9... | collective-permute-start | bytes 1572872 | tf_op jit(solution)/shard_map/ppermute | solution.py:228
  167.2 6.5 %collective-permute-start.19 = (bf16[8,128,128]{2,1,0:T(8,128)(2,1)S(1)}, bf16[8,128,128]{2,1,0:T(8,128)(2,1)S(1)}, u32[]{:S(2)}, u32[]{:S(2)}) collective-permute-start(bf16[8,128,128]{2,1,0:T(8,128)(2,1)S(1)} %get-tuple-element.57), channel_id=1, source_target_pairs={{7,0},{0,1},{1,2},{2,3},{3,4},{4,5},{5,6},{6,7},{15,8},{8,9},{9,10... | collective-permute-start | bytes 786440 | tf_op jit(solution)/shard_map/ppermute | solution.py:228
  167.7 6.1 %collective-permute-start.18 = (bf16[8,128,128]{2,1,0:T(8,128)(2,1)S(1)}, bf16[8,128,128]{2,1,0:T(8,128)(2,1)S(1)}, u32[]{:S(2)}, u32[]{:S(2)}) collective-permute-start(bf16[8,128,128]{2,1,0:T(8,128)(2,1)S(1)} %get-tuple-element.58), channel_id=1, source_target_pairs={{1,0},{2,1},{3,2},{4,3},{5,4},{6,5},{7,6},{0,7},{9,8},{10,9},{11,1... | collective-permute-start | bytes 786440 | tf_op jit(solution)/shard_map/ppermute | solution.py:228
  176.7 10.8 %collective-permute-start.20 = (bf16[128,128]{1,0:T(8,128)(2,1)S(1)}, bf16[128,128]{1,0:T(8,128)(2,1)S(1)}, u32[]{:S(2)}, u32[]{:S(2)}) collective-permute-start(bf16[128,128]{1,0:T(8,128)(2,1)S(1)} %get-tuple-element.56), channel_id=1, source_target_pairs={{0,64},{64,0},{1,65},{65,1},{2,66},{66,2},{3,67},{67,3},{4,68},{68... | collective-permute-start | bytes 98312 | tf_op jit(solution)/shard_map/ppermute | solution.py:303

commit v8 on v7

--- a/solution.py
+++ b/solution.py
@@ -44,39 +44,37 @@
 STEP = 4
 
 
+def member(colour, j):
+    step, half = j % SIDE, j // SIDE
+    return (colour + 2 * step + 4 * half) % SIDE, step
+
+
 def colour_groups(sections):
     groups = []
     for section in range(sections):
-        one = [[] for _ in range(STEP)]
-        for first in range(SIDE):
-            for second in range(SIDE):
+        for colour in range(STEP):
+            group = []
+            for j in range(FAR_COUNT):
+                first, second = member(colour, j)
                 x, y = (first, second) if section == 0 else (second, first)
-                one[(first + 2 * second) % STEP].append((section * SIDE + x) * SIDE + y)
-        groups += one
+                group.append((section * SIDE + x) * SIDE + y)
+            groups.append(group)
     return groups
 
 
-def for_chunks(buffers, layout, body, carry, unrolled=False):
+def for_chunks(buffers, layout, body, carry):
     swapped = lax.axis_index("section") != 0
-    x0, x1, y0, y1 = (lax.axis_index(name) for name in ("x0", "x1", "y0", "y1"))
-    own_odd = jnp.where(swapped, y0, x0)
-    own_half = jnp.where(swapped, y1 + x0, x1 + y0)
+    x, y = lax.axis_index(X), lax.axis_index(Y)
+    own = jnp.where(swapped, y + 2 * x, x + 2 * y)
     stride, side = jnp.where(swapped, 1, SIDE), jnp.where(swapped, SIDE, 1)
     for ref, (turn, skip) in zip(buffers, layout, strict=True):
-        colour = own_odd + 2 * own_half + turn
-        odd, half = colour % 2, colour // 2
-
-        def chunk(i, carry, ref=ref, odd=odd, half=half, skip=skip):
-            line = i + skip
-            place = stride * (odd + 2 * line) + side * ((half + line) % 2)
-            return body([(ref[i * STEP + k], place + side * 2 * k) for k in range(STEP)], carry)
-
-        count = ref.shape[0] // STEP
-        if unrolled:
-            for i in range(count):
-                carry = chunk(i, carry)
-        else:
-            carry = lax.fori_loop(0, count, chunk, carry)
+        colour = (own + turn) % STEP
+        for i in range(0, ref.shape[0], STEP):
+            chunk = []
+            for j in range(i, i + STEP):
+                first, second = member(colour, skip * STEP + j)
+                chunk.append((ref[j], stride * first + side * second))
+            carry = body(chunk, carry)
     return carry
 
 
@@ -137,7 +135,7 @@
         return q_sum, kv_sum
 
     zero = jnp.zeros((rows, width), jnp.float32), jnp.zeros((rows, columns), jnp.float32)
-    q_sum, kv_sum = for_chunks(buffers, layout, body, zero, unrolled=True)
+    q_sum, kv_sum = for_chunks(buffers, layout, body, zero)
     turned = jnp.concatenate([q_sum[:, HALF:], q_sum[:, :HALF]], axis=1)
     query[...] = (q_sum * cosine[...] + turned * sine[...]).astype(query.dtype)
     flat = kv_sum.T.astype(keyval.dtype)
@@ -171,7 +169,7 @@
         return mixed + jnp.dot(joined, weight, preferred_element_type=jnp.float32)
 
     mixed = before[...].astype(jnp.float32)
-    mixed = for_chunks(buffers, layout, body, mixed, unrolled=len(layout) > 1)
+    mixed = for_chunks(buffers, layout, body, mixed)
     out = mixed.astype(outs[0].dtype)
     if past:
         lower = lax.axis_index("section") == 0

time: 189 us -> 198 us (1.048)
  the two profiles are of different devices: /device:TPU:513 before, /device:TPU:647 now
where the time goes in v8:
time: 198 us
  blocking collectives  85.7 us (43%)
  waiting for transfers between devices  51.1 us (26%)
  starting transfers between devices  47.5 us (24%)
  Pallas kernels  12.7 us (6%)
    all_to_all x3, blocking collectives, far_stage(): lax.all_to_all(copies, axes, 0, 0, axis_index_groups=groups, tiled=True)  63.4 us
    ppermute x16, waiting for transfers between devices, from_neighbour(): return lax.ppermute(block, ('section',) + MESH, pairs)  36.2 us
    ppermute x16, starting transfers between devices, from_neighbour(): return lax.ppermute(block, ('section',) + MESH, pairs)  23.2 us
    all_to_all x2, blocking collectives, shards(): keyval = lax.all_to_all(keyval, Y, 0, 0, tiled=True).reshape(-1, rows)  22.3 us
    all_to_all x1, starting transfers between devices, far_stage(): lax.all_to_all(copies, axes, 0, 0, axis_index_groups=groups, tiled=True)  19.5 us
    all_to_all x1, waiting for transfers between devices, far_stage(): lax.all_to_all(copies, axes, 0, 0, axis_index_groups=groups, tiled=True)  14 us
    pallas_call x11, Pallas kernels, call(): pl.pallas_call(kernel, out_shape=outs, in_specs=[vmem] * len(args), out_s...  10.7 us
  transfers between devices with their start and end apart: 22, of which 10 were waited for; matrix products, arithmetic and copies ran while one was open for 0% of the time, Pallas kernels for 2%

profile of v8, /device:TPU:647, one launch (start us, length us, event | category | flops | bytes accessed | tf_op | source)
XLA Modules:
  0.0 197.9 jit_solution(4650270400603864342)
XLA Ops:
  0.0 1.9 shard_map.64
  1.9 19.5 %all-to-all-start = ((bf16[16,128,128]{2,1,0:T(8,128)(2,1)}), bf16[16,128,128]{2,1,0:T(8,128)(2,1)S(1)}, u32[]{:S(2)}, u32[]{:S(2)}) async-start(bf16[16,128,128]{2,1,0:T(8,128)(2,1)} %get-tuple-element.34), calls=%async_computation | async-start | bytes 1048576 | tf_op jit(solution)/shard_map/all_to_all | solution.py:232
  21.5 0.0 collective-permute-start.2
  21.5 0.5 collective-permute-start.1
  22.0 0.1 collective-permute-start.3
  22.1 0.4 collective-permute-start
  22.5 14.0 %all-to-all-done.own_set.rest_8_ = bf16[16,128,128]{2,1,0:T(8,128)(2,1)S(1)} async-done(((bf16[16,128,128]{2,1,0:T(8,128)(2,1)}), bf16[16,128,128]{2,1,0:T(8,128)(2,1)S(1)}, u32[]{:S(2)}, u32[]{:S(2)}) %all-to-all-start) | async-done | bytes 524320 | tf_op jit(solution)/shard_map/all_to_all | solution.py:232
  36.6 3.3 %collective-permute-start.7 = (bf16[8,128,128]{2,1,0:T(8,128)(2,1)S(1)}, bf16[8,128,128]{2,1,0:T(8,128)(2,1)S(1)}, u32[]{:S(2)}, u32[]{:S(2)}) collective-permute-start(bf16[8,128,128]{2,1,0:T(8,128)(2,1)S(1)} %get-tuple-element.63), channel_id=1, source_target_pairs={{7,0},{0,1},{1,2},{2,3},{3,4},{4,5},{5,6},{6,7},{15,8},{8,9},{9,10... | collective-permute-start | bytes 786440 | tf_op jit(solution)/shard_map/ppermute | solution.py:226
  39.9 0.2 fusion
  40.1 0.0 collective-permute-done.1.rest_1_
  40.1 0.7 collective-permute-start.5
  40.8 0.0 collective-permute-done.3.rest_5_
  40.8 2.1 %collective-permute-start.4 = (bf16[16,128,128]{2,1,0:T(8,128)(2,1)S(1)}, bf16[16,128,128]{2,1,0:T(8,128)(2,1)S(1)}, u32[]{:S(2)}, u32[]{:S(2)}) collective-permute-start(bf16[16,128,128]{2,1,0:T(8,128)(2,1)S(1)} %all-to-all-done.own_set.rest_8_), channel_id=1, source_target_pairs={{8,0},{9,1},{10,2},{11,3},{12,4},{13,5},{14,6},{15,7},{16,8},{17,9... | collective-permute-start | bytes 1572872 | tf_op jit(solution)/shard_map/ppermute | solution.py:226
  42.9 0.3 fusion.2
  43.2 1.5 collective-permute-done.7.rest_12_
  44.8 0.0 collective-permute-start.6
  44.8 0.1 pad_maximum_fusion
  44.9 0.1 shard_map.65.squares
  44.9 0.1 fusion.1.allowed
  45.0 8.5 %collective-permute-done.6.rest_11_ = bf16[8,128,128]{2,1,0:T(8,128)(2,1)S(1)} collective-permute-done((bf16[8,128,128]{2,1,0:T(8,128)(2,1)S(1)}, bf16[8,128,128]{2,1,0:T(8,128)(2,1)S(1)}, u32[]{:S(2)}, u32[]{:S(2)}) %collective-permute-start.6) | collective-permute-done | bytes 262176 | tf_op jit(solution)/shard_map/ppermute | solution.py:226
  53.5 0.0 collective-permute-done.5.rest_10_
  53.5 0.0 collective-permute-done.4.rest_9_
  53.5 0.0 collective-permute-done.2.rest_3_
  53.6 3.4 %shard_map.66 = (bf16[128,128]{1,0:T(8,128)(2,1)S(1)}, bf16[8,32,128]{2,1,0:T(8,128)(2,1)S(1)}) custom-call(f32[128,128]{1,0:T(8,128)S(1)} %shard_map.65.squares, bf16[1,8192]{1,0:T(2,128)(2,1)S(1)} %get-tuple-element.40.rest_0_, bf16[1,8192]{1,0:T(2,128)(2,1)S(1)} %collective-permute-done.1.rest_1_, bf16[8192,128]{1,0:T(8,128)(2,1)S(1)} %bitcast.16, ...), custom_call_target="tpu_custom_call" | custom-call | tf_op jit(solution)/shard_map/pallas_call | solution.py:208
  57.0 0.0 copy-start
  57.0 10.2 %all_to_all.30 = bf16[8,32,128]{2,1,0:T(8,128)(2,1)S(1)} all-to-all(bf16[8,32,128]{2,1,0:T(8,128)(2,1)S(1)} %get-tuple-element.45), channel_id=1, replica_groups=mesh['groups'=2,'section'=2,'x2'=2,'x1'=2,'x0'=2,'y2'=2,'y1'=2,'y0'=2] {..., dimensions={0} | all-to-all | bytes 131072 | tf_op jit(solution)/shard_map/all_to_all | solution.py:286
  67.2 0.5 shard_map.67
  67.8 21.7 %all_to_all.31.rest_0_ = bf16[16,128,128]{2,1,0:T(8,128)(2,1)S(1)} all-to-all(bf16[16,128,128]{2,1,0:T(8,128)(2,1)S(1)} %shard_map.67), channel_id=1, replica_groups={{0,17,34,51,4,21,38,55,32,49,2,19,36,53,6,23},{8,25,42,59,12,29,46,63,4..., dimensions={0} | all-to-all | bytes 1048576 | tf_op jit(solution)/shard_map/all_to_all | solution.py:232
  89.5 0.0 collective-permute-start.9
  89.5 2.7 %collective-permute-start.8 = (bf16[16,128,128]{2,1,0:T(8,128)(2,1)S(1)}, bf16[16,128,128]{2,1,0:T(8,128)(2,1)S(1)}, u32[]{:S(2)}, u32[]{:S(2)}) collective-permute-start(bf16[16,128,128]{2,1,0:T(8,128)(2,1)S(1)} %all_to_all.31.rest_0_), channel_id=1, source_target_pairs={{8,0},{9,1},{10,2},{11,3},{12,4},{13,5},{14,6},{15,7},{16,8},{17,9... | collective-permute-start | bytes 1572872 | tf_op jit(solution)/shard_map/ppermute | solution.py:226
  92.2 1.6 collective-permute-start.11
  93.8 0.0 collective-permute-start.10
  93.8 0.0 collective-permute-done.other
  93.8 0.4 shard_map.68.before
  94.1 6.5 %collective-permute-done.11.rest_3_ = bf16[8,128,128]{2,1,0:T(8,128)(2,1)S(1)} collective-permute-done((bf16[8,128,128]{2,1,0:T(8,128)(2,1)S(1)}, bf16[8,128,128]{2,1,0:T(8,128)(2,1)S(1)}, u32[]{:S(2)}, u32[]{:S(2)}) %collective-permute-start.11) | collective-permute-done | bytes 262176 | tf_op jit(solution)/shard_map/ppermute | solution.py:226
  100.6 1.8 collective-permute-done.10.rest_2_
  102.4 0.0 collective-permute-done.9.rest_1_
  102.4 0.0 collective-permute-done.8.rest_0_
  102.5 0.7 shard_map.69
  103.1 19.7 %all_to_all.32.own_set.rest_8_ = bf16[16,128,128]{2,1,0:T(8,128)(2,1)S(1)} all-to-all(bf16[16,128,128]{2,1,0:T(8,128)(2,1)S(1)} %get-tuple-element.48), channel_id=1, replica_groups={{0,17,34,51,4,21,38,55,32,49,2,19,36,53,6,23},{8,25,42,59,12,29,46,63,4..., dimensions={0} | all-to-all | bytes 1048576 | tf_op jit(solution)/shard_map/all_to_all | solution.py:232
  122.8 4.2 %collective-permute-start.13 = (bf16[16,128,128]{2,1,0:T(8,128)(2,1)S(1)}, bf16[16,128,128]{2,1,0:T(8,128)(2,1)S(1)}, u32[]{:S(2)}, u32[]{:S(2)}) collective-permute-start(bf16[16,128,128]{2,1,0:T(8,128)(2,1)S(1)} %all_to_all.32.own_set.rest_8_), channel_id=1, source_target_pairs={{56,0},{57,1},{58,2},{59,3},{60,4},{61,5},{62,6},{63,7},{0,8},{1,9... | collective-permute-start | bytes 1572872 | tf_op jit(solution)/shard_map/ppermute | solution.py:226
  127.0 0.2 collective-permute-start.12
  127.2 3.3 %collective-permute-start.15 = (bf16[8,128,128]{2,1,0:T(8,128)(2,1)S(1)}, bf16[8,128,128]{2,1,0:T(8,128)(2,1)S(1)}, u32[]{:S(2)}, u32[]{:S(2)}) collective-permute-start(bf16[8,128,128]{2,1,0:T(8,128)(2,1)S(1)} %get-tuple-element.59), channel_id=1, source_target_pairs={{7,0},{0,1},{1,2},{2,3},{3,4},{4,5},{5,6},{6,7},{15,8},{8,9},{9,10... | collective-permute-start | bytes 786440 | tf_op jit(solution)/shard_map/ppermute | solution.py:226
  130.5 0.0 collective-permute-start.14
  130.5 0.1 shard_map.70.squares
  130.6 5.9 %collective-permute-done.15.rest_12_ = bf16[8,128,128]{2,1,0:T(8,128)(2,1)S(1)} collective-permute-done((bf16[8,128,128]{2,1,0:T(8,128)(2,1)S(1)}, bf16[8,128,128]{2,1,0:T(8,128)(2,1)S(1)}, u32[]{:S(2)}, u32[]{:S(2)}) %collective-permute-start.15) | collective-permute-done | bytes 262176 | tf_op jit(solution)/shard_map/ppermute | solution.py:226
  136.5 3.1 %collective-permute-done.14.rest_11_ = bf16[8,128,128]{2,1,0:T(8,128)(2,1)S(1)} collective-permute-done((bf16[8,128,128]{2,1,0:T(8,128)(2,1)S(1)}, bf16[8,128,128]{2,1,0:T(8,128)(2,1)S(1)}, u32[]{:S(2)}, u32[]{:S(2)}) %collective-permute-start.14) | collective-permute-done | bytes 262176 | tf_op jit(solution)/shard_map/ppermute | solution.py:226
  139.7 0.0 collective-permute-done.13.rest_10_
  139.7 3.4 %shard_map.71 = (bf16[128,128]{1,0:T(8,128)(2,1)S(1)}, bf16[8,32,128]{2,1,0:T(8,128)(2,1)S(1)}) custom-call(f32[128,128]{1,0:T(8,128)S(1)} %shard_map.70.squares, bf16[1,8192]{1,0:T(2,128)(2,1)S(1)} %get-tuple-element.40.rest_0_, bf16[1,8192]{1,0:T(2,128)(2,1)S(1)} %collective-permute-done.1.rest_1_, bf16[8192,128]{1,0:T(8,128)(2,1)S(1)} %bitcast.17, ...), custom_call_target="tpu_custom_call" | custom-call | tf_op jit(solution)/shard_map/pallas_call | solution.py:208
  143.1 12.1 %all_to_all.33 = bf16[8,32,128]{2,1,0:T(8,128)(2,1)S(1)} all-to-all(bf16[8,32,128]{2,1,0:T(8,128)(2,1)S(1)} %get-tuple-element.53), channel_id=1, replica_groups=mesh['groups'=2,'section'=2,'x2'=2,'x1'=2,'x0'=2,'y2'=2,'y1'=2,'y0'=2] {..., dimensions={0} | all-to-all | bytes 131072 | tf_op jit(solution)/shard_map/all_to_all | solution.py:286
  155.2 0.5 shard_map.72
  155.8 22.1 %all_to_all.34.rest_0_ = bf16[16,128,128]{2,1,0:T(8,128)(2,1)S(1)} all-to-all(bf16[16,128,128]{2,1,0:T(8,128)(2,1)S(1)} %shard_map.72), channel_id=1, replica_groups={{0,17,34,51,4,21,38,55,32,49,2,19,36,53,6,23},{8,25,42,59,12,29,46,63,4..., dimensions={0} | all-to-all | bytes 1048576 | tf_op jit(solution)/shard_map/all_to_all | solution.py:232
  177.8 0.7 collective-permute-start.17
  178.6 1.9 collective-permute-start.16
  180.5 2.4 %collective-permute-start.19 = (bf16[8,128,128]{2,1,0:T(8,128)(2,1)S(1)}, bf16[8,128,128]{2,1,0:T(8,128)(2,1)S(1)}, u32[]{:S(2)}, u32[]{:S(2)}) collective-permute-start(bf16[8,128,128]{2,1,0:T(8,128)(2,1)S(1)} %get-tuple-element.57), channel_id=1, source_target_pairs={{7,0},{0,1},{1,2},{2,3},{3,4},{4,5},{5,6},{6,7},{15,8},{8,9},{9,10... | collective-permute-start | bytes 786440 | tf_op jit(solution)/shard_map/ppermute | solution.py:226
  182.9 0.3 shard_map.73.before
  183.2 5.6 %collective-permute-done.19.rest_4_ = bf16[8,128,128]{2,1,0:T(8,128)(2,1)S(1)} collective-permute-done((bf16[8,128,128]{2,1,0:T(8,128)(2,1)S(1)}, bf16[8,128,128]{2,1,0:T(8,128)(2,1)S(1)}, u32[]{:S(2)}, u32[]{:S(2)}) %collective-permute-start.19) | collective-permute-done | bytes 262176 | tf_op jit(solution)/shard_map/ppermute | solution.py:226
  188.9 3.1 %collective-permute-done.18.rest_3_ = bf16[8,128,128]{2,1,0:T(8,128)(2,1)S(1)} collective-permute-done((bf16[8,128,128]{2,1,0:T(8,128)(2,1)S(1)}, bf16[8,128,128]{2,1,0:T(8,128)(2,1)S(1)}, u32[]{:S(2)}, u32[]{:S(2)}) %collective-permute-start.18) | collective-permute-done | bytes 262176 | tf_op jit(solution)/shard_map/ppermute | solution.py:226
  192.0 0.0 collective-permute-done.17.rest_2_
  192.0 0.0 collective-permute-done.16.rest_1_
  192.0 0.6 shard_map.74
  192.7 3.7 %collective-permute-start.20 = (bf16[128,128]{1,0:T(8,128)(2,1)S(1)}, bf16[128,128]{1,0:T(8,128)(2,1)S(1)}, u32[]{:S(2)}, u32[]{:S(2)}) collective-permute-start(bf16[128,128]{1,0:T(8,128)(2,1)S(1)} %get-tuple-element.56), channel_id=1, source_target_pairs={{0,64},{64,0},{1,65},{65,1},{2,66},{66,2},{3,67},{67,3},{4,68},{68... | collective-permute-start | bytes 98312 | tf_op jit(solution)/shard_map/ppermute | solution.py:301
  196.4 0.9 collective-permute-done.20.theirs
  197.3 0.6 shard_map.75
  (11 shorter events, 0.2 us)
Async XLA Ops:
  1.9 34.6 %all-to-all-start = ((bf16[16,128,128]{2,1,0:T(8,128)(2,1)}), bf16[16,128,128]{2,1,0:T(8,128)(2,1)S(1)}, u32[]{:S(2)}, u32[]{:S(2)}) async-start(bf16[16,128,128]{2,1,0:T(8,128)(2,1)} %get-tuple-element.34), calls=%async_computation | async-start | bytes 1048576 | tf_op jit(solution)/shard_map/all_to_all | solution.py:232
  21.5 32.1 %collective-permute-start.2 = (bf16[8192,128]{1,0:T(8,128)(2,1)}, bf16[8192,128]{1,0:T(8,128)(2,1)}, u32[]{:S(2)}, u32[]{:S(2)}) collective-permute-start(bf16[8192,128]{1,0:T(8,128)(2,1)} %bitcast.15), channel_id=1, source_target_pairs={{0,64},{64,0},{1,65},{65,1},{2,66},{66,2},{3,67},{67,3},{4,68},{68... | collective-permute-start | bytes 6291464 | tf_op jit(solution)/shard_map/ppermute | solution.py:249
  21.5 18.6 %collective-permute-start.1 = (bf16[1,8192]{1,0:T(2,128)(2,1)}, bf16[1,8192]{1,0:T(2,128)(2,1)S(1)}, u32[]{:S(2)}, u32[]{:S(2)}) collective-permute-start(bf16[1,8192]{1,0:T(2,128)(2,1)} %bitcast.25), channel_id=1, source_target_pairs={{0,64},{64,0},{1,65},{65,1},{2,66},{66,2},{3,67},{67,3},{4,68},{68... | collective-permute-start | bytes 49160 | tf_op jit(solution)/shard_map/ppermute | solution.py:250
  22.0 18.8 %collective-permute-start.3 = (bf16[32,8192]{1,0:T(8,128)(2,1)}, bf16[32,8192]{1,0:T(8,128)(2,1)}, u32[]{:S(2)}, u32[]{:S(2)}) collective-permute-start(bf16[32,8192]{1,0:T(8,128)(2,1)} %bitcast.23), channel_id=1, source_target_pairs={{0,64},{64,0},{1,65},{65,1},{2,66},{66,2},{3,67},{67,3},{4,68},{68... | collective-permute-start | bytes 1572872 | tf_op jit(solution)/shard_map/ppermute | solution.py:249
  22.1 71.6 %collective-permute-start = (bf16[8192,128]{1,0:T(8,128)(2,1)}, bf16[8192,128]{1,0:T(8,128)(2,1)S(1)}, u32[]{:S(2)}, u32[]{:S(2)}) collective-permute-start(bf16[8192,128]{1,0:T(8,128)(2,1)} %bitcast.10), channel_id=1, source_target_pairs={{0,64},{64,0},{1,65},{65,1},{2,66},{66,2},{3,67},{67,3},{4,68},{68... | collective-permute-start | bytes 6291464 | tf_op jit(solution)/shard_map/ppermute | solution.py:249
  36.5 17.0 %copy-start.1 = (bf16[1,1,8192,128]{3,2,1,0:T(8,128)(2,1)S(1)}, bf16[1,1,8192,128]{3,2,1,0:T(8,128)(2,1)}, u32[]{:S(2)}) copy-start(bf16[1,1,8192,128]{3,2,1,0:T(8,128)(2,1)} %param.9) | copy-start | bytes 6291460
  36.6 8.2 %collective-permute-start.7 = (bf16[8,128,128]{2,1,0:T(8,128)(2,1)S(1)}, bf16[8,128,128]{2,1,0:T(8,128)(2,1)S(1)}, u32[]{:S(2)}, u32[]{:S(2)}) collective-permute-start(bf16[8,128,128]{2,1,0:T(8,128)(2,1)S(1)} %get-tuple-element.63), channel_id=1, source_target_pairs={{7,0},{0,1},{1,2},{2,3},{3,4},{4,5},{5,6},{6,7},{15,8},{8,9},{9,10... | collective-permute-start | bytes 786440 | tf_op jit(solution)/shard_map/ppermute | solution.py:226
  40.1 13.4 %collective-permute-start.5 = (bf16[16,128,128]{2,1,0:T(8,128)(2,1)S(1)}, bf16[16,128,128]{2,1,0:T(8,128)(2,1)S(1)}, u32[]{:S(2)}, u32[]{:S(2)}) collective-permute-start(bf16[16,128,128]{2,1,0:T(8,128)(2,1)S(1)} %all-to-all-done.own_set.rest_8_), channel_id=1, source_target_pairs={{56,0},{57,1},{58,2},{59,3},{60,4},{61,5},{62,6},{63,7},{0,8},{1,9... | collective-permute-start | bytes 1572872 | tf_op jit(solution)/shard_map/ppermute | solution.py:226
  40.8 12.7 %collective-permute-start.4 = (bf16[16,128,128]{2,1,0:T(8,128)(2,1)S(1)}, bf16[16,128,128]{2,1,0:T(8,128)(2,1)S(1)}, u32[]{:S(2)}, u32[]{:S(2)}) collective-permute-start(bf16[16,128,128]{2,1,0:T(8,128)(2,1)S(1)} %all-to-all-done.own_set.rest_8_), channel_id=1, source_target_pairs={{8,0},{9,1},{10,2},{11,3},{12,4},{13,5},{14,6},{15,7},{16,8},{17,9... | collective-permute-start | bytes 1572872 | tf_op jit(solution)/shard_map/ppermute | solution.py:226
  44.8 8.8 %collective-permute-start.6 = (bf16[8,128,128]{2,1,0:T(8,128)(2,1)S(1)}, bf16[8,128,128]{2,1,0:T(8,128)(2,1)S(1)}, u32[]{:S(2)}, u32[]{:S(2)}) collective-permute-start(bf16[8,128,128]{2,1,0:T(8,128)(2,1)S(1)} %get-tuple-element.64), channel_id=1, source_target_pairs={{1,0},{2,1},{3,2},{4,3},{5,4},{6,5},{7,6},{0,7},{9,8},{10,9},{11,1... | collective-permute-start | bytes 786440 | tf_op jit(solution)/shard_map/ppermute | solution.py:226
  57.0 36.8 %copy-start = (bf16[1,1,8192,128]{3,2,1,0:T(8,128)(2,1)S(1)}, bf16[1,1,8192,128]{3,2,1,0:T(8,128)(2,1)}, u32[]{:S(2)}) copy-start(bf16[1,1,8192,128]{3,2,1,0:T(8,128)(2,1)} %param.11) | copy-start | bytes 6291460
  89.5 13.0 %collective-permute-start.9 = (bf16[16,128,128]{2,1,0:T(8,128)(2,1)S(1)}, bf16[16,128,128]{2,1,0:T(8,128)(2,1)S(1)}, u32[]{:S(2)}, u32[]{:S(2)}) collective-permute-start(bf16[16,128,128]{2,1,0:T(8,128)(2,1)S(1)} %all_to_all.31.rest_0_), channel_id=1, source_target_pairs={{56,0},{57,1},{58,2},{59,3},{60,4},{61,5},{62,6},{63,7},{0,8},{1,9... | collective-permute-start | bytes 1572872 | tf_op jit(solution)/shard_map/ppermute | solution.py:226
  89.5 13.0 %collective-permute-start.8 = (bf16[16,128,128]{2,1,0:T(8,128)(2,1)S(1)}, bf16[16,128,128]{2,1,0:T(8,128)(2,1)S(1)}, u32[]{:S(2)}, u32[]{:S(2)}) collective-permute-start(bf16[16,128,128]{2,1,0:T(8,128)(2,1)S(1)} %all_to_all.31.rest_0_), channel_id=1, source_target_pairs={{8,0},{9,1},{10,2},{11,3},{12,4},{13,5},{14,6},{15,7},{16,8},{17,9... | collective-permute-start | bytes 1572872 | tf_op jit(solution)/shard_map/ppermute | solution.py:226
  92.2 8.4 %collective-permute-start.11 = (bf16[8,128,128]{2,1,0:T(8,128)(2,1)S(1)}, bf16[8,128,128]{2,1,0:T(8,128)(2,1)S(1)}, u32[]{:S(2)}, u32[]{:S(2)}) collective-permute-start(bf16[8,128,128]{2,1,0:T(8,128)(2,1)S(1)} %get-tuple-element.61), channel_id=1, source_target_pairs={{7,0},{0,1},{1,2},{2,3},{3,4},{4,5},{5,6},{6,7},{15,8},{8,9},{9,10... | collective-permute-start | bytes 786440 | tf_op jit(solution)/shard_map/ppermute | solution.py:226
  93.8 8.7 %collective-permute-start.10 = (bf16[8,128,128]{2,1,0:T(8,128)(2,1)S(1)}, bf16[8,128,128]{2,1,0:T(8,128)(2,1)S(1)}, u32[]{:S(2)}, u32[]{:S(2)}) collective-permute-start(bf16[8,128,128]{2,1,0:T(8,128)(2,1)S(1)} %get-tuple-element.62), channel_id=1, source_target_pairs={{1,0},{2,1},{3,2},{4,3},{5,4},{6,5},{7,6},{0,7},{9,8},{10,9},{11,1... | collective-permute-start | bytes 786440 | tf_op jit(solution)/shard_map/ppermute | solution.py:226
  122.8 16.9 %collective-permute-start.13 = (bf16[16,128,128]{2,1,0:T(8,128)(2,1)S(1)}, bf16[16,128,128]{2,1,0:T(8,128)(2,1)S(1)}, u32[]{:S(2)}, u32[]{:S(2)}) collective-permute-start(bf16[16,128,128]{2,1,0:T(8,128)(2,1)S(1)} %all_to_all.32.own_set.rest_8_), channel_id=1, source_target_pairs={{56,0},{57,1},{58,2},{59,3},{60,4},{61,5},{62,6},{63,7},{0,8},{1,9... | collective-permute-start | bytes 1572872 | tf_op jit(solution)/shard_map/ppermute | solution.py:226
  127.0 12.7 %collective-permute-start.12 = (bf16[16,128,128]{2,1,0:T(8,128)(2,1)S(1)}, bf16[16,128,128]{2,1,0:T(8,128)(2,1)S(1)}, u32[]{:S(2)}, u32[]{:S(2)}) collective-permute-start(bf16[16,128,128]{2,1,0:T(8,128)(2,1)S(1)} %all_to_all.32.own_set.rest_8_), channel_id=1, source_target_pairs={{8,0},{9,1},{10,2},{11,3},{12,4},{13,5},{14,6},{15,7},{16,8},{17,9... | collective-permute-start | bytes 1572872 | tf_op jit(solution)/shard_map/ppermute | solution.py:226
  127.2 9.3 %collective-permute-start.15 = (bf16[8,128,128]{2,1,0:T(8,128)(2,1)S(1)}, bf16[8,128,128]{2,1,0:T(8,128)(2,1)S(1)}, u32[]{:S(2)}, u32[]{:S(2)}) collective-permute-start(bf16[8,128,128]{2,1,0:T(8,128)(2,1)S(1)} %get-tuple-element.59), channel_id=1, source_target_pairs={{7,0},{0,1},{1,2},{2,3},{3,4},{4,5},{5,6},{6,7},{15,8},{8,9},{9,10... | collective-permute-start | bytes 786440 | tf_op jit(solution)/shard_map/ppermute | solution.py:226
  130.5 9.1 %collective-permute-start.14 = (bf16[8,128,128]{2,1,0:T(8,128)(2,1)S(1)}, bf16[8,128,128]{2,1,0:T(8,128)(2,1)S(1)}, u32[]{:S(2)}, u32[]{:S(2)}) collective-permute-start(bf16[8,128,128]{2,1,0:T(8,128)(2,1)S(1)} %get-tuple-element.60), channel_id=1, source_target_pairs={{1,0},{2,1},{3,2},{4,3},{5,4},{6,5},{7,6},{0,7},{9,8},{10,9},{11,1... | collective-permute-start | bytes 786440 | tf_op jit(solution)/shard_map/ppermute | solution.py:226
  177.8 14.2 %collective-permute-start.17 = (bf16[16,128,128]{2,1,0:T(8,128)(2,1)S(1)}, bf16[16,128,128]{2,1,0:T(8,128)(2,1)S(1)}, u32[]{:S(2)}, u32[]{:S(2)}) collective-permute-start(bf16[16,128,128]{2,1,0:T(8,128)(2,1)S(1)} %all_to_all.34.rest_0_), channel_id=1, source_target_pairs={{56,0},{57,1},{58,2},{59,3},{60,4},{61,5},{62,6},{63,7},{0,8},{1,9... | collective-permute-start | bytes 1572872 | tf_op jit(solution)/shard_map/ppermute | solution.py:226
  178.6 13.5 %collective-permute-start.16 = (bf16[16,128,128]{2,1,0:T(8,128)(2,1)S(1)}, bf16[16,128,128]{2,1,0:T(8,128)(2,1)S(1)}, u32[]{:S(2)}, u32[]{:S(2)}) collective-permute-start(bf16[16,128,128]{2,1,0:T(8,128)(2,1)S(1)} %all_to_all.34.rest_0_), channel_id=1, source_target_pairs={{8,0},{9,1},{10,2},{11,3},{12,4},{13,5},{14,6},{15,7},{16,8},{17,9... | collective-permute-start | bytes 1572872 | tf_op jit(solution)/shard_map/ppermute | solution.py:226
  180.5 8.4 %collective-permute-start.19 = (bf16[8,128,128]{2,1,0:T(8,128)(2,1)S(1)}, bf16[8,128,128]{2,1,0:T(8,128)(2,1)S(1)}, u32[]{:S(2)}, u32[]{:S(2)}) collective-permute-start(bf16[8,128,128]{2,1,0:T(8,128)(2,1)S(1)} %get-tuple-element.57), channel_id=1, source_target_pairs={{7,0},{0,1},{1,2},{2,3},{3,4},{4,5},{5,6},{6,7},{15,8},{8,9},{9,10... | collective-permute-start | bytes 786440 | tf_op jit(solution)/shard_map/ppermute | solution.py:226
  182.9 9.1 %collective-permute-start.18 = (bf16[8,128,128]{2,1,0:T(8,128)(2,1)S(1)}, bf16[8,128,128]{2,1,0:T(8,128)(2,1)S(1)}, u32[]{:S(2)}, u32[]{:S(2)}) collective-permute-start(bf16[8,128,128]{2,1,0:T(8,128)(2,1)S(1)} %get-tuple-element.58), channel_id=1, source_target_pairs={{1,0},{2,1},{3,2},{4,3},{5,4},{6,5},{7,6},{0,7},{9,8},{10,9},{11,1... | collective-permute-start | bytes 786440 | tf_op jit(solution)/shard_map/ppermute | solution.py:226
  192.7 4.6 %collective-permute-start.20 = (bf16[128,128]{1,0:T(8,128)(2,1)S(1)}, bf16[128,128]{1,0:T(8,128)(2,1)S(1)}, u32[]{:S(2)}, u32[]{:S(2)}) collective-permute-start(bf16[128,128]{1,0:T(8,128)(2,1)S(1)} %get-tuple-element.56), channel_id=1, source_target_pairs={{0,64},{64,0},{1,65},{65,1},{2,66},{66,2},{3,67},{67,3},{4,68},{68... | collective-permute-start | bytes 98312 | tf_op jit(solution)/shard_map/ppermute | solution.py:301

commit v9 on v8

--- a/solution.py
+++ b/solution.py
@@ -20,16 +20,13 @@
 MIB = 1024 * 1024
 
 
-def frequencies():
-    return rope_theta ** (-(2.0 * jnp.arange(HALF, dtype=jnp.float32)) / HD)
-
-
-def position_tables(segment_row, freqs):
+def position_tables(segment_row, steps):
     row_length = segment_row.shape[0]
     indices = jnp.arange(row_length, dtype=jnp.int32)
     same = segment_row[None, :] == segment_row[:, None]
     first_index = jnp.min(jnp.where(same, indices[None, :], row_length), axis=1)
     positions = (indices - first_index).astype(jnp.float32)
+    freqs = rope_theta ** (-(2.0 * steps) / HD)
     angles = positions[:, None] * freqs[None, :]
     cosine, sine = jnp.cos(angles), jnp.sin(angles)
     allowed = (indices[None, :] <= indices[:, None]) & same
@@ -267,15 +264,15 @@
         ],
         compiler_params=pltpu.CompilerParams(vmem_limit_bytes=4 * MIB),
     )(*(pltpu.with_memory_space_constraint(a, pltpu.HBM) for a in sources))
-    copies, segment_row, freqs = lax.optimization_barrier((copies, segment_row, frequencies()))
     stages = len(STAGES)
     for s in range(sections):
         far = far_stage(copies)
-        if s == 0:
-            far, segment_row = lax.optimization_barrier((far, segment_row))
-            cosine, sine, allowed = position_tables(segment_row[0], freqs)
         near = near_stage(far)
         squares = call(squares_kernel, f32((rows, width)), 4, *near[0])
+        if s == 0:
+            steps = jnp.arange(HALF, dtype=jnp.float32)
+            squares, segment_row, steps = lax.optimization_barrier((squares, segment_row, steps))
+            cosine, sine, allowed = position_tables(segment_row[0], steps)
         squares, cosine, sine, allowed = lax.optimization_barrier(
             (squares, cosine, sine, allowed)
         )

time: 198 us -> 199 us (level)
  no operation moved by 1% of the time
where the time goes in v9:
time: 199 us
  blocking collectives  84.3 us (42%)
  waiting for transfers between devices  52 us (26%)
  starting transfers between devices  48.8 us (25%)
  Pallas kernels  12.6 us (6%)
    all_to_all x3, blocking collectives, far_stage(): lax.all_to_all(copies, axes, 0, 0, axis_index_groups=groups, tiled=True)  62.4 us
    ppermute x16, waiting for transfers between devices, from_neighbour(): return lax.ppermute(block, ('section',) + MESH, pairs)  37.1 us
    ppermute x16, starting transfers between devices, from_neighbour(): return lax.ppermute(block, ('section',) + MESH, pairs)  24.8 us
    all_to_all x2, blocking collectives, shards(): keyval = lax.all_to_all(keyval, Y, 0, 0, tiled=True).reshape(-1, rows)  21.8 us
    all_to_all x1, starting transfers between devices, far_stage(): lax.all_to_all(copies, axes, 0, 0, axis_index_groups=groups, tiled=True)  19.5 us
    all_to_all x1, waiting for transfers between devices, far_stage(): lax.all_to_all(copies, axes, 0, 0, axis_index_groups=groups, tiled=True)  14 us
    pallas_call x11, Pallas kernels, call(): pl.pallas_call(kernel, out_shape=outs, in_specs=[vmem] * len(args), out_s...  10.7 us
  transfers between devices with their start and end apart: 22, of which 10 were waited for; matrix products, arithmetic and copies ran while one was open for 0% of the time, Pallas kernels for 2%

profile of v9, /device:TPU:647, one launch (start us, length us, event | category | flops | bytes accessed | tf_op | source)
XLA Modules:
  0.0 198.8 jit_solution(13296843288459292510)
XLA Ops:
  0.0 1.9 shard_map.64
  1.9 19.5 %all-to-all-start = ((bf16[16,128,128]{2,1,0:T(8,128)(2,1)}), bf16[16,128,128]{2,1,0:T(8,128)(2,1)S(1)}, u32[]{:S(2)}, u32[]{:S(2)}) async-start(bf16[16,128,128]{2,1,0:T(8,128)(2,1)} %get-tuple-element.30), calls=%async_computation | async-start | bytes 1048576 | tf_op jit(solution)/shard_map/all_to_all | solution.py:229
  21.5 0.0 collective-permute-start.2
  21.5 0.5 collective-permute-start.1
  22.0 0.1 collective-permute-start.3
  22.1 0.4 collective-permute-start
  22.5 14.0 %all-to-all-done.own_set.rest_8_ = bf16[16,128,128]{2,1,0:T(8,128)(2,1)S(1)} async-done(((bf16[16,128,128]{2,1,0:T(8,128)(2,1)}), bf16[16,128,128]{2,1,0:T(8,128)(2,1)S(1)}, u32[]{:S(2)}, u32[]{:S(2)}) %all-to-all-start) | async-done | bytes 524320 | tf_op jit(solution)/shard_map/all_to_all | solution.py:229
  36.5 0.1 shard_map.65.squares
  36.7 3.3 %collective-permute-start.7 = (bf16[8,128,128]{2,1,0:T(8,128)(2,1)S(1)}, bf16[8,128,128]{2,1,0:T(8,128)(2,1)S(1)}, u32[]{:S(2)}, u32[]{:S(2)}) collective-permute-start(bf16[8,128,128]{2,1,0:T(8,128)(2,1)S(1)} %get-tuple-element.59), channel_id=1, source_target_pairs={{7,0},{0,1},{1,2},{2,3},{3,4},{4,5},{5,6},{6,7},{15,8},{8,9},{9,10... | collective-permute-start | bytes 786440 | tf_op jit(solution)/shard_map/ppermute | solution.py:223
  40.0 0.2 fusion
  40.2 0.0 collective-permute-done.1.rest_1_
  40.2 0.7 collective-permute-start.5
  40.9 0.0 collective-permute-done.3.rest_5_
  40.9 2.1 %collective-permute-start.4 = (bf16[16,128,128]{2,1,0:T(8,128)(2,1)S(1)}, bf16[16,128,128]{2,1,0:T(8,128)(2,1)S(1)}, u32[]{:S(2)}, u32[]{:S(2)}) collective-permute-start(bf16[16,128,128]{2,1,0:T(8,128)(2,1)S(1)} %all-to-all-done.own_set.rest_8_), channel_id=1, source_target_pairs={{8,0},{9,1},{10,2},{11,3},{12,4},{13,5},{14,6},{15,7},{16,8},{17,9... | collective-permute-start | bytes 1572872 | tf_op jit(solution)/shard_map/ppermute | solution.py:223
  43.0 0.3 fusion.2
  43.3 1.5 collective-permute-done.7.rest_12_
  44.8 0.0 collective-permute-start.6
  44.8 0.1 pad_maximum_fusion
  44.9 0.1 fusion.1.allowed
  45.0 8.6 %collective-permute-done.6.rest_11_ = bf16[8,128,128]{2,1,0:T(8,128)(2,1)S(1)} collective-permute-done((bf16[8,128,128]{2,1,0:T(8,128)(2,1)S(1)}, bf16[8,128,128]{2,1,0:T(8,128)(2,1)S(1)}, u32[]{:S(2)}, u32[]{:S(2)}) %collective-permute-start.6) | collective-permute-done | bytes 262176 | tf_op jit(solution)/shard_map/ppermute | solution.py:223
  53.6 0.0 collective-permute-done.5.rest_10_
  53.6 0.0 collective-permute-done.4.rest_9_
  53.6 0.0 collective-permute-done.2.rest_3_
  53.6 3.5 %shard_map.66 = (bf16[128,128]{1,0:T(8,128)(2,1)S(1)}, bf16[8,32,128]{2,1,0:T(8,128)(2,1)S(1)}) custom-call(f32[128,128]{1,0:T(8,128)S(1)} %shard_map.65.squares, bf16[1,8192]{1,0:T(2,128)(2,1)S(1)} %get-tuple-element.36.rest_0_, bf16[1,8192]{1,0:T(2,128)(2,1)S(1)} %collective-permute-done.1.rest_1_, bf16[8192,128]{1,0:T(8,128)(2,1)S(1)} %bitcast.16, ...), custom_call_target="tpu_custom_call" | custom-call | tf_op jit(solution)/shard_map/pallas_call | solution.py:205
  57.1 0.0 copy-start
  57.1 10.2 %all_to_all.30 = bf16[8,32,128]{2,1,0:T(8,128)(2,1)S(1)} all-to-all(bf16[8,32,128]{2,1,0:T(8,128)(2,1)S(1)} %get-tuple-element.41), channel_id=1, replica_groups=mesh['groups'=2,'section'=2,'x2'=2,'x1'=2,'x0'=2,'y2'=2,'y1'=2,'y0'=2] {..., dimensions={0} | all-to-all | bytes 131072 | tf_op jit(solution)/shard_map/all_to_all | solution.py:283
  67.3 0.5 shard_map.67
  67.9 21.7 %all_to_all.31.rest_0_ = bf16[16,128,128]{2,1,0:T(8,128)(2,1)S(1)} all-to-all(bf16[16,128,128]{2,1,0:T(8,128)(2,1)S(1)} %shard_map.67), channel_id=1, replica_groups={{0,17,34,51,4,21,38,55,32,49,2,19,36,53,6,23},{8,25,42,59,12,29,46,63,4..., dimensions={0} | all-to-all | bytes 1048576 | tf_op jit(solution)/shard_map/all_to_all | solution.py:229
  89.6 0.0 collective-permute-start.9
  89.6 2.7 %collective-permute-start.8 = (bf16[16,128,128]{2,1,0:T(8,128)(2,1)S(1)}, bf16[16,128,128]{2,1,0:T(8,128)(2,1)S(1)}, u32[]{:S(2)}, u32[]{:S(2)}) collective-permute-start(bf16[16,128,128]{2,1,0:T(8,128)(2,1)S(1)} %all_to_all.31.rest_0_), channel_id=1, source_target_pairs={{8,0},{9,1},{10,2},{11,3},{12,4},{13,5},{14,6},{15,7},{16,8},{17,9... | collective-permute-start | bytes 1572872 | tf_op jit(solution)/shard_map/ppermute | solution.py:223
  92.3 1.6 collective-permute-start.11
  93.9 0.0 collective-permute-start.10
  93.9 0.0 collective-permute-done.other
  93.9 0.4 shard_map.68.before
  94.3 6.5 %collective-permute-done.11.rest_3_ = bf16[8,128,128]{2,1,0:T(8,128)(2,1)S(1)} collective-permute-done((bf16[8,128,128]{2,1,0:T(8,128)(2,1)S(1)}, bf16[8,128,128]{2,1,0:T(8,128)(2,1)S(1)}, u32[]{:S(2)}, u32[]{:S(2)}) %collective-permute-start.11) | collective-permute-done | bytes 262176 | tf_op jit(solution)/shard_map/ppermute | solution.py:223
  100.8 2.0 %collective-permute-done.10.rest_2_ = bf16[8,128,128]{2,1,0:T(8,128)(2,1)S(1)} collective-permute-done((bf16[8,128,128]{2,1,0:T(8,128)(2,1)S(1)}, bf16[8,128,128]{2,1,0:T(8,128)(2,1)S(1)}, u32[]{:S(2)}, u32[]{:S(2)}) %collective-permute-start.10) | collective-permute-done | bytes 262176 | tf_op jit(solution)/shard_map/ppermute | solution.py:223
  102.7 0.0 collective-permute-done.9.rest_1_
  102.8 0.0 collective-permute-done.8.rest_0_
  102.8 0.7 shard_map.69
  103.4 18.7 %all_to_all.32.own_set.rest_8_ = bf16[16,128,128]{2,1,0:T(8,128)(2,1)S(1)} all-to-all(bf16[16,128,128]{2,1,0:T(8,128)(2,1)S(1)} %get-tuple-element.44), channel_id=1, replica_groups={{0,17,34,51,4,21,38,55,32,49,2,19,36,53,6,23},{8,25,42,59,12,29,46,63,4..., dimensions={0} | all-to-all | bytes 1048576 | tf_op jit(solution)/shard_map/all_to_all | solution.py:229
  122.2 5.0 %collective-permute-start.13 = (bf16[16,128,128]{2,1,0:T(8,128)(2,1)S(1)}, bf16[16,128,128]{2,1,0:T(8,128)(2,1)S(1)}, u32[]{:S(2)}, u32[]{:S(2)}) collective-permute-start(bf16[16,128,128]{2,1,0:T(8,128)(2,1)S(1)} %all_to_all.32.own_set.rest_8_), channel_id=1, source_target_pairs={{56,0},{57,1},{58,2},{59,3},{60,4},{61,5},{62,6},{63,7},{0,8},{1,9... | collective-permute-start | bytes 1572872 | tf_op jit(solution)/shard_map/ppermute | solution.py:223
  127.2 0.0 collective-permute-start.12
  127.3 4.1 %collective-permute-start.15 = (bf16[8,128,128]{2,1,0:T(8,128)(2,1)S(1)}, bf16[8,128,128]{2,1,0:T(8,128)(2,1)S(1)}, u32[]{:S(2)}, u32[]{:S(2)}) collective-permute-start(bf16[8,128,128]{2,1,0:T(8,128)(2,1)S(1)} %get-tuple-element.55), channel_id=1, source_target_pairs={{7,0},{0,1},{1,2},{2,3},{3,4},{4,5},{5,6},{6,7},{15,8},{8,9},{9,10... | collective-permute-start | bytes 786440 | tf_op jit(solution)/shard_map/ppermute | solution.py:223
  131.3 0.0 collective-permute-start.14
  131.3 0.1 shard_map.70.squares
  131.4 6.0 %collective-permute-done.15.rest_12_ = bf16[8,128,128]{2,1,0:T(8,128)(2,1)S(1)} collective-permute-done((bf16[8,128,128]{2,1,0:T(8,128)(2,1)S(1)}, bf16[8,128,128]{2,1,0:T(8,128)(2,1)S(1)}, u32[]{:S(2)}, u32[]{:S(2)}) %collective-permute-start.15) | collective-permute-done | bytes 262176 | tf_op jit(solution)/shard_map/ppermute | solution.py:223
  137.4 3.4 %collective-permute-done.14.rest_11_ = bf16[8,128,128]{2,1,0:T(8,128)(2,1)S(1)} collective-permute-done((bf16[8,128,128]{2,1,0:T(8,128)(2,1)S(1)}, bf16[8,128,128]{2,1,0:T(8,128)(2,1)S(1)}, u32[]{:S(2)}, u32[]{:S(2)}) %collective-permute-start.14) | collective-permute-done | bytes 262176 | tf_op jit(solution)/shard_map/ppermute | solution.py:223
  140.8 0.0 collective-permute-done.13.rest_10_
  140.8 0.0 collective-permute-done.12.rest_9_
  140.8 3.4 %shard_map.71 = (bf16[128,128]{1,0:T(8,128)(2,1)S(1)}, bf16[8,32,128]{2,1,0:T(8,128)(2,1)S(1)}) custom-call(f32[128,128]{1,0:T(8,128)S(1)} %shard_map.70.squares, bf16[1,8192]{1,0:T(2,128)(2,1)S(1)} %get-tuple-element.36.rest_0_, bf16[1,8192]{1,0:T(2,128)(2,1)S(1)} %collective-permute-done.1.rest_1_, bf16[8192,128]{1,0:T(8,128)(2,1)S(1)} %bitcast.17, ...), custom_call_target="tpu_custom_call" | custom-call | tf_op jit(solution)/shard_map/pallas_call | solution.py:205
  144.3 11.6 %all_to_all.33 = bf16[8,32,128]{2,1,0:T(8,128)(2,1)S(1)} all-to-all(bf16[8,32,128]{2,1,0:T(8,128)(2,1)S(1)} %get-tuple-element.49), channel_id=1, replica_groups=mesh['groups'=2,'section'=2,'x2'=2,'x1'=2,'x0'=2,'y2'=2,'y1'=2,'y0'=2] {..., dimensions={0} | all-to-all | bytes 131072 | tf_op jit(solution)/shard_map/all_to_all | solution.py:283
  155.9 0.5 shard_map.72
  156.5 22.0 %all_to_all.34.rest_0_ = bf16[16,128,128]{2,1,0:T(8,128)(2,1)S(1)} all-to-all(bf16[16,128,128]{2,1,0:T(8,128)(2,1)S(1)} %shard_map.72), channel_id=1, replica_groups={{0,17,34,51,4,21,38,55,32,49,2,19,36,53,6,23},{8,25,42,59,12,29,46,63,4..., dimensions={0} | all-to-all | bytes 1048576 | tf_op jit(solution)/shard_map/all_to_all | solution.py:229
  178.4 0.9 collective-permute-start.17
  179.3 1.8 collective-permute-start.16
  181.2 2.6 %collective-permute-start.19 = (bf16[8,128,128]{2,1,0:T(8,128)(2,1)S(1)}, bf16[8,128,128]{2,1,0:T(8,128)(2,1)S(1)}, u32[]{:S(2)}, u32[]{:S(2)}) collective-permute-start(bf16[8,128,128]{2,1,0:T(8,128)(2,1)S(1)} %get-tuple-element.53), channel_id=1, source_target_pairs={{7,0},{0,1},{1,2},{2,3},{3,4},{4,5},{5,6},{6,7},{15,8},{8,9},{9,10... | collective-permute-start | bytes 786440 | tf_op jit(solution)/shard_map/ppermute | solution.py:223
  183.8 0.0 collective-permute-start.18
  183.8 0.3 shard_map.73.before
  184.1 5.8 %collective-permute-done.19.rest_4_ = bf16[8,128,128]{2,1,0:T(8,128)(2,1)S(1)} collective-permute-done((bf16[8,128,128]{2,1,0:T(8,128)(2,1)S(1)}, bf16[8,128,128]{2,1,0:T(8,128)(2,1)S(1)}, u32[]{:S(2)}, u32[]{:S(2)}) %collective-permute-start.19) | collective-permute-done | bytes 262176 | tf_op jit(solution)/shard_map/ppermute | solution.py:223
  189.9 3.2 %collective-permute-done.18.rest_3_ = bf16[8,128,128]{2,1,0:T(8,128)(2,1)S(1)} collective-permute-done((bf16[8,128,128]{2,1,0:T(8,128)(2,1)S(1)}, bf16[8,128,128]{2,1,0:T(8,128)(2,1)S(1)}, u32[]{:S(2)}, u32[]{:S(2)}) %collective-permute-start.18) | collective-permute-done | bytes 262176 | tf_op jit(solution)/shard_map/ppermute | solution.py:223
  193.2 0.6 shard_map.74
  193.8 3.5 %collective-permute-start.20 = (bf16[128,128]{1,0:T(8,128)(2,1)S(1)}, bf16[128,128]{1,0:T(8,128)(2,1)S(1)}, u32[]{:S(2)}, u32[]{:S(2)}) collective-permute-start(bf16[128,128]{1,0:T(8,128)(2,1)S(1)} %get-tuple-element.52), channel_id=1, source_target_pairs={{0,64},{64,0},{1,65},{65,1},{2,66},{66,2},{3,67},{67,3},{4,68},{68... | collective-permute-start | bytes 98312 | tf_op jit(solution)/shard_map/ppermute | solution.py:298
  197.3 0.9 collective-permute-done.20.theirs
  198.1 0.6 shard_map.75
  (12 shorter events, 0.2 us)
Async XLA Ops:
  1.9 34.6 %all-to-all-start = ((bf16[16,128,128]{2,1,0:T(8,128)(2,1)}), bf16[16,128,128]{2,1,0:T(8,128)(2,1)S(1)}, u32[]{:S(2)}, u32[]{:S(2)}) async-start(bf16[16,128,128]{2,1,0:T(8,128)(2,1)} %get-tuple-element.30), calls=%async_computation | async-start | bytes 1048576 | tf_op jit(solution)/shard_map/all_to_all | solution.py:229
  21.5 32.2 %collective-permute-start.2 = (bf16[8192,128]{1,0:T(8,128)(2,1)}, bf16[8192,128]{1,0:T(8,128)(2,1)}, u32[]{:S(2)}, u32[]{:S(2)}) collective-permute-start(bf16[8192,128]{1,0:T(8,128)(2,1)} %bitcast.15), channel_id=1, source_target_pairs={{0,64},{64,0},{1,65},{65,1},{2,66},{66,2},{3,67},{67,3},{4,68},{68... | collective-permute-start | bytes 6291464 | tf_op jit(solution)/shard_map/ppermute | solution.py:246
  21.5 18.7 %collective-permute-start.1 = (bf16[1,8192]{1,0:T(2,128)(2,1)}, bf16[1,8192]{1,0:T(2,128)(2,1)S(1)}, u32[]{:S(2)}, u32[]{:S(2)}) collective-permute-start(bf16[1,8192]{1,0:T(2,128)(2,1)} %bitcast.25), channel_id=1, source_target_pairs={{0,64},{64,0},{1,65},{65,1},{2,66},{66,2},{3,67},{67,3},{4,68},{68... | collective-permute-start | bytes 49160 | tf_op jit(solution)/shard_map/ppermute | solution.py:247
  22.0 18.9 %collective-permute-start.3 = (bf16[32,8192]{1,0:T(8,128)(2,1)}, bf16[32,8192]{1,0:T(8,128)(2,1)}, u32[]{:S(2)}, u32[]{:S(2)}) collective-permute-start(bf16[32,8192]{1,0:T(8,128)(2,1)} %bitcast.23), channel_id=1, source_target_pairs={{0,64},{64,0},{1,65},{65,1},{2,66},{66,2},{3,67},{67,3},{4,68},{68... | collective-permute-start | bytes 1572872 | tf_op jit(solution)/shard_map/ppermute | solution.py:246
  22.1 71.8 %collective-permute-start = (bf16[8192,128]{1,0:T(8,128)(2,1)}, bf16[8192,128]{1,0:T(8,128)(2,1)S(1)}, u32[]{:S(2)}, u32[]{:S(2)}) collective-permute-start(bf16[8192,128]{1,0:T(8,128)(2,1)} %bitcast.10), channel_id=1, source_target_pairs={{0,64},{64,0},{1,65},{65,1},{2,66},{66,2},{3,67},{67,3},{4,68},{68... | collective-permute-start | bytes 6291464 | tf_op jit(solution)/shard_map/ppermute | solution.py:246
  36.5 17.1 %copy-start.1 = (bf16[1,1,8192,128]{3,2,1,0:T(8,128)(2,1)S(1)}, bf16[1,1,8192,128]{3,2,1,0:T(8,128)(2,1)}, u32[]{:S(2)}) copy-start(bf16[1,1,8192,128]{3,2,1,0:T(8,128)(2,1)} %param.9) | copy-start | bytes 6291460
  36.7 8.2 %collective-permute-start.7 = (bf16[8,128,128]{2,1,0:T(8,128)(2,1)S(1)}, bf16[8,128,128]{2,1,0:T(8,128)(2,1)S(1)}, u32[]{:S(2)}, u32[]{:S(2)}) collective-permute-start(bf16[8,128,128]{2,1,0:T(8,128)(2,1)S(1)} %get-tuple-element.59), channel_id=1, source_target_pairs={{7,0},{0,1},{1,2},{2,3},{3,4},{4,5},{5,6},{6,7},{15,8},{8,9},{9,10... | collective-permute-start | bytes 786440 | tf_op jit(solution)/shard_map/ppermute | solution.py:223
  40.2 13.4 %collective-permute-start.5 = (bf16[16,128,128]{2,1,0:T(8,128)(2,1)S(1)}, bf16[16,128,128]{2,1,0:T(8,128)(2,1)S(1)}, u32[]{:S(2)}, u32[]{:S(2)}) collective-permute-start(bf16[16,128,128]{2,1,0:T(8,128)(2,1)S(1)} %all-to-all-done.own_set.rest_8_), channel_id=1, source_target_pairs={{56,0},{57,1},{58,2},{59,3},{60,4},{61,5},{62,6},{63,7},{0,8},{1,9... | collective-permute-start | bytes 1572872 | tf_op jit(solution)/shard_map/ppermute | solution.py:223
  40.9 12.7 %collective-permute-start.4 = (bf16[16,128,128]{2,1,0:T(8,128)(2,1)S(1)}, bf16[16,128,128]{2,1,0:T(8,128)(2,1)S(1)}, u32[]{:S(2)}, u32[]{:S(2)}) collective-permute-start(bf16[16,128,128]{2,1,0:T(8,128)(2,1)S(1)} %all-to-all-done.own_set.rest_8_), channel_id=1, source_target_pairs={{8,0},{9,1},{10,2},{11,3},{12,4},{13,5},{14,6},{15,7},{16,8},{17,9... | collective-permute-start | bytes 1572872 | tf_op jit(solution)/shard_map/ppermute | solution.py:223
  44.8 8.8 %collective-permute-start.6 = (bf16[8,128,128]{2,1,0:T(8,128)(2,1)S(1)}, bf16[8,128,128]{2,1,0:T(8,128)(2,1)S(1)}, u32[]{:S(2)}, u32[]{:S(2)}) collective-permute-start(bf16[8,128,128]{2,1,0:T(8,128)(2,1)S(1)} %get-tuple-element.60), channel_id=1, source_target_pairs={{1,0},{2,1},{3,2},{4,3},{5,4},{6,5},{7,6},{0,7},{9,8},{10,9},{11,1... | collective-permute-start | bytes 786440 | tf_op jit(solution)/shard_map/ppermute | solution.py:223
  57.1 36.8 %copy-start = (bf16[1,1,8192,128]{3,2,1,0:T(8,128)(2,1)S(1)}, bf16[1,1,8192,128]{3,2,1,0:T(8,128)(2,1)}, u32[]{:S(2)}) copy-start(bf16[1,1,8192,128]{3,2,1,0:T(8,128)(2,1)} %param.11) | copy-start | bytes 6291460
  89.6 13.2 %collective-permute-start.9 = (bf16[16,128,128]{2,1,0:T(8,128)(2,1)S(1)}, bf16[16,128,128]{2,1,0:T(8,128)(2,1)S(1)}, u32[]{:S(2)}, u32[]{:S(2)}) collective-permute-start(bf16[16,128,128]{2,1,0:T(8,128)(2,1)S(1)} %all_to_all.31.rest_0_), channel_id=1, source_target_pairs={{56,0},{57,1},{58,2},{59,3},{60,4},{61,5},{62,6},{63,7},{0,8},{1,9... | collective-permute-start | bytes 1572872 | tf_op jit(solution)/shard_map/ppermute | solution.py:223
  89.6 13.2 %collective-permute-start.8 = (bf16[16,128,128]{2,1,0:T(8,128)(2,1)S(1)}, bf16[16,128,128]{2,1,0:T(8,128)(2,1)S(1)}, u32[]{:S(2)}, u32[]{:S(2)}) collective-permute-start(bf16[16,128,128]{2,1,0:T(8,128)(2,1)S(1)} %all_to_all.31.rest_0_), channel_id=1, source_target_pairs={{8,0},{9,1},{10,2},{11,3},{12,4},{13,5},{14,6},{15,7},{16,8},{17,9... | collective-permute-start | bytes 1572872 | tf_op jit(solution)/shard_map/ppermute | solution.py:223
  92.3 8.4 %collective-permute-start.11 = (bf16[8,128,128]{2,1,0:T(8,128)(2,1)S(1)}, bf16[8,128,128]{2,1,0:T(8,128)(2,1)S(1)}, u32[]{:S(2)}, u32[]{:S(2)}) collective-permute-start(bf16[8,128,128]{2,1,0:T(8,128)(2,1)S(1)} %get-tuple-element.57), channel_id=1, source_target_pairs={{7,0},{0,1},{1,2},{2,3},{3,4},{4,5},{5,6},{6,7},{15,8},{8,9},{9,10... | collective-permute-start | bytes 786440 | tf_op jit(solution)/shard_map/ppermute | solution.py:223
  93.9 8.8 %collective-permute-start.10 = (bf16[8,128,128]{2,1,0:T(8,128)(2,1)S(1)}, bf16[8,128,128]{2,1,0:T(8,128)(2,1)S(1)}, u32[]{:S(2)}, u32[]{:S(2)}) collective-permute-start(bf16[8,128,128]{2,1,0:T(8,128)(2,1)S(1)} %get-tuple-element.58), channel_id=1, source_target_pairs={{1,0},{2,1},{3,2},{4,3},{5,4},{6,5},{7,6},{0,7},{9,8},{10,9},{11,1... | collective-permute-start | bytes 786440 | tf_op jit(solution)/shard_map/ppermute | solution.py:223
  122.2 18.7 %collective-permute-start.13 = (bf16[16,128,128]{2,1,0:T(8,128)(2,1)S(1)}, bf16[16,128,128]{2,1,0:T(8,128)(2,1)S(1)}, u32[]{:S(2)}, u32[]{:S(2)}) collective-permute-start(bf16[16,128,128]{2,1,0:T(8,128)(2,1)S(1)} %all_to_all.32.own_set.rest_8_), channel_id=1, source_target_pairs={{56,0},{57,1},{58,2},{59,3},{60,4},{61,5},{62,6},{63,7},{0,8},{1,9... | collective-permute-start | bytes 1572872 | tf_op jit(solution)/shard_map/ppermute | solution.py:223
  127.2 13.6 %collective-permute-start.12 = (bf16[16,128,128]{2,1,0:T(8,128)(2,1)S(1)}, bf16[16,128,128]{2,1,0:T(8,128)(2,1)S(1)}, u32[]{:S(2)}, u32[]{:S(2)}) collective-permute-start(bf16[16,128,128]{2,1,0:T(8,128)(2,1)S(1)} %all_to_all.32.own_set.rest_8_), channel_id=1, source_target_pairs={{8,0},{9,1},{10,2},{11,3},{12,4},{13,5},{14,6},{15,7},{16,8},{17,9... | collective-permute-start | bytes 1572872 | tf_op jit(solution)/shard_map/ppermute | solution.py:223
  127.3 10.2 %collective-permute-start.15 = (bf16[8,128,128]{2,1,0:T(8,128)(2,1)S(1)}, bf16[8,128,128]{2,1,0:T(8,128)(2,1)S(1)}, u32[]{:S(2)}, u32[]{:S(2)}) collective-permute-start(bf16[8,128,128]{2,1,0:T(8,128)(2,1)S(1)} %get-tuple-element.55), channel_id=1, source_target_pairs={{7,0},{0,1},{1,2},{2,3},{3,4},{4,5},{5,6},{6,7},{15,8},{8,9},{9,10... | collective-permute-start | bytes 786440 | tf_op jit(solution)/shard_map/ppermute | solution.py:223
  131.3 9.5 %collective-permute-start.14 = (bf16[8,128,128]{2,1,0:T(8,128)(2,1)S(1)}, bf16[8,128,128]{2,1,0:T(8,128)(2,1)S(1)}, u32[]{:S(2)}, u32[]{:S(2)}) collective-permute-start(bf16[8,128,128]{2,1,0:T(8,128)(2,1)S(1)} %get-tuple-element.56), channel_id=1, source_target_pairs={{1,0},{2,1},{3,2},{4,3},{5,4},{6,5},{7,6},{0,7},{9,8},{10,9},{11,1... | collective-permute-start | bytes 786440 | tf_op jit(solution)/shard_map/ppermute | solution.py:223
  178.4 14.7 %collective-permute-start.17 = (bf16[16,128,128]{2,1,0:T(8,128)(2,1)S(1)}, bf16[16,128,128]{2,1,0:T(8,128)(2,1)S(1)}, u32[]{:S(2)}, u32[]{:S(2)}) collective-permute-start(bf16[16,128,128]{2,1,0:T(8,128)(2,1)S(1)} %all_to_all.34.rest_0_), channel_id=1, source_target_pairs={{56,0},{57,1},{58,2},{59,3},{60,4},{61,5},{62,6},{63,7},{0,8},{1,9... | collective-permute-start | bytes 1572872 | tf_op jit(solution)/shard_map/ppermute | solution.py:223
  179.3 13.9 %collective-permute-start.16 = (bf16[16,128,128]{2,1,0:T(8,128)(2,1)S(1)}, bf16[16,128,128]{2,1,0:T(8,128)(2,1)S(1)}, u32[]{:S(2)}, u32[]{:S(2)}) collective-permute-start(bf16[16,128,128]{2,1,0:T(8,128)(2,1)S(1)} %all_to_all.34.rest_0_), channel_id=1, source_target_pairs={{8,0},{9,1},{10,2},{11,3},{12,4},{13,5},{14,6},{15,7},{16,8},{17,9... | collective-permute-start | bytes 1572872 | tf_op jit(solution)/shard_map/ppermute | solution.py:223
  181.2 8.8 %collective-permute-start.19 = (bf16[8,128,128]{2,1,0:T(8,128)(2,1)S(1)}, bf16[8,128,128]{2,1,0:T(8,128)(2,1)S(1)}, u32[]{:S(2)}, u32[]{:S(2)}) collective-permute-start(bf16[8,128,128]{2,1,0:T(8,128)(2,1)S(1)} %get-tuple-element.53), channel_id=1, source_target_pairs={{7,0},{0,1},{1,2},{2,3},{3,4},{4,5},{5,6},{6,7},{15,8},{8,9},{9,10... | collective-permute-start | bytes 786440 | tf_op jit(solution)/shard_map/ppermute | solution.py:223
  183.8 9.4 %collective-permute-start.18 = (bf16[8,128,128]{2,1,0:T(8,128)(2,1)S(1)}, bf16[8,128,128]{2,1,0:T(8,128)(2,1)S(1)}, u32[]{:S(2)}, u32[]{:S(2)}) collective-permute-start(bf16[8,128,128]{2,1,0:T(8,128)(2,1)S(1)} %get-tuple-element.54), channel_id=1, source_target_pairs={{1,0},{2,1},{3,2},{4,3},{5,4},{6,5},{7,6},{0,7},{9,8},{10,9},{11,1... | collective-permute-start | bytes 786440 | tf_op jit(solution)/shard_map/ppermute | solution.py:223
  193.8 4.3 %collective-permute-start.20 = (bf16[128,128]{1,0:T(8,128)(2,1)S(1)}, bf16[128,128]{1,0:T(8,128)(2,1)S(1)}, u32[]{:S(2)}, u32[]{:S(2)}) collective-permute-start(bf16[128,128]{1,0:T(8,128)(2,1)S(1)} %get-tuple-element.52), channel_id=1, source_target_pairs={{0,64},{64,0},{1,65},{65,1},{2,66},{66,2},{3,67},{67,3},{4,68},{68... | collective-permute-start | bytes 98312 | tf_op jit(solution)/shard_map/ppermute | solution.py:298
